TPU v7x, 512 devices: a whole 4x8x8 slice. The times are simulated.
512 devices in a mesh: dp: 128 (over z, y, core), mp: 4 (over x).
Axes of the slice: x: 4, y: 8, z: 8, core: 2. Of those that a mesh axis runs over, the one named last changes fastest.
Arguments:
- bag_lengths: int32 [16, 16384], P('mp', 'dp'), may hold values from 1 to 8
- owners: int32 [16, 16384, 8, 1], P('mp', 'dp'), may hold values from 0 to 127; in each aligned block of 1024 rows (0 to 1023, 1024 to 2047, ..., all dimensions but the last counted through in order) at most 16 rows name the same one
- row_slots: int32 [16, 16384, 8], P('mp', 'dp'), may hold values from 0 to 511
- admit_mask: int32 [16, 16384, 8], P('mp', 'dp'), may hold values 0 or 1
- expired: int32 [16, 65536], P('mp', 'dp'), may hold values 0 or 1
- embeddings: float32 [16, 65536, 128], P('mp', 'dp'), may hold values from -3 to 3
- accumulator: float32 [16, 65536], P('mp', 'dp'), may hold values from 0.001 to 0.01
- hidden_weight: bfloat16 [2048, 1024], P(None, 'mp'), may hold values from -0.125 to 0.125
- output_weight: float32 [1024], P('mp'), may hold values from -0.9 to 0.9
- labels: int32 [16384], P('dp'), may hold values 0 or 1
Outputs:
- new_table: float32 [16, 65536, 128], P('mp', 'dp')
- new_accum: float32 [16, 65536], P('mp', 'dp')
- weight_grad: bfloat16 [2048, 1024], P(None, 'mp')
- logits: float32 [16384], P('dp')
Inputs may be any that keep to these rules, and one draw needn't show every extreme that they name: Among the 128 x 8 lookups of one index of dp into one table (aligned blocks of owners' rows), at most 16 name the same owner; in some blocks one owner is named exactly 16 times.
All inputs are finite; a program needn't handle non-finite values. No bound on the sum of `admit_mask` or of `expired` or of `labels` on one device may be relied on, other than what follows from the above.
Results may differ from a plain program's by a relative error of at most 0.0085.
Values may be sent and summed in bfloat16 or wider, within the bound.
No kernel may reach another device: no remote copies, remote signals or barrier semaphores. Data moves between devices by JAX's collectives and lax.ppermute only.
A program may use at most 64 MiB of HBM per device.

v0:
```python
import jax
import jax.numpy as jnp
from jax import lax
from jax.sharding import Mesh
from jax.sharding import PartitionSpec as P

DP = ("dp_0", "dp_1", "dp_2")


LEARN_RATE = 0.05
ACC_RESET = 0.001


def joined_along(parts, dim):
    parts = jnp.moveaxis(parts, 0, dim)
    dims = parts.shape
    return parts.reshape(*dims[:dim], dims[dim] * dims[dim + 1], *dims[dim + 2 :])


def from_everyone(value, axis):
    size = lax.axis_size(axis)
    return lax.all_to_all(
        jnp.broadcast_to(value[None], (size, *value.shape)), axis, 0, 0, tiled=True
    )


def collect_2(value, axis, dim):
    return joined_along(from_everyone(value, axis), dim)


def taken_together(value, axis):
    return from_everyone(value, axis).sum(axis=0)


def cut_along(value, dim, size):
    dims = value.shape
    parts = value.reshape(*dims[:dim], size, dims[dim] // size, *dims[dim + 1 :])
    return jnp.moveaxis(parts, dim, 0)


def summed_on_arrival(value, axis, dim):
    parts = cut_along(value, dim, lax.axis_size(axis))
    arrived = lax.all_to_all(parts, axis, split_axis=0, concat_axis=0, tiled=True)
    return arrived.astype(jnp.float32).sum(axis=0)


def sum_in_two_steps(value, axes, dim):
    far, near = axes
    parts = cut_along(value, dim, lax.axis_size(far))
    nearer = summed_on_arrival(parts, near, dim + 1)
    arrived = lax.all_to_all(
        nearer.astype(jnp.bfloat16), far, split_axis=0, concat_axis=0, tiled=True
    )
    return arrived.astype(jnp.float32).sum(axis=0)


def filled_up(lines, size):
    spare = -lines.shape[0] % size
    if not spare:
        return lines
    return jnp.concatenate([lines, jnp.zeros((spare, *lines.shape[1:]), lines.dtype)])


def gathered_by_axis(value, axes, dim):
    far, near = axes
    parts = from_everyone(from_everyone(value, far), near)
    return joined_along(parts.swapaxes(0, 1).reshape(-1, *value.shape), dim)


def sum_by_parts(value, axes):
    lines = value.reshape(-1, value.shape[-1])
    own = sum_in_two_steps(
        filled_up(lines, lax.axis_size(axes[0]) * lax.axis_size(axes[1])), axes, 0
    )
    whole = gathered_by_axis(own.astype(jnp.bfloat16), axes, 0)
    return whole[: len(lines)].reshape(value.shape).astype(jnp.float32)


def silu_slope(preact):
    sig = jax.nn.sigmoid(preact)
    return sig * (1.0 + preact * (1.0 - sig))


def shards(
    bag_lengths,
    owners,
    row_slots,
    admit_mask,
    expired,
    embeddings,
    accumulator,
    hidden_weight,
    output_weight,
    labels,
):
    groups = lax.axis_size(DP)
    tab_dev, tok_dev, bag_size = row_slots.shape
    rows_dev = embeddings.shape[1]
    row_width = embeddings.shape[2]
    lookups = tok_dev * bag_size
    capacity = 2 * lookups // groups
    buffer_len = groups * capacity
    places = jnp.arange(bag_size, dtype=jnp.int32)
    live_mask = ((places[None, None, :] < bag_lengths[:, :, None]) & (admit_mask == 1)).astype(
        jnp.float32
    )
    counted = jnp.sum(live_mask, axis=2)
    bag_weight = live_mask / jnp.maximum(counted, 1.0)[:, :, None]
    target = owners[..., 0].reshape(tab_dev, lookups)
    lookup_ids = jnp.arange(lookups, dtype=jnp.int32)
    earlier = lookup_ids[None, :] < lookup_ids[:, None]
    same_owner = target[:, :, None] == target[:, None, :]
    ranked = jnp.sum((same_owner & earlier[None, :, :]).astype(jnp.int32), axis=2)
    placed = target * capacity + ranked
    slot_ids = jnp.arange(buffer_len, dtype=jnp.int32)
    hits = placed[:, :, None] == slot_ids[None, None, :]
    flat_slots = row_slots.reshape(tab_dev, lookups)
    request = jnp.sum(jnp.where(hits, flat_slots[:, :, None], 0), axis=1)
    sample_of = lookup_ids // bag_size
    slot_sample = jnp.sum(jnp.where(hits, sample_of[None, :, None], 0), axis=1)
    flat_weight = bag_weight.reshape(tab_dev, lookups)
    slot_weight = jnp.sum(jnp.where(hits, flat_weight[:, :, None], jnp.float32(0.0)), axis=1)
    pool_matrix = jnp.sum(
        jnp.where(
            hits.reshape(tab_dev, tok_dev, bag_size, buffer_len),
            bag_weight[:, :, :, None],
            jnp.float32(0.0),
        ),
        axis=2,
    )
    request = request.reshape(tab_dev, groups, capacity)
    arrived = lax.all_to_all(request, DP, split_axis=1, concat_axis=1, tiled=True)
    fresh_rows = jnp.where(expired[:, :, None] == 1, jnp.float32(0.0), embeddings)
    fresh_acc = jnp.where(expired == 1, jnp.float32(ACC_RESET), accumulator)
    row_pick = (
        arrived.reshape(tab_dev, buffer_len)[:, :, None]
        == jnp.arange(rows_dev, dtype=jnp.int32)[None, None, :]
    ).astype(jnp.bfloat16)
    fetched = jnp.einsum(
        "tbr,tre->tbe",
        row_pick,
        fresh_rows.astype(jnp.bfloat16),
        preferred_element_type=jnp.float32,
    ).astype(jnp.bfloat16)
    fetched = fetched.reshape(tab_dev, groups, capacity, row_width)
    returned = lax.all_to_all(fetched, DP, split_axis=1, concat_axis=1, tiled=True)
    returned_rows = returned.reshape(tab_dev, buffer_len, row_width).astype(jnp.float32)
    pooled = jnp.einsum("tnb,tbe->tne", pool_matrix, returned_rows, precision=lax.Precision.HIGHEST)
    features = pooled.transpose(1, 0, 2).reshape(tok_dev, tab_dev * row_width).astype(jnp.bfloat16)
    portion = collect_2(features, "mp", 1)
    summed_pre = jnp.dot(portion, hidden_weight, preferred_element_type=jnp.float32)
    hidden = jax.nn.silu(summed_pre).astype(jnp.bfloat16)
    logits = taken_together(jnp.sum(hidden.astype(jnp.float32) * output_weight, axis=1), "mp")
    dlogit = jax.nn.sigmoid(logits) - labels.astype(jnp.float32)
    dhidden = (dlogit[:, None] * output_weight * silu_slope(summed_pre)).astype(jnp.bfloat16)
    feature_grad = summed_on_arrival(
        lax.dot_general(
            hidden_weight, dhidden, (((1,), (1,)), ((), ())), preferred_element_type=jnp.float32
        ).astype(jnp.bfloat16),
        "mp",
        0,
    )
    per_table = feature_grad.reshape(tab_dev, row_width, tok_dev).transpose(0, 2, 1)
    sample_pick = (
        slot_sample[:, :, None] == jnp.arange(tok_dev, dtype=jnp.int32)[None, None, :]
    ).astype(jnp.float32)
    slot_grad = jnp.einsum("tbn,tne->tbe", sample_pick, per_table, precision=lax.Precision.HIGHEST)
    outgoing = (slot_weight[:, :, None] * slot_grad).astype(jnp.bfloat16)
    outgoing = outgoing.reshape(tab_dev, groups, capacity, row_width)
    grad_part = lax.all_to_all(outgoing, DP, split_axis=1, concat_axis=1, tiled=True)
    slot_part = lax.all_to_all(request, DP, split_axis=1, concat_axis=1, tiled=True)
    items = grad_part.shape[0]
    selector = (
        slot_part.reshape(items, -1)[:, :, None] == jnp.arange(rows_dev, dtype=jnp.int32)
    ).astype(jnp.bfloat16)
    summed = jnp.einsum(
        "ksr,kse->kre",
        selector,
        grad_part.reshape(items, -1, row_width),
        preferred_element_type=jnp.float32,
    )
    new_acc = fresh_acc + jnp.mean(summed * summed, axis=2)
    new_rows = fresh_rows - LEARN_RATE * summed / jnp.sqrt(new_acc)[:, :, None]
    local_grad = lax.dot_general(
        portion, dhidden, (((0,), (0,)), ((), ())), preferred_element_type=jnp.float32
    )
    weight_grad = sum_by_parts(local_grad.astype(jnp.bfloat16), (("dp_0", "dp_1"), "dp_2")).astype(
        jnp.bfloat16
    )
    return (new_rows, new_acc, weight_grad, logits)


def solution(mesh):
    split = Mesh(mesh.devices.reshape(8, 8, 2, mesh.shape["mp"]), ("dp_0", "dp_1", "dp_2", "mp"))
    return jax.shard_map(
        shards,
        mesh=split,
        in_specs=(
            P("mp", DP),
            P("mp", DP, None, None),
            P("mp", DP, None),
            P("mp", DP, None),
            P("mp", DP),
            P("mp", DP, None),
            P("mp", DP),
            P(None, "mp"),
            P("mp"),
            P(DP),
        ),
        out_specs=(P("mp", DP, None), P("mp", DP), P(None, "mp"), P(DP)),
        check_vma=False,
    )
```

profile of v0, /device:TPU:8, one launch (start us, length us, event | category | flops | bytes accessed | tf_op | source)
XLA Modules:
  0.0 286.2 jit_solution(5932102573414470503)
XLA Ops:
  2.1 3.6 %convert_reduce_fusion = s32[4,1024]{1,0:T(4,128)S(1)} fusion(s32[4,1024]{1,0:T(4,128)S(1)} %reshape_squeeze.3, pred[1024,1024]{1,0:T(8,128)(4,1)S(1)} %iota_compare_fusion.6), kind=kLoop, calls=%fused_computation.9 | loop fusion | flops 16773120 | bytes 1081344 | tf_op jit(solution)/shard_map/reduce_sum | solution.py:113
  6.7 11.5 %select_reduce_fusion.1 = (s32[4,2048]{1,0:T(4,128)S(1)}, s32[4,2048]{1,0:T(4,128)S(1)}) fusion(s32[1024]{0:T(1024)S(1)} %add_select_fusion, s32[4,1024]{1,0:T(4,128)S(1)} %multiply_add_fusion, s32[4,1024]{1,0:T(4,128)S(1)} %broadcast_in_dim.76), kind=kLoop, calls=%fused_computation.2 | loop fusion | flops 41926656 | bytes 102400 | tf_op jit(solution)/shard_map/reduce_sum | solution.py:120
  19.3 17.8 %all-to-all-start = ((s32[4,128,16]{2,0,1:T(4,128)}), s32[4,128,16]{2,0,1:T(4,128)}, u32[]{:S(2)}, u32[]{:S(2)}) async-start(s32[4,128,16]{2,0,1:T(4,128)} %copy.97), calls=%async_computation | async-start | bytes 524288 | tf_op jit(solution)/shard_map/all_to_all | solution.py:171
  37.5 13.9 %all-to-all-done = s32[4,128,16]{2,0,1:T(4,128)} async-done(((s32[4,128,16]{2,0,1:T(4,128)}), s32[4,128,16]{2,0,1:T(4,128)}, u32[]{:S(2)}, u32[]{:S(2)}) %all-to-all-start) | async-done | bytes 32800 | tf_op jit(solution)/shard_map/all_to_all | solution.py:171
  52.5 3.3 %fusion.5 = bf16[4,2048,128]{2,1,0:T(8,128)(2,1)S(1)} fusion(s32[4,2048]{1,0:T(4,128)S(1)} %eq.91, f32[4,512,128]{1,2,0:T(8,128)S(1)} %copy.94, pred[4,512]{1,0:T(4,128)(4,1)S(1)} %broadcast_compare_fusion), kind=kOutput, calls=%fused_computation.16 | convolution fusion | flops 1079246848 | bytes 3180544 | tf_op jit(solution)/shard_map/tbr,tre->tbe/dot_general | solution.py:139
  57.9 6.1 %all-to-all-start.1 = ((bf16[4,128,16,128]{3,2,0,1:T(8,128)(2,1)}), bf16[4,128,16,128]{3,2,0,1:T(8,128)(2,1)S(1)}, u32[]{:S(2)}, u32[]{:S(2)}) async-start(bf16[4,128,16,128]{3,2,0,1:T(8,128)(2,1)} %copy.103), calls=%async_computation.1 | async-start | bytes 4194304 | tf_op jit(solution)/shard_map/all_to_all | solution.py:146
  66.2 12.9 %select_reduce_fusion = f32[4,128,2048]{2,1,0:T(8,128)} fusion(f32[4,128,8]{2,1,0:T(8,128)S(1)} %copy.99, s32[4,128,8]{2,1,0:T(8,128)S(1)} %bitcast_add_fusion), kind=kLoop, calls=%fused_computation | loop fusion | flops 24117248 | bytes 4227072 | tf_op jit(solution)/shard_map/reduce_sum | solution.py:123
  79.1 39.1 %all-to-all-done.1 = bf16[4,128,16,128]{3,2,0,1:T(8,128)(2,1)S(1)} async-done(((bf16[4,128,16,128]{3,2,0,1:T(8,128)(2,1)}), bf16[4,128,16,128]{3,2,0,1:T(8,128)(2,1)S(1)}, u32[]{:S(2)}, u32[]{:S(2)}) %all-to-all-start.1) | async-done | bytes 2097184 | tf_op jit(solution)/shard_map/all_to_all | solution.py:146
  120.3 2.5 convolution_convert_fusion.2
  122.9 12.9 %all_to_all.52 = bf16[4,128,512]{1,2,0:T(8,128)(2,1)S(1)} all-to-all(bf16[4,128,512]{1,2,0:T(8,128)(2,1)S(1)} %broadcast_in_dim.121), channel_id=1, replica_groups=mesh['dp_0'=8,'dp_1'=8,'dp_2'=2,'mp'=4] {'mp'}, dimensions={0} | all-to-all | bytes 1048576 | tf_op jit(solution)/shard_map/all_to_all | solution.py:22
  136.3 7.6 %all_to_all.53 = f32[4,1,128]{2,1,0:T(1,128)S(1)} all-to-all(f32[4,1,128]{2,1,0:T(1,128)S(1)} %broadcast_in_dim.122), channel_id=1, replica_groups=mesh['dp_0'=8,'dp_1'=8,'dp_2'=2,'mp'=4] {'mp'}, dimensions={0} | all-to-all | bytes 4096 | tf_op jit(solution)/shard_map/all_to_all | solution.py:22
  144.5 4.6 %all_to_all.54 = bf16[2,64,16,256]{3,2,1,0:T(8,128)(2,1)S(1)} all-to-all(bf16[2,64,16,256]{3,2,1,0:T(8,128)(2,1)S(1)} %bitcast.40), channel_id=1, replica_groups=mesh['dp_0'=8,'dp_1'=8,'dp_2'=2,'mp'=4] {'dp_2'}, dimensions={0} | all-to-all | bytes 2097152 | tf_op jit(solution)/shard_map/all_to_all | solution.py:43
  150.2 6.2 %all-to-all-start.7 = ((bf16[64,16,256]{2,1,0:T(8,128)(2,1)}), bf16[64,16,256]{2,1,0:T(8,128)(2,1)S(1)}, u32[]{:S(2)}, u32[]{:S(2)}) async-start(bf16[64,16,256]{2,1,0:T(8,128)(2,1)} %reduce_sum.127), calls=%async_computation.7 | async-start | bytes 1048576 | tf_op jit(solution)/shard_map/all_to_all | solution.py:51
  157.8 18.2 %all-to-all-done.7 = bf16[64,16,256]{2,1,0:T(8,128)(2,1)S(1)} async-done(((bf16[64,16,256]{2,1,0:T(8,128)(2,1)}), bf16[64,16,256]{2,1,0:T(8,128)(2,1)S(1)}, u32[]{:S(2)}, u32[]{:S(2)}) %all-to-all-start.7) | async-done | bytes 524320 | tf_op jit(solution)/shard_map/all_to_all | solution.py:51
  175.9 3.5 %all-to-all-start.4 = ((bf16[4,512,128]{1,2,0:T(8,128)(2,1)}), bf16[4,512,128]{1,2,0:T(8,128)(2,1)S(1)}, u32[]{:S(2)}, u32[]{:S(2)}) async-start(bf16[4,512,128]{1,2,0:T(8,128)(2,1)} %bitcast.37), calls=%async_computation.4 | async-start | bytes 1048576 | tf_op jit(solution)/shard_map/all_to_all | solution.py:43
  179.7 7.8 %all-to-all-done.4 = bf16[4,512,128]{1,2,0:T(8,128)(2,1)S(1)} async-done(((bf16[4,512,128]{1,2,0:T(8,128)(2,1)}), bf16[4,512,128]{1,2,0:T(8,128)(2,1)S(1)}, u32[]{:S(2)}, u32[]{:S(2)}) %all-to-all-start.4) | async-done | bytes 524320 | tf_op jit(solution)/shard_map/all_to_all | solution.py:43
  188.3 6.7 %all-to-all-start.8 = ((bf16[64,16,256]{2,1,0:T(8,128)(2,1)}), bf16[64,16,256]{2,1,0:T(8,128)(2,1)S(1)}, u32[]{:S(2)}, u32[]{:S(2)}) async-start(bf16[64,16,256]{2,1,0:T(8,128)(2,1)} %broadcast_in_dim.124), calls=%async_computation.8 | async-start | bytes 1048576 | tf_op jit(solution)/shard_map/all_to_all | solution.py:22
  195.0 4.9 %select_reduce_fusion.2 = f32[4,2048]{1,0:T(4,128)S(1)} fusion(f32[4,1024]{1,0:T(4,128)S(1)} %broadcast_in_dim.115, s32[4,1024]{1,0:T(4,128)S(1)} %multiply_add_fusion), kind=kLoop, calls=%fused_computation.3 | loop fusion | flops 25157632 | bytes 65536 | tf_op jit(solution)/shard_map/reduce_sum | solution.py:122
  200.2 3.8 %multiply_convert_fusion = bf16[4,2048,128]{2,1,0:T(8,128)(2,1)S(1)} fusion(f32[4,128,128]{2,1,0:T(8,128)S(1)} %bitcast.49, s32[4,2048]{1,0:T(4,128)S(1)} %get-tuple-element.28, f32[4,2048]{1,0:T(4,128)S(1)} %select_reduce_fusion.2), kind=kOutput, calls=%fused_computation.12 | convolution fusion | flops 1613758464 | bytes 2424832 | tf_op jit(solution)/shard_map/tbn,tne->tbe/dot_general | solution.py:167
  206.0 7.5 %all-to-all-done.8 = bf16[64,16,256]{2,1,0:T(8,128)(2,1)S(1)} async-done(((bf16[64,16,256]{2,1,0:T(8,128)(2,1)}), bf16[64,16,256]{2,1,0:T(8,128)(2,1)S(1)}, u32[]{:S(2)}, u32[]{:S(2)}) %all-to-all-start.8) | async-done | bytes 524320 | tf_op jit(solution)/shard_map/all_to_all | solution.py:22
  213.5 5.4 %all_to_all.55 = bf16[2,64,16,256]{3,2,1,0:T(8,128)(2,1)} all-to-all(bf16[2,64,16,256]{3,2,1,0:T(8,128)(2,1)S(1)} %broadcast_in_dim.125), channel_id=1, replica_groups=mesh['dp_0'=8,'dp_1'=8,'dp_2'=2,'mp'=4] {'dp_2'}, dimensions={0} | all-to-all | bytes 2097152 | tf_op jit(solution)/shard_map/all_to_all | solution.py:22
  218.9 6.1 %all-to-all-start.5 = ((bf16[4,128,16,128]{3,2,0,1:T(8,128)(2,1)}), bf16[4,128,16,128]{3,2,0,1:T(8,128)(2,1)S(1)}, u32[]{:S(2)}, u32[]{:S(2)}) async-start(bf16[4,128,16,128]{3,2,0,1:T(8,128)(2,1)} %copy.110), calls=%async_computation.5 | async-start | bytes 4194304 | tf_op jit(solution)/shard_map/all_to_all | solution.py:170
  227.4 51.8 %all-to-all-done.5 = bf16[4,128,16,128]{3,2,0,1:T(8,128)(2,1)S(1)} async-done(((bf16[4,128,16,128]{3,2,0,1:T(8,128)(2,1)}), bf16[4,128,16,128]{3,2,0,1:T(8,128)(2,1)S(1)}, u32[]{:S(2)}, u32[]{:S(2)}) %all-to-all-start.5) | async-done | bytes 2097184 | tf_op jit(solution)/shard_map/all_to_all | solution.py:170
  279.6 4.4 %multiply_reduce_fusion = (f32[4,512]{1,0:T(4,128)S(1)}, f32[4,512,128]{1,2,0:T(8,128)S(1)}) fusion(bf16[4,2048,128]{2,1,0:T(8,128)(2,1)S(1)} %bitcast.41, s32[4,2048]{1,0:T(4,128)S(1)} %eq.91), kind=kOutput, calls=%fused_computation.23 | convolution fusion | flops 1078458368 | bytes 3186688 | tf_op jit(solution)/shard_map/ksr,kse->kre/dot_general | solution.py:176
  (69 shorter events, 23.0 us)
Async XLA Ops:
  0.6 135.2 %copy-start = (bf16[2048,256]{1,0:T(8,128)(2,1)S(1)}, bf16[2048,256]{1,0:T(8,128)(2,1)}, u32[]{:S(2)}) copy-start(bf16[2048,256]{1,0:T(8,128)(2,1)} %param.17) | copy-start | bytes 3145732
  0.6 36.4 %copy-start.6 = (s32[4,512]{1,0:T(4,128)S(1)}, s32[4,512]{1,0:T(4,128)}, u32[]{:S(2)}) copy-start(s32[4,512]{1,0:T(4,128)} %param.14) | copy-start | bytes 24580
  0.7 36.5 %copy-start.5 = (f32[4,512,128]{2,1,0:T(8,128)S(1)}, f32[4,512,128]{2,1,0:T(8,128)}, u32[]{:S(2)}) copy-start(f32[4,512,128]{2,1,0:T(8,128)} %param.15) | copy-start | bytes 3145732
  1.9 53.9 %copy-start.4 = (s32[4,128,8,1]{2,1,0,3:T(8,128)}, s32[4,128,8,1]{2,1,0,3:T(8,128)S(1)}, u32[]{:S(2)}) copy-start(s32[4,128,8,1]{2,1,0,3:T(8,128)S(1)} %copy.95) | copy-start | bytes 49156
  19.3 32.2 %all-to-all-start = ((s32[4,128,16]{2,0,1:T(4,128)}), s32[4,128,16]{2,0,1:T(4,128)}, u32[]{:S(2)}, u32[]{:S(2)}) async-start(s32[4,128,16]{2,0,1:T(4,128)} %copy.97), calls=%async_computation | async-start | bytes 524288 | tf_op jit(solution)/shard_map/all_to_all | solution.py:171
  37.5 18.4 %copy-start.2 = (f32[4,512,128]{1,2,0:T(8,128)}, f32[4,512,128]{1,2,0:T(8,128)S(1)}, u32[]{:S(2)}) copy-start(f32[4,512,128]{1,2,0:T(8,128)S(1)} %copy.94) | copy-start | bytes 3145732
  55.9 9.0 %copy-start.7 = (s32[4,128,8]{1,2,0:T(8,128)S(1)}, s32[4,128,8]{1,2,0:T(8,128)}, u32[]{:S(2)}) copy-start(s32[4,128,8]{1,2,0:T(8,128)} %param.13) | copy-start | bytes 49156
  55.9 9.0 %copy-start.10 = (s32[4,128]{1,0:T(4,128)S(1)}, s32[4,128]{1,0:T(4,128)}, u32[]{:S(2)}) copy-start(s32[4,128]{1,0:T(4,128)} %param.10) | copy-start | bytes 6148
  57.9 60.3 %all-to-all-start.1 = ((bf16[4,128,16,128]{3,2,0,1:T(8,128)(2,1)}), bf16[4,128,16,128]{3,2,0,1:T(8,128)(2,1)S(1)}, u32[]{:S(2)}, u32[]{:S(2)}) async-start(bf16[4,128,16,128]{3,2,0,1:T(8,128)(2,1)} %copy.103), calls=%async_computation.1 | async-start | bytes 4194304 | tf_op jit(solution)/shard_map/all_to_all | solution.py:146
  118.2 2.2 copy-start.1
  118.5 17.3 %copy-start.9 = (f32[256]{0:T(256)S(1)}, f32[256]{0:T(256)}, u32[]{:S(2)}) copy-start(f32[256]{0:T(256)} %param.18) | copy-start | bytes 3076
  120.3 23.6 %copy-start.12 = (s32[128]{0:T(128)S(1)}, s32[128]{0:T(128)}, u32[]{:S(2)}) copy-start(s32[128]{0:T(128)} %param.19) | copy-start | bytes 1540
  143.9 6.3 %copy-start.11 = (f32[128]{0:T(128)}, f32[128]{0:T(128)S(1)}, u32[]{:S(2)}) copy-start(f32[128]{0:T(128)S(1)} %reduce_sum.124) | copy-start | bytes 1540
  150.2 25.7 %all-to-all-start.7 = ((bf16[64,16,256]{2,1,0:T(8,128)(2,1)}), bf16[64,16,256]{2,1,0:T(8,128)(2,1)S(1)}, u32[]{:S(2)}, u32[]{:S(2)}) async-start(bf16[64,16,256]{2,1,0:T(8,128)(2,1)} %reduce_sum.127), calls=%async_computation.7 | async-start | bytes 1048576 | tf_op jit(solution)/shard_map/all_to_all | solution.py:51
  175.9 11.5 %all-to-all-start.4 = ((bf16[4,512,128]{1,2,0:T(8,128)(2,1)}), bf16[4,512,128]{1,2,0:T(8,128)(2,1)S(1)}, u32[]{:S(2)}, u32[]{:S(2)}) async-start(bf16[4,512,128]{1,2,0:T(8,128)(2,1)} %bitcast.37), calls=%async_computation.4 | async-start | bytes 1048576 | tf_op jit(solution)/shard_map/all_to_all | solution.py:43
  188.3 25.2 %all-to-all-start.8 = ((bf16[64,16,256]{2,1,0:T(8,128)(2,1)}), bf16[64,16,256]{2,1,0:T(8,128)(2,1)S(1)}, u32[]{:S(2)}, u32[]{:S(2)}) async-start(bf16[64,16,256]{2,1,0:T(8,128)(2,1)} %broadcast_in_dim.124), calls=%async_computation.8 | async-start | bytes 1048576 | tf_op jit(solution)/shard_map/all_to_all | solution.py:22
  218.9 60.3 %all-to-all-start.5 = ((bf16[4,128,16,128]{3,2,0,1:T(8,128)(2,1)}), bf16[4,128,16,128]{3,2,0,1:T(8,128)(2,1)S(1)}, u32[]{:S(2)}, u32[]{:S(2)}) async-start(bf16[4,128,16,128]{3,2,0,1:T(8,128)(2,1)} %copy.110), calls=%async_computation.5 | async-start | bytes 4194304 | tf_op jit(solution)/shard_map/all_to_all | solution.py:170
  279.6 4.4 %copy-start.8 = (f32[4,512]{1,0:T(4,128)S(1)}, f32[4,512]{1,0:T(4,128)}, u32[]{:S(2)}) copy-start(f32[4,512]{1,0:T(4,128)} %param.16) | copy-start | bytes 24580
  279.6 5.0 %copy-start.3 = (f32[4,512,128]{1,2,0:T(8,128)S(1)}, f32[4,512,128]{1,2,0:T(8,128)}, u32[]{:S(2)}) copy-start(f32[4,512,128]{1,2,0:T(8,128)} %copy-done.2) | copy-start | bytes 3145732
where the time goes:
time: 287 us; the launch traced here: 286 us
  waiting for transfers between devices  138 us (48%)
  starting transfers between devices  46.5 us (16%)
  other arithmetic  36.5 us (13%)
  blocking collectives  30.5 us (11%)
  local copies, waits for them, and re-layouts  18 us (6%)
  matrix products  15.4 us (5%)
    all_to_all x1, waiting for transfers between devices, shards(): lax.all_to_all(outgoing, DP, split_axis=1, concat_axis=1, tiled=True)  51.8 us
    all_to_all x1, waiting for transfers between devices, shards(): lax.all_to_all(fetched, DP, split_axis=1, concat_axis=1, tiled=True)  39.1 us
    all_to_all x3, blocking collectives, from_everyone(): lax.all_to_all(jnp.broadcast_to(value[None], (size, *value.shape)), axis,...  25.9 us
    all_to_all x1, waiting for transfers between devices, sum_in_two_steps(): lax.all_to_all(nearer.astype(jnp.bfloat16), far, split_axis=0, concat_axi...  18.2 us
    all_to_all x1, starting transfers between devices, shards(): lax.all_to_all(request, DP, split_axis=1, concat_axis=1, tiled=True)  17.8 us
    all_to_all x1, waiting for transfers between devices, shards(): lax.all_to_all(request, DP, split_axis=1, concat_axis=1, tiled=True)  13.9 us
    reduce_sum x1, other arithmetic, shards(): jnp.sum(jnp.where(hits.reshape(tab_dev, tok_dev, bag_size, buffer_len), b...  12.9 us
    reduce_sum x1, other arithmetic, shards(): slot_sample = jnp.sum(jnp.where(hits, sample_of[None, :, None], 0), axis=1)  11.5 us
  transfers between devices with their start and end apart: 6, of which 6 were waited for; matrix products, arithmetic and copies ran while one was open for 11% of the time, Pallas kernels for 0%

commit v1 on v0

v1 whole, which is shorter than its diff:
```python
import jax
import jax.numpy as jnp
from jax import lax
from jax.experimental import pallas as pl
from jax.experimental.pallas import tpu as pltpu
from jax.sharding import Mesh
from jax.sharding import PartitionSpec as P

DP = ("dp_0", "dp_1", "dp_2")
FAR = ("dp_0", "dp_1")
NEAR = "dp_2"

LEARN_RATE = 0.05
ACC_RESET = 0.001
F32, BF16, I32 = jnp.float32, jnp.bfloat16, jnp.int32
NT = (((1,), (1,)), ((), ()))


def iota(shape, dim):
    return lax.broadcasted_iota(I32, shape, dim)


def dot(a, b, dims=(((1,), (0,)), ((), ()))):
    return lax.dot_general(a, b, dims, preferred_element_type=F32)


def flag(cond):
    return jnp.where(cond, 1.0, 0.0).astype(BF16)


def slots_kernel(len_ref, own_ref, slot_ref, adm_ref, req_ref, sample_ref, inv_ref):
    tabs, bag, toks = own_ref.shape
    groups, width = req_ref.shape
    cap = width // tabs
    row_o, lane = iota((groups, toks), 0), iota((groups, toks), 1)
    tri = jnp.concatenate(
        [flag(row_o < lane), jnp.ones((groups, toks), BF16)], axis=1
    )
    rank_row = iota((cap, toks), 0).astype(F32)
    sample_no = (iota((1, toks), 1) + 1).astype(F32)
    for t in range(tabs):
        hot = [row_o == own_ref[t, p : p + 1, :] for p in range(bag)]
        hot16 = [flag(h) for h in hot]
        counts = dot(jnp.concatenate(hot16, axis=0), tri)
        base = jnp.zeros((groups, toks), F32)
        live_count = jnp.zeros((1, toks), F32)
        values = []
        for p in range(bag):
            part = counts[p * groups : (p + 1) * groups]
            rank = jnp.sum(
                jnp.where(hot[p], part[:, :toks] + base, 0.0), axis=0, keepdims=True
            )
            base = base + part[:, toks:]
            live = (p < len_ref[t : t + 1, :]) & (adm_ref[t, p : p + 1, :] == 1)
            live_count = live_count + jnp.where(live, 1.0, 0.0)
            slot = slot_ref[t, p : p + 1, :]
            here = rank_row == rank
            values.append(
                jnp.concatenate(
                    [
                        jnp.where(here, (slot >> 4).astype(F32), 0.0),
                        jnp.where(here, (slot & 15).astype(F32), 0.0),
                        jnp.where(here & live, sample_no, 0.0),
                    ],
                    axis=0,
                ).astype(BF16)
            )
        found = dot(
            jnp.concatenate(hot16, axis=1), jnp.concatenate(values, axis=1), NT
        )
        cols = slice(t * cap, (t + 1) * cap)
        req_ref[:, cols] = (16.0 * found[:, :cap] + found[:, cap : 2 * cap]).astype(I32)
        sample_ref[:, cols] = found[:, 2 * cap :]
        inv = 1.0 / jnp.maximum(live_count, 1.0)
        column = jnp.sum(
            jnp.where(iota((toks, toks), 0) == iota((toks, toks), 1), inv, 0.0),
            axis=1,
            keepdims=True,
        )
        inv_ref[t] = jnp.broadcast_to(column, (toks, toks))


def spread_rows(length, groups, cap, start):
    return flag((iota((length, groups), 0) + start) // cap == iota((length, groups), 1))


def samples_kernel(sample_ref, pick_ref, row_ref):
    tabs, slots, toks = pick_ref.shape
    groups, width = sample_ref.shape
    cap = width // tabs
    spread = spread_rows(slots, groups, cap, 0)
    every = dot(spread, sample_ref[...].astype(BF16))
    place = iota((slots, width), 0) % cap
    lane = iota((slots, width), 1)
    wanted = (iota((slots, toks), 1) + 1).astype(F32)
    for t in range(tabs):
        own = jnp.where(lane == place + t * cap, every, 0.0).astype(BF16)
        pick_ref[t] = flag(dot(own, jnp.ones((width, toks), BF16)) == wanted)
        row_ref[t] = dot(jnp.ones((8, width), BF16), own, NT)


def labels_kernel(label_ref, out_ref):
    dims = out_ref.shape
    row = label_ref[...].astype(F32)
    column = jnp.sum(
        jnp.where(iota(dims, 0) == iota(dims, 1), row, 0.0), axis=1, keepdims=True
    )
    out_ref[...] = jnp.broadcast_to(column, dims)


def halves_of(arrived):
    return jnp.concatenate(
        [(arrived >> 4).astype(F32), (arrived & 15).astype(F32)], axis=1
    ).astype(BF16)


def fetch_kernel(arrived_ref, expired_ref, emb_ref, out_ref):
    groups, width = arrived_ref.shape
    rows, emb = emb_ref.shape[1:]
    cap = out_ref.shape[1]
    t = pl.program_id(0)
    halves = halves_of(arrived_ref[...])
    table = emb_ref[0].astype(BF16)
    scale = jnp.where(iota((2 * width, emb), 0) < width, 16.0, 1.0).astype(BF16)
    gone = expired_ref[pl.ds(t, 1), :]
    names = jnp.where(gone == 1, -1.0, iota((1, rows), 1).astype(F32))
    part = 32
    for c in range(groups // part):
        length = part * cap
        spread = spread_rows(length, groups, cap, c * length)
        every = dot(spread, halves)
        lane = iota((length, 2 * width), 1) & (width - 1)
        own = jnp.where(
            lane == iota((length, 2 * width), 0) % cap + t * cap, every, 0.0
        ).astype(BF16)
        wanted = dot(own, scale)
        pick = jnp.concatenate(
            [flag(wanted == names[:, j : j + emb]) for j in range(0, rows, emb)], axis=1
        )
        out_ref[c * part : (c + 1) * part] = (
            dot(pick, table).astype(BF16).reshape(part, cap, emb)
        )


def wanted_kernel(arrived_ref, row_ref):
    groups, width = arrived_ref.shape
    tabs, eight, slots = row_ref.shape
    cap = width // tabs
    every = dot(spread_rows(slots, groups, cap, 0), halves_of(arrived_ref[...]))
    place = iota((slots, 2 * width), 0) % cap
    lane = iota((slots, 2 * width), 1) & (width - 1)
    scale = jnp.where(iota((eight, 2 * width), 1) < width, 16.0, 1.0).astype(BF16)
    for t in range(tabs):
        own = jnp.where(lane == place + t * cap, every, 0.0).astype(BF16)
        row_ref[t] = dot(scale, own, NT)


def pool_kernel(rows_ref, sample_ref, inv_ref, out_ref):
    groups, cap, emb = rows_ref.shape
    toks = inv_ref.shape[1]
    slots = groups * cap
    wanted = (iota((toks, slots), 0) + 1).astype(F32)
    pick = flag(sample_ref[0, 0:1, :] == wanted)
    pooled = dot(pick, rows_ref[...].reshape(slots, emb))
    out_ref[...] = (pooled * inv_ref[0]).astype(BF16)


def silu_slope(preact):
    sig = jax.nn.sigmoid(preact)
    return sig * (1.0 + preact * (1.0 - sig))


def dense_kernel(
    at_ref, feat_ref, w0, w1, w2, w3, u0, u1, u2, u3, labels_ref,
    logits_ref, grad_ref, mine_ref, other_ref,
):
    parts, toks, feats = feat_ref.shape
    weights, units = (w0, w1, w2, w3), (u0, u1, u2, u3)
    me, core = at_ref[0], at_ref[1]
    preacts, scores = [], []
    for w, u in zip(weights, units):
        pre = sum(
            dot(feat_ref[q], w[q * feats : (q + 1) * feats, :]) for q in range(parts)
        )
        hidden = jax.nn.silu(pre).astype(BF16).astype(F32)
        preacts.append(pre)
        scores.append(jnp.sum(hidden * u[...], axis=1, keepdims=True))
    logits = jnp.zeros((toks, 1), F32)
    for shard in range(parts):
        far = (me + parts - shard) % parts
        score = scores[0]
        for k in range(1, parts):
            score = jnp.where(far == k, scores[k], score)
        logits = logits + score
    dlogit = (jax.nn.sigmoid(logits) - labels_ref[...])[:, 0:1]
    logits_ref[...] = jnp.broadcast_to(logits, logits_ref.shape)
    start = pl.multiple_of(me * feats, feats)
    grads = jnp.zeros((toks, feats), F32)
    for k, (w, u, pre) in enumerate(zip(weights, units, preacts)):
        dhidden = (dlogit * u[...] * silu_slope(pre)).astype(BF16)
        if k == 0:
            half = dhidden.shape[1] // 2
            low, high = dhidden[:, :half], dhidden[:, half:]
            mine, other = jnp.where(core == 0, low, high), jnp.where(core == 0, high, low)
            for q in range(parts):
                lines = slice(q * feats, (q + 1) * feats)
                part = dot(
                    feat_ref[q],
                    jnp.concatenate([mine, other], axis=1),
                    (((0,), (0,)), ((), ())),
                ).astype(BF16)
                mine_ref[lines, :] = part[:, :half]
                other_ref[lines, :] = part[:, half:]
        grads = grads + dot(dhidden, w[pl.ds(start, feats), :], NT)
    grad_ref[...] = grads


def spread_kernel(grad_ref, inv_ref, pick_ref, out_ref):
    slots = pick_ref.shape[1]
    cap, emb = out_ref.shape[1:]
    grad = (inv_ref[0] * grad_ref[...]).astype(BF16)
    out_ref[...] = dot(pick_ref[0], grad).astype(BF16).reshape(slots // cap, cap, emb)


def update_kernel(grads_ref, wanted_ref, emb_ref, expired_ref, acc_ref, new_ref, new_acc_ref):
    groups, cap, emb = grads_ref.shape
    rows = emb_ref.shape[1]
    slots = groups * cap
    t = pl.program_id(0)
    grads = grads_ref[...].reshape(slots, emb)
    wanted = wanted_ref[0, 0:1, :]
    gone = expired_ref[pl.ds(t, 1), :]
    fresh_acc = jnp.where(gone == 1, ACC_RESET, acc_ref[pl.ds(t, 1), :])
    kept = jnp.where(gone == 1, 0.0, 1.0)
    diag = iota((emb, emb), 0) == iota((emb, emb), 1)
    for j in range(0, rows, emb):
        names = (iota((emb, slots), 0) + j).astype(F32)
        summed = dot(flag(wanted == names), grads)
        cols = slice(j, j + emb)
        old = jnp.sum(jnp.where(diag, fresh_acc[:, cols], 0.0), axis=1, keepdims=True)
        keep = jnp.sum(jnp.where(diag, kept[:, cols], 0.0), axis=1, keepdims=True)
        acc = old + jnp.sum(summed * summed, axis=1, keepdims=True) * (1.0 / emb)
        fresh = jnp.where(keep > 0.5, emb_ref[0, j : j + emb, :], 0.0)
        new_ref[0, j : j + emb, :] = fresh - LEARN_RATE * summed / jnp.sqrt(acc)
        line = jnp.sum(jnp.where(diag, acc, 0.0), axis=0, keepdims=True)
        for table in range(acc_ref.shape[0]):

            @pl.when(t == table)
            def _(table=table, cols=cols, line=line):
                new_acc_ref[table : table + 1, cols] = line


def shape(dims, dtype):
    return jax.ShapeDtypeStruct(dims, dtype)


def block(dims, index=None):
    if index is None:
        return pl.BlockSpec(dims, lambda *_: (0,) * len(dims))
    return pl.BlockSpec(dims, index)


def params(mib):
    return pltpu.CompilerParams(vmem_limit_bytes=mib << 20)


def cost(flops):
    return pl.CostEstimate(flops=flops, bytes_accessed=1 << 20, transcendentals=0)


def a2a(value, axis):
    return lax.all_to_all(value, axis, split_axis=0, concat_axis=0, tiled=True)


def from_everyone(value, axis):
    size = lax.axis_size(axis)
    return a2a(jnp.broadcast_to(value[None], (size, *value.shape)), axis)


def ring(value, axis, step):
    size = lax.axis_size(axis)
    return lax.ppermute(value, axis, [(i, (i + step) % size) for i in range(size)])


def shards(
    bag_lengths, owners, row_slots, admit_mask, expired, embeddings, accumulator,
    hidden_weight, output_weight, labels,
):
    groups = lax.axis_size(DP)
    parts = lax.axis_size("mp")
    tabs, toks, bag = row_slots.shape
    rows, emb = embeddings.shape[1:]
    cap = 2 * toks * bag // groups
    width = tabs * cap
    slots = groups * cap
    feats = tabs * emb
    core = lax.axis_index(NEAR).astype(I32)
    place = jnp.stack([lax.axis_index("mp").astype(I32), core])

    request, sample, inv = pl.pallas_call(
        slots_kernel,
        out_shape=(
            shape((groups, width), I32),
            shape((groups, width), F32),
            shape((tabs, toks, toks), F32),
        ),
        compiler_params=params(24),
        name="slots",
    )(
        bag_lengths,
        owners[..., 0].swapaxes(1, 2),
        row_slots.swapaxes(1, 2),
        admit_mask.swapaxes(1, 2),
    )
    arrived = a2a(request, DP)
    weight, _ = lax.optimization_barrier((hidden_weight, request))
    weights = [weight] + [ring(weight, "mp", k) for k in range(1, parts)]
    pick, sample_row = pl.pallas_call(
        samples_kernel,
        out_shape=(shape((tabs, slots, toks), BF16), shape((tabs, 8, slots), F32)),
        compiler_params=params(24),
        cost_estimate=cost(4 << 30),
        name="samples",
    )(sample)
    fetched = pl.pallas_call(
        fetch_kernel,
        grid=(tabs,),
        in_specs=[
            block((groups, width)),
            block((tabs, rows)),
            block((1, rows, emb), lambda t: (t, 0, 0)),
        ],
        out_specs=block((groups, cap, emb), lambda t: (0, t, 0)),
        out_shape=pltpu.HBM((groups, width, emb), BF16),
        compiler_params=params(24),
        name="fetch",
    )(arrived, expired, embeddings)
    returned = a2a(fetched, DP)
    unit, later = lax.optimization_barrier((output_weight, arrived))
    unit = unit.reshape(1, -1)
    units = [unit] + [ring(unit, "mp", k) for k in range(1, parts)]
    wanted = pl.pallas_call(
        wanted_kernel,
        out_shape=shape((tabs, 8, slots), F32),
        compiler_params=params(24),
        cost_estimate=cost(4 << 30),
        name="wanted",
    )(later)
    features = pl.pallas_call(
        pool_kernel,
        grid=(tabs,),
        in_specs=[
            block((groups, cap, emb), lambda t: (0, t, 0)),
            block((1, 8, slots), lambda t: (t, 0, 0)),
            block((1, toks, toks), lambda t: (t, 0, 0)),
        ],
        out_specs=block((toks, emb), lambda t: (0, t)),
        out_shape=shape((toks, feats), BF16),
        compiler_params=params(24),
        name="pool",
    )(returned, sample_row, inv)
    portion = from_everyone(features, "mp")
    label_column = pl.pallas_call(
        labels_kernel,
        out_shape=shape((toks, toks), F32),
        compiler_params=params(4),
        name="labels",
    )(labels.reshape(1, toks))
    units_dev = hidden_weight.shape[1]
    lines, half = hidden_weight.shape[0], units_dev // 2
    logits, grad, mine, other = pl.pallas_call(
        dense_kernel,
        in_specs=[pl.BlockSpec(memory_space=pltpu.SMEM)]
        + [pl.BlockSpec(memory_space=pltpu.VMEM)] * (2 * parts + 2),
        out_shape=(
            shape((toks, toks), F32),
            shape((toks, feats), F32),
            shape((lines, half), BF16),
            shape((lines, half), BF16),
        ),
        compiler_params=params(24),
        name="dense",
    )(place, portion, *weights, *units, label_column)
    joined = ring(other, NEAR, 1)
    share = lines // groups
    outgoing = pl.pallas_call(
        spread_kernel,
        grid=(tabs,),
        in_specs=[
            block((toks, emb), lambda t: (0, t)),
            block((1, toks, toks), lambda t: (t, 0, 0)),
            block((1, slots, toks), lambda t: (t, 0, 0)),
        ],
        out_specs=block((groups, cap, emb), lambda t: (0, t, 0)),
        out_shape=shape((groups, width + share, emb), BF16),
        compiler_params=params(24),
        cost_estimate=cost(4 << 30),
        name="spread",
    )(grad, inv, pick)
    pair = (mine.astype(F32) + joined.astype(F32)).astype(BF16)
    pair = pair.reshape(2, groups // 2, share, half).swapaxes(0, 1)
    outgoing = lax.dynamic_update_slice(
        outgoing, pair.reshape(groups, share, half), (0, width, 0)
    )
    gradients = a2a(outgoing, DP)
    shares = gradients[:, width:].reshape(groups // 2, 2, 2, share // 2, half)
    own = shares.astype(F32).sum(axis=0).astype(BF16).swapaxes(0, 1)
    near = from_everyone(own, FAR)
    near = near.transpose(0, 1, 3, 2, 4).reshape(lines // 2, units_dev)
    far = ring(near, NEAR, 1)
    weight_grad = jnp.concatenate(
        [jnp.where(core == 0, near, far), jnp.where(core == 0, far, near)]
    )
    new_rows, new_acc = pl.pallas_call(
        update_kernel,
        grid=(tabs,),
        in_specs=[
            block((groups, cap, emb), lambda t: (0, t, 0)),
            block((1, 8, slots), lambda t: (t, 0, 0)),
            block((1, rows, emb), lambda t: (t, 0, 0)),
            block((tabs, rows)),
            block((tabs, rows)),
        ],
        out_specs=(
            block((1, rows, emb), lambda t: (t, 0, 0)),
            block((tabs, rows)),
        ),
        out_shape=(shape(embeddings.shape, F32), shape(accumulator.shape, F32)),
        compiler_params=params(24),
        cost_estimate=cost(4 << 30),
        name="update",
    )(gradients, wanted, embeddings, expired, accumulator)
    return (new_rows, new_acc, weight_grad, logits[:, 0])


def solution(mesh):
    split = Mesh(mesh.devices.reshape(8, 8, 2, mesh.shape["mp"]), (*DP, "mp"))

    return jax.shard_map(
        shards,
        mesh=split,
        in_specs=(
            P("mp", DP),
            P("mp", DP, None, None),
            P("mp", DP, None),
            P("mp", DP, None),
            P("mp", DP),
            P("mp", DP, None),
            P("mp", DP),
            P(None, "mp"),
            P("mp"),
            P(DP),
        ),
        out_specs=(P("mp", DP, None), P("mp", DP), P(None, "mp"), P(DP)),
        check_vma=False,
    )
```

time: 287 us -> 244 us (0.85)
  the two profiles are of different devices: /device:TPU:8 before, /device:TPU:1 now
where the time goes in v1:
time: 244 us; the launch traced here: 243 us
  blocking collectives  98.2 us (40%)
  waiting for transfers between devices  56.1 us (23%)
  starting transfers between devices  51.6 us (21%)
  Pallas kernels  24.4 us (10%)
  local copies, waits for them, and re-layouts  10.2 us (4%)
    all_to_all x2, blocking collectives, a2a(): return lax.all_to_all(value, axis, split_axis=0, concat_axis=0, tiled=True)  98.2 us
    all_to_all x3, waiting for transfers between devices, a2a(): return lax.all_to_all(value, axis, split_axis=0, concat_axis=0, tiled=True)  54.6 us
    ppermute x8, starting transfers between devices, ring(): lax.ppermute(value, axis, [(i, (i + step) % size) for i in range(size)])  32.4 us
    all_to_all x3, starting transfers between devices, a2a(): return lax.all_to_all(value, axis, split_axis=0, concat_axis=0, tiled=True)  19.1 us
    unnamed x32, local copies, waits for them, and re-layouts  7.72 us
    pallas_call x1, Pallas kernels, shards(): pl.pallas_call(update_kernel, grid=(tabs,), in_specs=[block((groups, cap,...  7.15 us
    pallas_call x1, Pallas kernels, shards(): pl.pallas_call(fetch_kernel, grid=(tabs,), in_specs=[block((groups, width...  6.11 us
  transfers between devices with their start and end apart: 11, of which 4 were waited for; matrix products, arithmetic and copies ran while one was open for 1% of the time, Pallas kernels for 5%

profile of v1, /device:TPU:1, one launch (start us, length us, event | category | flops | bytes accessed | tf_op | source)
XLA Modules:
  0.0 242.9 jit_solution(783952917530830090)
XLA Ops:
  3.5 1.9 slots.1
  5.4 29.7 %all_to_all.31 = s32[128,1,64]{2,1,0:T(1,128)S(1)} all-to-all(s32[128,1,64]{2,1,0:T(1,128)S(1)} %bitcast.24), channel_id=1, replica_groups=mesh['dp_0'=8,'dp_1'=8,'dp_2'=2,'mp'=4] {'dp_0','dp_1','dp_2'}, dimensions={0} | all-to-all | bytes 65536 | tf_op jit(solution)/shard_map/all_to_all | solution.py:272
  37.0 6.1 %fetch.1 = bf16[128,64,128]{2,1,0:T(8,128)(2,1)} custom-call(s32[128,64]{1,0:T(8,128)S(1)} %bitcast.22, s32[4,512]{1,0:T(4,128)S(1)} %copy-done.8, f32[4,512,128]{2,1,0:T(8,128)S(1)} %copy-done), custom_call_target="tpu_custom_call" | custom-call | tf_op jit(solution)/shard_map/fetch/pallas_call | solution.py:325
  43.1 5.9 %all-to-all-start.1 = ((bf16[128,64,128]{2,1,0:T(8,128)(2,1)}), bf16[128,64,128]{2,1,0:T(8,128)(2,1)S(1)}, u32[]{:S(2)}, u32[]{:S(2)}) async-start(bf16[128,64,128]{2,1,0:T(8,128)(2,1)} %fetch.1), calls=%async_computation.1 | async-start | bytes 4194304 | tf_op jit(solution)/shard_map/all_to_all | solution.py:272
  49.0 3.1 %collective-permute-start = (bf16[2048,256]{1,0:T(8,128)(2,1)S(1)}, bf16[2048,256]{1,0:T(8,128)(2,1)}, u32[]{:S(2)}, u32[]{:S(2)}) collective-permute-start(bf16[2048,256]{1,0:T(8,128)(2,1)S(1)} %copy-done.2), channel_id=1, source_target_pairs={{0,1},{1,2},{2,3},{3,0},{4,5},{5,6},{6,7},{7,4},{8,9},{9,10},{10,1... | collective-permute-start | bytes 3145736 | tf_op jit(solution)/shard_map/ppermute | solution.py:282
  52.1 4.4 %collective-permute-start.1 = (bf16[2048,256]{1,0:T(8,128)(2,1)S(1)}, bf16[2048,256]{1,0:T(8,128)(2,1)}, u32[]{:S(2)}, u32[]{:S(2)}) collective-permute-start(bf16[2048,256]{1,0:T(8,128)(2,1)S(1)} %copy-done.2), channel_id=1, source_target_pairs={{0,2},{1,3},{2,0},{3,1},{4,6},{5,7},{6,4},{7,5},{8,10},{9,11},{10,... | collective-permute-start | bytes 3145736 | tf_op jit(solution)/shard_map/ppermute | solution.py:282
  56.5 3.1 %collective-permute-start.2 = (bf16[2048,256]{1,0:T(8,128)(2,1)S(1)}, bf16[2048,256]{1,0:T(8,128)(2,1)}, u32[]{:S(2)}, u32[]{:S(2)}) collective-permute-start(bf16[2048,256]{1,0:T(8,128)(2,1)S(1)} %copy-done.2), channel_id=1, source_target_pairs={{0,3},{1,0},{2,1},{3,2},{4,7},{5,4},{6,5},{7,6},{8,11},{9,8},{10,9... | collective-permute-start | bytes 3145736 | tf_op jit(solution)/shard_map/ppermute | solution.py:282
  59.6 1.7 samples.1
  62.0 1.3 copy-done.14
  63.3 37.1 %all-to-all-done.1.rows_ref = bf16[128,64,128]{2,1,0:T(8,128)(2,1)S(1)} async-done(((bf16[128,64,128]{2,1,0:T(8,128)(2,1)}), bf16[128,64,128]{2,1,0:T(8,128)(2,1)S(1)}, u32[]{:S(2)}, u32[]{:S(2)}) %all-to-all-start.1) | async-done | bytes 2097184 | tf_op jit(solution)/shard_map/all_to_all | solution.py:272
  101.3 1.5 pool.1
  103.7 4.0 %all-to-all-start.2 = ((bf16[4,128,512]{2,1,0:T(8,128)(2,1)}), bf16[4,128,512]{2,1,0:T(8,128)(2,1)S(1)}, u32[]{:S(2)}, u32[]{:S(2)}) async-start(bf16[4,128,512]{2,1,0:T(8,128)(2,1)} %broadcast_in_dim.4), calls=%async_computation.2 | async-start | bytes 1048576 | tf_op jit(solution)/shard_map/all_to_all | solution.py:272
  107.7 3.4 %collective-permute-start.3 = (f32[1,256]{1,0:T(1,128)S(1)}, f32[1,256]{1,0:T(1,128)S(1)}, u32[]{:S(2)}, u32[]{:S(2)}) collective-permute-start(f32[1,256]{1,0:T(1,128)S(1)} %bitcast.28), channel_id=1, source_target_pairs={{0,1},{1,2},{2,3},{3,0},{4,5},{5,6},{6,7},{7,4},{8,9},{9,10},{10,1... | collective-permute-start | bytes 3080 | tf_op jit(solution)/shard_map/ppermute | solution.py:282
  111.1 4.3 %collective-permute-start.4 = (f32[1,256]{1,0:T(1,128)S(1)}, f32[1,256]{1,0:T(1,128)S(1)}, u32[]{:S(2)}, u32[]{:S(2)}) collective-permute-start(f32[1,256]{1,0:T(1,128)S(1)} %bitcast.29), channel_id=1, source_target_pairs={{0,2},{1,3},{2,0},{3,1},{4,6},{5,7},{6,4},{7,5},{8,10},{9,11},{10,... | collective-permute-start | bytes 3080 | tf_op jit(solution)/shard_map/ppermute | solution.py:282
  115.4 3.1 %collective-permute-start.5 = (f32[1,256]{1,0:T(1,128)S(1)}, f32[1,256]{1,0:T(1,128)S(1)}, u32[]{:S(2)}, u32[]{:S(2)}) collective-permute-start(f32[1,256]{1,0:T(1,128)S(1)} %bitcast.30), channel_id=1, source_target_pairs={{0,3},{1,0},{2,1},{3,2},{4,7},{5,4},{6,5},{7,6},{8,11},{9,8},{10,9... | collective-permute-start | bytes 3080 | tf_op jit(solution)/shard_map/ppermute | solution.py:282
  118.7 1.3 collective-permute-done.5.u3
  120.1 3.7 %dense.1 = (f32[128,128]{1,0:T(8,128)S(1)}, f32[128,512]{1,0:T(8,128)S(1)}, bf16[2048,128]{1,0:T(8,128)(2,1)S(1)}, bf16[2048,128]{1,0:T(8,128)(2,1)S(1)}) custom-call(s32[2]{0:T(128)S(1)} %pad_add_fusion.at_ref, bf16[4,128,512]{2,1,0:T(8,128)(2,1)S(1)} %all-to-all-done.2.feat_ref, bf16[2048,256]{1,0:T(8,128)(2,1)S(1)} %copy-done.2, ...), custom_call_target="tpu_custom_call" | custom-call | tf_op jit(solution)/shard_map/dense/pallas_call | solution.py:371
  123.7 6.1 %collective-permute-start.6 = (bf16[2048,128]{1,0:T(8,128)(2,1)S(1)}, bf16[2048,128]{1,0:T(8,128)(2,1)S(1)}, u32[]{:S(2)}, u32[]{:S(2)}) collective-permute-start(bf16[2048,128]{1,0:T(8,128)(2,1)S(1)} %get-tuple-element.27), channel_id=1, source_target_pairs={{0,4},{4,0},{1,5},{5,1},{2,6},{6,2},{3,7},{7,3},{8,12},{12,8},{9,1... | collective-permute-start | bytes 1572872 | tf_op jit(solution)/shard_map/ppermute | solution.py:282
  129.8 1.4 spread.1
  131.6 68.5 %all_to_all.32.grads_ref = bf16[128,80,128]{2,1,0:T(8,128)(2,1)S(1)} all-to-all(bf16[128,80,128]{2,1,0:T(8,128)(2,1)S(1)} %constant_dynamic-update-slice_fusion), channel_id=1, replica_groups=mesh['dp_0'=8,'dp_1'=8,'dp_2'=2,'mp'=4] {'dp_0','dp_1','dp_2'}, dimensions={0} | all-to-all | bytes 5242880 | tf_op jit(solution)/shard_map/all_to_all | solution.py:272
  201.1 9.2 %all-to-all-start.4 = ((bf16[64,2,2,8,128]{4,3,2,1,0:T(8,128)(2,1)}), bf16[64,2,2,8,128]{4,3,2,1,0:T(8,128)(2,1)S(1)}, u32[]{:S(2)}, u32[]{:S(2)}) async-start(bf16[64,2,2,8,128]{4,3,2,1,0:T(8,128)(2,1)} %broadcast_in_dim.5), calls=%async_computation.4 | async-start | bytes 1048576 | tf_op jit(solution)/shard_map/all_to_all | solution.py:272
  210.3 17.5 %all-to-all-done.4 = bf16[64,2,2,8,128]{4,3,2,1,0:T(8,128)(2,1)S(1)} async-done(((bf16[64,2,2,8,128]{4,3,2,1,0:T(8,128)(2,1)}), bf16[64,2,2,8,128]{4,3,2,1,0:T(8,128)(2,1)S(1)}, u32[]{:S(2)}, u32[]{:S(2)}) %all-to-all-start.4) | async-done | bytes 524320 | tf_op jit(solution)/shard_map/all_to_all | solution.py:272
  227.9 5.1 %collective-permute-start.7 = (bf16[1024,256]{1,0:T(8,128)(2,1)S(1)}, bf16[1024,256]{1,0:T(8,128)(2,1)S(1)}, u32[]{:S(2)}, u32[]{:S(2)}) collective-permute-start(bf16[1024,256]{1,0:T(8,128)(2,1)S(1)} %bitcast.33), channel_id=1, source_target_pairs={{0,4},{4,0},{1,5},{5,1},{2,6},{6,2},{3,7},{7,3},{8,12},{12,8},{9,1... | collective-permute-start | bytes 1572872 | tf_op jit(solution)/shard_map/ppermute | solution.py:282
  234.6 7.2 %update.1 = (f32[4,512,128]{2,1,0:T(8,128)}, f32[4,512]{1,0:T(4,128)}) custom-call(bf16[128,80,128]{2,1,0:T(8,128)(2,1)S(1)} %all_to_all.32.grads_ref, f32[4,8,2048]{2,1,0:T(8,128)S(1)} %wanted.1.wanted_ref, f32[4,512,128]{2,1,0:T(8,128)S(1)} %copy-done.1, s32[4,512]{1,0:T(4,128)S(1)} %copy-done.9, f32[4,512]{1,0:T(4,128)S(1)} %copy-done.13), custom_call_target="tpu_custom_call" | custom-call | flops 4294967296 | bytes 1048576 | tf_op jit(solution)/shard_map/update/pallas_call | solution.py:414
  (53 shorter events, 11.6 us)
Async XLA Ops:
  0.6 0.7 copy-start.5
  1.4 0.7 copy-start.6
  2.1 0.7 copy-start.7
  35.1 1.2 copy-start
  43.1 5.9 %copy-start.2 = (bf16[2048,256]{1,0:T(8,128)(2,1)S(1)}, bf16[2048,256]{1,0:T(8,128)(2,1)}, u32[]{:S(2)}) copy-start(bf16[2048,256]{1,0:T(8,128)(2,1)} %w0) | copy-start | bytes 3145732
  43.1 57.3 %all-to-all-start.1 = ((bf16[128,64,128]{2,1,0:T(8,128)(2,1)}), bf16[128,64,128]{2,1,0:T(8,128)(2,1)S(1)}, u32[]{:S(2)}, u32[]{:S(2)}) async-start(bf16[128,64,128]{2,1,0:T(8,128)(2,1)} %fetch.1), calls=%async_computation.1 | async-start | bytes 4194304 | tf_op jit(solution)/shard_map/all_to_all | solution.py:272
  49.0 71.0 %collective-permute-start = (bf16[2048,256]{1,0:T(8,128)(2,1)S(1)}, bf16[2048,256]{1,0:T(8,128)(2,1)}, u32[]{:S(2)}, u32[]{:S(2)}) collective-permute-start(bf16[2048,256]{1,0:T(8,128)(2,1)S(1)} %copy-done.2), channel_id=1, source_target_pairs={{0,1},{1,2},{2,3},{3,0},{4,5},{5,6},{6,7},{7,4},{8,9},{9,10},{10,1... | collective-permute-start | bytes 3145736 | tf_op jit(solution)/shard_map/ppermute | solution.py:282
  52.1 67.9 %collective-permute-start.1 = (bf16[2048,256]{1,0:T(8,128)(2,1)S(1)}, bf16[2048,256]{1,0:T(8,128)(2,1)}, u32[]{:S(2)}, u32[]{:S(2)}) collective-permute-start(bf16[2048,256]{1,0:T(8,128)(2,1)S(1)} %copy-done.2), channel_id=1, source_target_pairs={{0,2},{1,3},{2,0},{3,1},{4,6},{5,7},{6,4},{7,5},{8,10},{9,11},{10,... | collective-permute-start | bytes 3145736 | tf_op jit(solution)/shard_map/ppermute | solution.py:282
  56.5 63.5 %collective-permute-start.2 = (bf16[2048,256]{1,0:T(8,128)(2,1)S(1)}, bf16[2048,256]{1,0:T(8,128)(2,1)}, u32[]{:S(2)}, u32[]{:S(2)}) collective-permute-start(bf16[2048,256]{1,0:T(8,128)(2,1)S(1)} %copy-done.2), channel_id=1, source_target_pairs={{0,3},{1,0},{2,1},{3,2},{4,7},{5,4},{6,5},{7,6},{8,11},{9,8},{10,9... | collective-permute-start | bytes 3145736 | tf_op jit(solution)/shard_map/ppermute | solution.py:282
  61.9 1.3 copy-start.14
  100.4 1.0 copy-start.4
  101.3 6.4 %copy-start.11 = (f32[256]{0:T(256)S(1)}, f32[256]{0:T(256)}, u32[]{:S(2)}) copy-start(f32[256]{0:T(256)} %param.18) | copy-start | bytes 3076
  101.3 17.2 %copy-start.12 = (s32[128]{0:T(128)S(1)}, s32[128]{0:T(128)}, u32[]{:S(2)}) copy-start(s32[128]{0:T(128)} %param.19) | copy-start | bytes 1540
  103.7 16.3 %all-to-all-start.2 = ((bf16[4,128,512]{2,1,0:T(8,128)(2,1)}), bf16[4,128,512]{2,1,0:T(8,128)(2,1)S(1)}, u32[]{:S(2)}, u32[]{:S(2)}) async-start(bf16[4,128,512]{2,1,0:T(8,128)(2,1)} %broadcast_in_dim.4), calls=%async_computation.2 | async-start | bytes 1048576 | tf_op jit(solution)/shard_map/all_to_all | solution.py:272
  107.7 7.7 %collective-permute-start.3 = (f32[1,256]{1,0:T(1,128)S(1)}, f32[1,256]{1,0:T(1,128)S(1)}, u32[]{:S(2)}, u32[]{:S(2)}) collective-permute-start(f32[1,256]{1,0:T(1,128)S(1)} %bitcast.28), channel_id=1, source_target_pairs={{0,1},{1,2},{2,3},{3,0},{4,5},{5,6},{6,7},{7,4},{8,9},{9,10},{10,1... | collective-permute-start | bytes 3080 | tf_op jit(solution)/shard_map/ppermute | solution.py:282
  111.1 7.6 %collective-permute-start.4 = (f32[1,256]{1,0:T(1,128)S(1)}, f32[1,256]{1,0:T(1,128)S(1)}, u32[]{:S(2)}, u32[]{:S(2)}) collective-permute-start(f32[1,256]{1,0:T(1,128)S(1)} %bitcast.29), channel_id=1, source_target_pairs={{0,2},{1,3},{2,0},{3,1},{4,6},{5,7},{6,4},{7,5},{8,10},{9,11},{10,... | collective-permute-start | bytes 3080 | tf_op jit(solution)/shard_map/ppermute | solution.py:282
  115.4 4.6 %collective-permute-start.5 = (f32[1,256]{1,0:T(1,128)S(1)}, f32[1,256]{1,0:T(1,128)S(1)}, u32[]{:S(2)}, u32[]{:S(2)}) collective-permute-start(f32[1,256]{1,0:T(1,128)S(1)} %bitcast.30), channel_id=1, source_target_pairs={{0,3},{1,0},{2,1},{3,2},{4,7},{5,4},{6,5},{7,6},{8,11},{9,8},{10,9... | collective-permute-start | bytes 3080 | tf_op jit(solution)/shard_map/ppermute | solution.py:282
  120.0 9.8 %copy-start.15 = (bf16[4,2048,128]{2,1,0:T(8,128)(2,1)S(1)}, bf16[4,2048,128]{2,1,0:T(8,128)(2,1)}, u32[]{:S(2)}) copy-start(bf16[4,2048,128]{2,1,0:T(8,128)(2,1)} %copy-done.14) | copy-start | bytes 6291460
  123.7 7.6 %collective-permute-start.6 = (bf16[2048,128]{1,0:T(8,128)(2,1)S(1)}, bf16[2048,128]{1,0:T(8,128)(2,1)S(1)}, u32[]{:S(2)}, u32[]{:S(2)}) collective-permute-start(bf16[2048,128]{1,0:T(8,128)(2,1)S(1)} %get-tuple-element.27), channel_id=1, source_target_pairs={{0,4},{4,0},{1,5},{5,1},{2,6},{6,2},{3,7},{7,3},{8,12},{12,8},{9,1... | collective-permute-start | bytes 1572872 | tf_op jit(solution)/shard_map/ppermute | solution.py:282
  201.1 26.8 %all-to-all-start.4 = ((bf16[64,2,2,8,128]{4,3,2,1,0:T(8,128)(2,1)}), bf16[64,2,2,8,128]{4,3,2,1,0:T(8,128)(2,1)S(1)}, u32[]{:S(2)}, u32[]{:S(2)}) async-start(bf16[64,2,2,8,128]{4,3,2,1,0:T(8,128)(2,1)} %broadcast_in_dim.5), calls=%async_computation.4 | async-start | bytes 1048576 | tf_op jit(solution)/shard_map/all_to_all | solution.py:272
  227.9 6.8 %copy-start.1 = (f32[4,512,128]{2,1,0:T(8,128)S(1)}, f32[4,512,128]{2,1,0:T(8,128)}, u32[]{:S(2)}) copy-start(f32[4,512,128]{2,1,0:T(8,128)} %emb_ref.3) | copy-start | bytes 3145732
  227.9 6.8 %copy-start.9 = (s32[4,512]{1,0:T(4,128)S(1)}, s32[4,512]{1,0:T(4,128)}, u32[]{:S(2)}) copy-start(s32[4,512]{1,0:T(4,128)} %expired_ref.3) | copy-start | bytes 24580
  227.9 6.8 %copy-start.13 = (f32[4,512]{1,0:T(4,128)S(1)}, f32[4,512]{1,0:T(4,128)}, u32[]{:S(2)}) copy-start(f32[4,512]{1,0:T(4,128)} %acc_ref.1) | copy-start | bytes 24580
  227.9 13.9 %collective-permute-start.7 = (bf16[1024,256]{1,0:T(8,128)(2,1)S(1)}, bf16[1024,256]{1,0:T(8,128)(2,1)S(1)}, u32[]{:S(2)}, u32[]{:S(2)}) collective-permute-start(bf16[1024,256]{1,0:T(8,128)(2,1)S(1)} %bitcast.33), channel_id=1, source_target_pairs={{0,4},{4,0},{1,5},{5,1},{2,6},{6,2},{3,7},{7,3},{8,12},{12,8},{9,1... | collective-permute-start | bytes 1572872 | tf_op jit(solution)/shard_map/ppermute | solution.py:282
  (3 other events, 2.1 us)

commit v2 on v1

--- a/solution.py
+++ b/solution.py
@@ -1,3 +1,5 @@
+import functools
+
 import jax
 import jax.numpy as jnp
 from jax import lax
@@ -80,23 +82,33 @@
         inv_ref[t] = jnp.broadcast_to(column, (toks, toks))
 
 
-def spread_rows(length, groups, cap, start):
-    return flag((iota((length, groups), 0) + start) // cap == iota((length, groups), 1))
+def spread_rows(length, groups, cap):
+    return flag(iota((length, groups), 0) // cap == iota((length, groups), 1))
+
+
+def own_lines(table, slots):
+    groups, lanes = table.shape
+    cap = slots // groups
+    every = dot(spread_rows(slots, groups, cap), table)
+    rank = iota((slots, lanes), 0) % cap
+    return jnp.where(iota((slots, lanes), 1) % cap == rank, every, 0.0).astype(BF16)
+
+
+def of_table(shape, lane_dim, t, kind, width, cap):
+    lane = iota(shape, lane_dim)
+    return flag((lane // width == kind) & (lane % width // cap == t))
 
 
 def samples_kernel(sample_ref, pick_ref, row_ref):
     tabs, slots, toks = pick_ref.shape
-    groups, width = sample_ref.shape
+    width = sample_ref.shape[1]
     cap = width // tabs
-    spread = spread_rows(slots, groups, cap, 0)
-    every = dot(spread, sample_ref[...].astype(BF16))
-    place = iota((slots, width), 0) % cap
-    lane = iota((slots, width), 1)
+    own = own_lines(sample_ref[...].astype(BF16), slots)
     wanted = (iota((slots, toks), 1) + 1).astype(F32)
     for t in range(tabs):
-        own = jnp.where(lane == place + t * cap, every, 0.0).astype(BF16)
-        pick_ref[t] = flag(dot(own, jnp.ones((width, toks), BF16)) == wanted)
-        row_ref[t] = dot(jnp.ones((8, width), BF16), own, NT)
+        mine = of_table((width, toks), 0, t, 0, width, cap)
+        pick_ref[t] = flag(dot(own, mine) == wanted)
+        row_ref[t] = dot(of_table((8, width), 1, t, 0, width, cap), own, NT)
 
 
 def labels_kernel(label_ref, out_ref):
@@ -108,61 +120,90 @@
     out_ref[...] = jnp.broadcast_to(column, dims)
 
 
+def rows_kernel(expired_ref, emb_ref, out_ref):
+    tabs, rows, emb = emb_ref.shape
+    diag = iota((emb, emb), 0) == iota((emb, emb), 1)
+    for t in range(tabs):
+        for j in range(0, rows, emb):
+            gone = expired_ref[t : t + 1, j : j + emb].astype(F32)
+            column = jnp.sum(jnp.where(diag, gone, 0.0), axis=1, keepdims=True)
+            out_ref[t, j : j + emb, :] = jnp.where(
+                column > 0.5, 0.0, emb_ref[t, j : j + emb, :]
+            ).astype(BF16)
+
+
 def halves_of(arrived):
     return jnp.concatenate(
-        [(arrived >> 4).astype(F32), (arrived & 15).astype(F32)], axis=1
+        [(arrived >> 7).astype(F32), (arrived & 127).astype(F32)], axis=1
     ).astype(BF16)
 
 
-def fetch_kernel(arrived_ref, expired_ref, emb_ref, out_ref):
+def fetch_kernel(arrived_ref, rows_ref, out_ref, own_ref):
     groups, width = arrived_ref.shape
-    rows, emb = emb_ref.shape[1:]
+    rows, emb = rows_ref.shape[1:]
     cap = out_ref.shape[1]
+    slots = groups * cap
     t = pl.program_id(0)
-    halves = halves_of(arrived_ref[...])
-    table = emb_ref[0].astype(BF16)
-    scale = jnp.where(iota((2 * width, emb), 0) < width, 16.0, 1.0).astype(BF16)
-    gone = expired_ref[pl.ds(t, 1), :]
-    names = jnp.where(gone == 1, -1.0, iota((1, rows), 1).astype(F32))
-    part = 32
-    for c in range(groups // part):
-        length = part * cap
-        spread = spread_rows(length, groups, cap, c * length)
-        every = dot(spread, halves)
-        lane = iota((length, 2 * width), 1) & (width - 1)
-        own = jnp.where(
-            lane == iota((length, 2 * width), 0) % cap + t * cap, every, 0.0
-        ).astype(BF16)
-        wanted = dot(own, scale)
+
+    @pl.when(t == 0)
+    def _():
+        own_ref[...] = own_lines(halves_of(arrived_ref[...]), slots)
+
+    lanes = (2 * width, emb)
+    which = jnp.concatenate(
+        [of_table(lanes, 0, t, 1, width, cap), of_table(lanes, 0, t, 0, width, cap)],
+        axis=1,
+    )
+    part = slots // 4
+    lane = iota((16, emb), 1).astype(F32).astype(BF16)
+    lane = jnp.concatenate([lane] * (part // 16), axis=0)
+    one, zero = jnp.ones((part, emb), BF16), jnp.zeros((part, emb), BF16)
+    for c in range(0, slots, part):
+        found = dot(own_ref[c : c + part, :], which)
+        hot = jnp.where(found[:, :emb].astype(BF16) == lane, one, zero)
+        at = found[:, emb:].astype(BF16)
         pick = jnp.concatenate(
-            [flag(wanted == names[:, j : j + emb]) for j in range(0, rows, emb)], axis=1
+            [jnp.where(at == jnp.full_like(at, j), hot, zero) for j in range(rows // emb)],
+            axis=1,
         )
-        out_ref[c * part : (c + 1) * part] = (
-            dot(pick, table).astype(BF16).reshape(part, cap, emb)
+        out_ref[c // cap : (c + part) // cap] = (
+            dot(pick, rows_ref[0]).astype(BF16).reshape(part // cap, cap, emb)
         )
 
 
 def wanted_kernel(arrived_ref, row_ref):
-    groups, width = arrived_ref.shape
-    tabs, eight, slots = row_ref.shape
+    width = arrived_ref.shape[1]
+    tabs, _, slots = row_ref.shape
     cap = width // tabs
-    every = dot(spread_rows(slots, groups, cap, 0), halves_of(arrived_ref[...]))
-    place = iota((slots, 2 * width), 0) % cap
-    lane = iota((slots, 2 * width), 1) & (width - 1)
-    scale = jnp.where(iota((eight, 2 * width), 1) < width, 16.0, 1.0).astype(BF16)
+    own = own_lines(halves_of(arrived_ref[...]), slots)
     for t in range(tabs):
-        own = jnp.where(lane == place + t * cap, every, 0.0).astype(BF16)
-        row_ref[t] = dot(scale, own, NT)
+        for kind in range(2):
+            row_ref[t, 8 * kind : 8 * kind + 8, :] = dot(
+                of_table((8, 2 * width), 1, t, kind, width, cap), own, NT
+            )
+
+
+def sublanes(length, wide):
+    column = iota((length, 128), 0).astype(F32).astype(BF16)
+    return jnp.concatenate([column] * (wide // 128), axis=1)
+
+
+def down(row, length):
+    return jnp.concatenate([row] * (length // 8), axis=0).astype(BF16)
 
 
 def pool_kernel(rows_ref, sample_ref, inv_ref, out_ref):
     groups, cap, emb = rows_ref.shape
     toks = inv_ref.shape[1]
     slots = groups * cap
-    wanted = (iota((toks, slots), 0) + 1).astype(F32)
-    pick = flag(sample_ref[0, 0:1, :] == wanted)
+    row = down(sample_ref[0] - 1.0, 16)
+    row = jnp.concatenate([row] * (toks // 16), axis=0)
+    one, zero = jnp.ones((toks, slots), BF16), jnp.zeros((toks, slots), BF16)
+    pick = jnp.where(row == sublanes(toks, slots), one, zero)
     pooled = dot(pick, rows_ref[...].reshape(slots, emb))
-    out_ref[...] = (pooled * inv_ref[0]).astype(BF16)
+    feature = (pooled * inv_ref[0]).astype(BF16)
+    for k in range(out_ref.shape[0]):
+        out_ref[k] = feature
 
 
 def silu_slope(preact):
@@ -172,15 +213,23 @@
 
 def dense_kernel(
     at_ref, feat_ref, w0, w1, w2, w3, u0, u1, u2, u3, labels_ref,
-    logits_ref, grad_ref, mine_ref, other_ref,
+    logits_ref, dhidden_ref, mine_ref, other_ref, held_ref, sem_ref,
 ):
     parts, toks, feats = feat_ref.shape
     weights, units = (w0, w1, w2, w3), (u0, u1, u2, u3)
+    copies = [
+        pltpu.make_async_copy(w, held_ref.at[k], sem_ref.at[k])
+        for k, w in enumerate(weights)
+    ]
+    for copy in copies:
+        copy.start()
     me, core = at_ref[0], at_ref[1]
     preacts, scores = [], []
-    for w, u in zip(weights, units):
+    for k, u in enumerate(units):
+        copies[k].wait()
         pre = sum(
-            dot(feat_ref[q], w[q * feats : (q + 1) * feats, :]) for q in range(parts)
+            dot(feat_ref[q], held_ref[k, q * feats : (q + 1) * feats, :])
+            for q in range(parts)
         )
         hidden = jax.nn.silu(pre).astype(BF16).astype(F32)
         preacts.append(pre)
@@ -194,31 +243,46 @@
         logits = logits + score
     dlogit = (jax.nn.sigmoid(logits) - labels_ref[...])[:, 0:1]
     logits_ref[...] = jnp.broadcast_to(logits, logits_ref.shape)
-    start = pl.multiple_of(me * feats, feats)
-    grads = jnp.zeros((toks, feats), F32)
-    for k, (w, u, pre) in enumerate(zip(weights, units, preacts)):
+    for k, (u, pre) in enumerate(zip(units, preacts)):
         dhidden = (dlogit * u[...] * silu_slope(pre)).astype(BF16)
+        dhidden_ref[k] = dhidden
         if k == 0:
             half = dhidden.shape[1] // 2
             low, high = dhidden[:, :half], dhidden[:, half:]
             mine, other = jnp.where(core == 0, low, high), jnp.where(core == 0, high, low)
+            both = jnp.concatenate([mine, other], axis=1)
             for q in range(parts):
                 lines = slice(q * feats, (q + 1) * feats)
-                part = dot(
-                    feat_ref[q],
-                    jnp.concatenate([mine, other], axis=1),
-                    (((0,), (0,)), ((), ())),
-                ).astype(BF16)
+                part = dot(feat_ref[q], both, (((0,), (0,)), ((), ()))).astype(BF16)
                 mine_ref[lines, :] = part[:, :half]
                 other_ref[lines, :] = part[:, half:]
-        grads = grads + dot(dhidden, w[pl.ds(start, feats), :], NT)
-    grad_ref[...] = grads
-
-
-def spread_kernel(grad_ref, inv_ref, pick_ref, out_ref):
+
+
+def spread_kernel(
+    at_ref, dhidden_ref, w0, w1, w2, w3, inv_ref, pick_ref, out_ref,
+    held_ref, grad_ref, sem_ref,
+):
+    parts, feats, _ = held_ref.shape
     slots = pick_ref.shape[1]
     cap, emb = out_ref.shape[1:]
-    grad = (inv_ref[0] * grad_ref[...]).astype(BF16)
+    t = pl.program_id(0)
+
+    @pl.when(t == 0)
+    def _():
+        start = pl.multiple_of(at_ref[0] * feats, feats)
+        copies = [
+            pltpu.make_async_copy(w.at[pl.ds(start, feats)], held_ref.at[k], sem_ref.at[k])
+            for k, w in enumerate((w0, w1, w2, w3))
+        ]
+        for copy in copies:
+            copy.start()
+        for copy in copies:
+            copy.wait()
+        grads = sum(dot(dhidden_ref[k], held_ref[k], NT) for k in range(parts))
+        for j in range(feats // emb):
+            grad_ref[j] = grads[:, j * emb : (j + 1) * emb]
+
+    grad = (inv_ref[0] * grad_ref[t]).astype(BF16)
     out_ref[...] = dot(pick_ref[0], grad).astype(BF16).reshape(slots // cap, cap, emb)
 
 
@@ -228,14 +292,18 @@
     slots = groups * cap
     t = pl.program_id(0)
     grads = grads_ref[...].reshape(slots, emb)
-    wanted = wanted_ref[0, 0:1, :]
+    at = down(wanted_ref[0, 0:8, :], 16)
+    low = down(wanted_ref[0, 8:16, :], 16)
+    low = jnp.concatenate([low] * (emb // 16), axis=0)
+    one, zero = jnp.ones((emb, slots), BF16), jnp.zeros((emb, slots), BF16)
+    hot = jnp.where(low == sublanes(emb, slots), one, zero)
     gone = expired_ref[pl.ds(t, 1), :]
     fresh_acc = jnp.where(gone == 1, ACC_RESET, acc_ref[pl.ds(t, 1), :])
     kept = jnp.where(gone == 1, 0.0, 1.0)
     diag = iota((emb, emb), 0) == iota((emb, emb), 1)
     for j in range(0, rows, emb):
-        names = (iota((emb, slots), 0) + j).astype(F32)
-        summed = dot(flag(wanted == names), grads)
+        here = jnp.concatenate([at == jnp.full_like(at, j // emb)] * (emb // 16), axis=0)
+        summed = dot(jnp.where(here, hot, zero), grads)
         cols = slice(j, j + emb)
         old = jnp.sum(jnp.where(diag, fresh_acc[:, cols], 0.0), axis=1, keepdims=True)
         keep = jnp.sum(jnp.where(diag, kept[:, cols], 0.0), axis=1, keepdims=True)
@@ -250,6 +318,18 @@
                 new_acc_ref[table : table + 1, cols] = line
 
 
+def join_kernel(at_ref, near_ref, far_ref, out_ref):
+    far, two, lines, half = near_ref.shape
+    first = at_ref[1] == 0
+    for c in range(2):
+        for side in range(two):
+            near, other = near_ref[:, side], far_ref[:, side]
+            part = jnp.where(first, near, other) if c == 0 else jnp.where(first, other, near)
+            out_ref[c * far * lines : (c + 1) * far * lines, side * half : (side + 1) * half] = (
+                part.reshape(far * lines, half)
+            )
+
+
 def shape(dims, dtype):
     return jax.ShapeDtypeStruct(dims, dtype)
 
@@ -270,11 +350,6 @@
 
 def a2a(value, axis):
     return lax.all_to_all(value, axis, split_axis=0, concat_axis=0, tiled=True)
-
-
-def from_everyone(value, axis):
-    size = lax.axis_size(axis)
-    return a2a(jnp.broadcast_to(value[None], (size, *value.shape)), axis)
 
 
 def ring(value, axis, step):
@@ -307,41 +382,57 @@
         compiler_params=params(24),
         name="slots",
     )(
-        bag_lengths,
-        owners[..., 0].swapaxes(1, 2),
-        row_slots.swapaxes(1, 2),
-        admit_mask.swapaxes(1, 2),
+        *map(
+            functools.partial(pltpu.with_memory_space_constraint, memory_space=pltpu.HBM),
+            (
+                bag_lengths,
+                owners[..., 0].swapaxes(1, 2),
+                row_slots.swapaxes(1, 2),
+                admit_mask.swapaxes(1, 2),
+            ),
+        )
     )
     arrived = a2a(request, DP)
     weight, _ = lax.optimization_barrier((hidden_weight, request))
     weights = [weight] + [ring(weight, "mp", k) for k in range(1, parts)]
     pick, sample_row = pl.pallas_call(
         samples_kernel,
-        out_shape=(shape((tabs, slots, toks), BF16), shape((tabs, 8, slots), F32)),
+        out_shape=(
+            pltpu.HBM((tabs, slots, toks), BF16),
+            pltpu.HBM((tabs, 8, slots), F32),
+        ),
         compiler_params=params(24),
         cost_estimate=cost(4 << 30),
         name="samples",
     )(sample)
+    held = functools.partial(pltpu.with_memory_space_constraint, memory_space=pltpu.HBM)
+    sent = pl.pallas_call(
+        rows_kernel,
+        out_shape=pltpu.HBM((tabs, rows, emb), BF16),
+        compiler_params=params(8),
+        cost_estimate=cost(1 << 30),
+        name="rows",
+    )(expired, held(embeddings))
     fetched = pl.pallas_call(
         fetch_kernel,
         grid=(tabs,),
         in_specs=[
             block((groups, width)),
-            block((tabs, rows)),
             block((1, rows, emb), lambda t: (t, 0, 0)),
         ],
         out_specs=block((groups, cap, emb), lambda t: (0, t, 0)),
         out_shape=pltpu.HBM((groups, width, emb), BF16),
+        scratch_shapes=[pltpu.VMEM((slots, 2 * width), BF16)],
         compiler_params=params(24),
         name="fetch",
-    )(arrived, expired, embeddings)
+    )(arrived, held(sent))
     returned = a2a(fetched, DP)
     unit, later = lax.optimization_barrier((output_weight, arrived))
     unit = unit.reshape(1, -1)
     units = [unit] + [ring(unit, "mp", k) for k in range(1, parts)]
     wanted = pl.pallas_call(
         wanted_kernel,
-        out_shape=shape((tabs, 8, slots), F32),
+        out_shape=pltpu.HBM((tabs, 16, slots), F32),
         compiler_params=params(24),
         cost_estimate=cost(4 << 30),
         name="wanted",
@@ -354,12 +445,12 @@
             block((1, 8, slots), lambda t: (t, 0, 0)),
             block((1, toks, toks), lambda t: (t, 0, 0)),
         ],
-        out_specs=block((toks, emb), lambda t: (0, t)),
-        out_shape=shape((toks, feats), BF16),
+        out_specs=block((parts, toks, emb), lambda t: (0, 0, t)),
+        out_shape=pltpu.HBM((parts, toks, feats), BF16),
         compiler_params=params(24),
         name="pool",
-    )(returned, sample_row, inv)
-    portion = from_everyone(features, "mp")
+    )(returned, held(sample_row), inv)
+    portion = a2a(features, "mp")
     label_column = pl.pallas_call(
         labels_kernel,
         out_shape=shape((toks, toks), F32),
@@ -368,55 +459,72 @@
     )(labels.reshape(1, toks))
     units_dev = hidden_weight.shape[1]
     lines, half = hidden_weight.shape[0], units_dev // 2
-    logits, grad, mine, other = pl.pallas_call(
+    smem, vmem, hbm = (
+        pl.BlockSpec(memory_space=space) for space in (pltpu.SMEM, pltpu.VMEM, pltpu.HBM)
+    )
+    logits, dhidden, mine, other = pl.pallas_call(
         dense_kernel,
-        in_specs=[pl.BlockSpec(memory_space=pltpu.SMEM)]
-        + [pl.BlockSpec(memory_space=pltpu.VMEM)] * (2 * parts + 2),
+        in_specs=[smem, vmem] + [hbm] * parts + [vmem] * (parts + 1),
         out_shape=(
             shape((toks, toks), F32),
-            shape((toks, feats), F32),
+            shape((parts, toks, units_dev), BF16),
             shape((lines, half), BF16),
             shape((lines, half), BF16),
         ),
+        scratch_shapes=[
+            pltpu.VMEM((parts, lines, units_dev), BF16),
+            pltpu.SemaphoreType.DMA((parts,)),
+        ],
         compiler_params=params(24),
         name="dense",
-    )(place, portion, *weights, *units, label_column)
+    )(place, portion, *map(held, weights), *units, label_column)
     joined = ring(other, NEAR, 1)
     share = lines // groups
     outgoing = pl.pallas_call(
         spread_kernel,
         grid=(tabs,),
         in_specs=[
-            block((toks, emb), lambda t: (0, t)),
+            smem,
+            block((parts, toks, units_dev)),
+            *[hbm] * parts,
             block((1, toks, toks), lambda t: (t, 0, 0)),
             block((1, slots, toks), lambda t: (t, 0, 0)),
         ],
         out_specs=block((groups, cap, emb), lambda t: (0, t, 0)),
         out_shape=shape((groups, width + share, emb), BF16),
+        scratch_shapes=[
+            pltpu.VMEM((parts, feats, units_dev), BF16),
+            pltpu.VMEM((tabs, toks, emb), F32),
+            pltpu.SemaphoreType.DMA((parts,)),
+        ],
         compiler_params=params(24),
         cost_estimate=cost(4 << 30),
         name="spread",
-    )(grad, inv, pick)
+    )(place, dhidden, *map(held, weights), inv, held(pick))
     pair = (mine.astype(F32) + joined.astype(F32)).astype(BF16)
     pair = pair.reshape(2, groups // 2, share, half).swapaxes(0, 1)
+    shares = a2a(pair, FAR)
+    own = shares.astype(F32).sum(axis=0).astype(BF16)
+    own = jnp.broadcast_to(own[None], (groups // 2, *own.shape))
     outgoing = lax.dynamic_update_slice(
-        outgoing, pair.reshape(groups, share, half), (0, width, 0)
+        outgoing, own.reshape(groups, share, half), (0, width, 0)
     )
     gradients = a2a(outgoing, DP)
-    shares = gradients[:, width:].reshape(groups // 2, 2, 2, share // 2, half)
-    own = shares.astype(F32).sum(axis=0).astype(BF16).swapaxes(0, 1)
-    near = from_everyone(own, FAR)
-    near = near.transpose(0, 1, 3, 2, 4).reshape(lines // 2, units_dev)
+    near = gradients[:, width:].reshape(groups // 2, 2, share, half)
     far = ring(near, NEAR, 1)
-    weight_grad = jnp.concatenate(
-        [jnp.where(core == 0, near, far), jnp.where(core == 0, far, near)]
-    )
+    weight_grad = pl.pallas_call(
+        join_kernel,
+        in_specs=[smem, vmem, vmem],
+        out_shape=shape((lines, units_dev), BF16),
+        compiler_params=params(8),
+        name="join",
+    )(place, near, far)
     new_rows, new_acc = pl.pallas_call(
         update_kernel,
         grid=(tabs,),
         in_specs=[
             block((groups, cap, emb), lambda t: (0, t, 0)),
-            block((1, 8, slots), lambda t: (t, 0, 0)),
+            block((1, 16, slots), lambda t: (t, 0, 0)),
             block((1, rows, emb), lambda t: (t, 0, 0)),
             block((tabs, rows)),
             block((tabs, rows)),
@@ -429,7 +537,7 @@
         compiler_params=params(24),
         cost_estimate=cost(4 << 30),
         name="update",
-    )(gradients, wanted, embeddings, expired, accumulator)
+    )(gradients, held(wanted), held(embeddings), expired, accumulator)
     return (new_rows, new_acc, weight_grad, logits[:, 0])
 
 

time: 244 us -> 244 us (level)
  the two profiles are of different devices: /device:TPU:1 before, /device:TPU:15 now
where the time goes in v2:
time: 244 us; the launch traced here: 243 us
  blocking collectives  72.4 us (30%)
  waiting for transfers between devices  67.6 us (28%)
  starting transfers between devices  58.8 us (24%)
  Pallas kernels  40 us (16%)
    all_to_all x1, blocking collectives, a2a(): return lax.all_to_all(value, axis, split_axis=0, concat_axis=0, tiled=True)  72.4 us
    all_to_all x4, waiting for transfers between devices, a2a(): return lax.all_to_all(value, axis, split_axis=0, concat_axis=0, tiled=True)  62.6 us
    all_to_all x4, starting transfers between devices, a2a(): return lax.all_to_all(value, axis, split_axis=0, concat_axis=0, tiled=True)  33.8 us
    ppermute x8, starting transfers between devices, ring(): lax.ppermute(value, axis, [(i, (i + step) % size) for i in range(size)])  25 us
    pallas_call x1, Pallas kernels, shards(): pl.pallas_call(update_kernel, grid=(tabs,), in_specs=[block((groups, cap,...  8.17 us
    pallas_call x1, Pallas kernels, shards(): pl.pallas_call(fetch_kernel, grid=(tabs,), in_specs=[block((groups, width...  6.11 us
    ppermute x8, waiting for transfers between devices, ring(): lax.ppermute(value, axis, [(i, (i + step) % size) for i in range(size)])  4.95 us
  transfers between devices with their start and end apart: 12, of which 5 were waited for; matrix products, arithmetic and copies ran while one was open for 0% of the time, Pallas kernels for 10%

profile of v2, /device:TPU:15, one launch (start us, length us, event | category | flops | bytes accessed | tf_op | source)
XLA Modules:
  0.0 243.3 jit_solution(14750088215148722683)
XLA Ops:
  0.6 3.3 %slots.1 = (s32[128,64]{1,0:T(8,128)}, f32[128,64]{1,0:T(8,128)S(1)}, f32[4,128,128]{2,1,0:T(8,128)S(1)}) custom-call(s32[4,128]{1,0:T(4,128)} %len_ref.1, s32[4,8,128]{2,1,0:T(8,128)} %bitcast.30, s32[4,8,128]{2,1,0:T(8,128)} %bitcast.31, s32[4,8,128]{2,1,0:T(8,128)} %bitcast.32), custom_call_target="tpu_custom_call" | custom-call | tf_op jit(solution)/shard_map/slots/pallas_call | solution.py:375
  3.9 17.6 %all-to-all-start = ((s32[128,1,64]{2,1,0:T(1,128)}), s32[128,1,64]{2,1,0:T(1,128)S(1)}, u32[]{:S(2)}, u32[]{:S(2)}) async-start(s32[128,1,64]{2,1,0:T(1,128)} %bitcast.7), calls=%async_computation | async-start | bytes 131072 | tf_op jit(solution)/shard_map/all_to_all | solution.py:352
  22.3 2.4 rows.1.rows_ref
  24.6 7.5 %all-to-all-done = s32[128,1,64]{2,1,0:T(1,128)S(1)} async-done(((s32[128,1,64]{2,1,0:T(1,128)}), s32[128,1,64]{2,1,0:T(1,128)S(1)}, u32[]{:S(2)}, u32[]{:S(2)}) %all-to-all-start) | async-done | bytes 32800 | tf_op jit(solution)/shard_map/all_to_all | solution.py:352
  32.1 6.1 %fetch.1 = bf16[128,64,128]{2,1,0:T(8,128)(2,1)} custom-call(s32[128,64]{1,0:T(8,128)S(1)} %bitcast.21, bf16[4,512,128]{2,1,0:T(8,128)(2,1)} %rows.1.rows_ref), custom_call_target="tpu_custom_call" | custom-call | tf_op jit(solution)/shard_map/fetch/pallas_call | solution.py:416
  38.3 6.6 %all-to-all-start.1 = ((bf16[128,64,128]{2,1,0:T(8,128)(2,1)}), bf16[128,64,128]{2,1,0:T(8,128)(2,1)S(1)}, u32[]{:S(2)}, u32[]{:S(2)}) async-start(bf16[128,64,128]{2,1,0:T(8,128)(2,1)} %fetch.1), calls=%async_computation.1 | async-start | bytes 4194304 | tf_op jit(solution)/shard_map/all_to_all | solution.py:352
  44.9 2.1 collective-permute-start
  47.0 4.1 %collective-permute-start.1 = (bf16[2048,256]{1,0:T(8,128)(2,1)}, bf16[2048,256]{1,0:T(8,128)(2,1)}, u32[]{:S(2)}, u32[]{:S(2)}) collective-permute-start(bf16[2048,256]{1,0:T(8,128)(2,1)} %w0.1), channel_id=1, source_target_pairs={{0,2},{1,3},{2,0},{3,1},{4,6},{5,7},{6,4},{7,5},{8,10},{9,11},{10,... | collective-permute-start | bytes 3145736 | tf_op jit(solution)/shard_map/ppermute | solution.py:357
  51.1 1.9 collective-permute-start.2
  53.0 2.8 %samples.1 = (bf16[4,2048,128]{2,1,0:T(8,128)(2,1)}, f32[4,8,2048]{2,1,0:T(8,128)}) custom-call(f32[128,64]{1,0:T(8,128)S(1)} %get-tuple-element.19.sample_ref), custom_call_target="tpu_custom_call" | custom-call | flops 4294967296 | bytes 1048576 | tf_op jit(solution)/shard_map/samples/pallas_call | solution.py:398
  55.9 42.2 %all-to-all-done.1.rows_ref = bf16[128,64,128]{2,1,0:T(8,128)(2,1)S(1)} async-done(((bf16[128,64,128]{2,1,0:T(8,128)(2,1)}), bf16[128,64,128]{2,1,0:T(8,128)(2,1)S(1)}, u32[]{:S(2)}, u32[]{:S(2)}) %all-to-all-start.1) | async-done | bytes 2097184 | tf_op jit(solution)/shard_map/all_to_all | solution.py:352
  98.1 3.7 %pool.1 = bf16[4,128,512]{2,1,0:T(8,128)(2,1)} custom-call(bf16[128,64,128]{2,1,0:T(8,128)(2,1)S(1)} %all-to-all-done.1.rows_ref, f32[4,8,2048]{2,1,0:T(8,128)} %get-tuple-element.20.sample_ref, f32[4,128,128]{2,1,0:T(8,128)S(1)} %get-tuple-element.21.inv_ref), custom_call_target="tpu_custom_call" | custom-call | tf_op jit(solution)/shard_map/pool/pallas_call | solution.py:440
  101.8 4.2 %all-to-all-start.2 = ((bf16[4,128,512]{2,1,0:T(8,128)(2,1)}), bf16[4,128,512]{2,1,0:T(8,128)(2,1)S(1)}, u32[]{:S(2)}, u32[]{:S(2)}) async-start(bf16[4,128,512]{2,1,0:T(8,128)(2,1)} %pool.1), calls=%async_computation.2 | async-start | bytes 1048576 | tf_op jit(solution)/shard_map/all_to_all | solution.py:352
  107.9 4.3 %collective-permute-start.4 = (f32[1,256]{1,0:T(1,128)S(1)}, f32[1,256]{1,0:T(1,128)S(1)}, u32[]{:S(2)}, u32[]{:S(2)}) collective-permute-start(f32[1,256]{1,0:T(1,128)S(1)} %bitcast.24), channel_id=1, source_target_pairs={{0,2},{1,3},{2,0},{3,1},{4,6},{5,7},{6,4},{7,5},{8,10},{9,11},{10,... | collective-permute-start | bytes 3080 | tf_op jit(solution)/shard_map/ppermute | solution.py:357
  114.3 3.4 %collective-permute-done.5.u3 = f32[1,256]{1,0:T(1,128)S(1)} collective-permute-done((f32[1,256]{1,0:T(1,128)S(1)}, f32[1,256]{1,0:T(1,128)S(1)}, u32[]{:S(2)}, u32[]{:S(2)}) %collective-permute-start.5) | collective-permute-done | bytes 1056 | tf_op jit(solution)/shard_map/ppermute | solution.py:357
  117.8 4.4 %dense.1 = (f32[128,128]{1,0:T(8,128)S(1)}, bf16[4,128,256]{2,1,0:T(8,128)(2,1)S(1)}, bf16[2048,128]{1,0:T(8,128)(2,1)S(1)}, bf16[2048,128]{1,0:T(8,128)(2,1)S(1)}) custom-call(s32[2]{0:T(128)S(1)} %pad_add_fusion.at_ref, bf16[4,128,512]{2,1,0:T(8,128)(2,1)S(1)} %all-to-all-done.2.feat_ref, bf16[2048,256]{1,0:T(8,128)(2,1)} %w0.1, ...), custom_call_target="tpu_custom_call" | custom-call | tf_op jit(solution)/shard_map/dense/pallas_call | solution.py:465
  122.2 5.5 %collective-permute-start.6 = (bf16[2048,128]{1,0:T(8,128)(2,1)S(1)}, bf16[2048,128]{1,0:T(8,128)(2,1)S(1)}, u32[]{:S(2)}, u32[]{:S(2)}) collective-permute-start(bf16[2048,128]{1,0:T(8,128)(2,1)S(1)} %get-tuple-element.27), channel_id=1, source_target_pairs={{0,4},{4,0},{1,5},{5,1},{2,6},{6,2},{3,7},{7,3},{8,12},{12,8},{9,1... | collective-permute-start | bytes 1572872 | tf_op jit(solution)/shard_map/ppermute | solution.py:357
  130.2 5.2 %all-to-all-start.3 = ((bf16[64,2,16,128]{3,2,1,0:T(8,128)(2,1)}), bf16[64,2,16,128]{3,2,1,0:T(8,128)(2,1)}, u32[]{:S(2)}, u32[]{:S(2)}) async-start(bf16[64,2,16,128]{3,2,1,0:T(8,128)(2,1)} %bitcast.18), calls=%async_computation.3 | async-start | bytes 1048576 | tf_op jit(solution)/shard_map/all_to_all | solution.py:352
  135.4 4.9 %spread.1 = bf16[128,80,128]{2,1,0:T(8,128)(2,1)S(1)} custom-call(s32[2]{0:T(128)S(1)} %pad_add_fusion.at_ref, bf16[4,128,256]{2,1,0:T(8,128)(2,1)S(1)} %get-tuple-element.24.dhidden_ref, bf16[2048,256]{1,0:T(8,128)(2,1)} %w0.1, bf16[2048,256]{1,0:T(8,128)(2,1)} %collective-permute-done.w1, bf16[2048,256]{1,0:T(8,128)(2,1)} %collective-permute-done.1.w2, ...), custom_call_target="tpu_custom_call" | custom-call | flops 4294967296 | bytes 1048576 | tf_op jit(solution)/shard_map/spread/pallas_call | solution.py:483
  140.3 12.9 %all-to-all-done.3 = bf16[64,2,16,128]{3,2,1,0:T(8,128)(2,1)} async-done(((bf16[64,2,16,128]{3,2,1,0:T(8,128)(2,1)}), bf16[64,2,16,128]{3,2,1,0:T(8,128)(2,1)}, u32[]{:S(2)}, u32[]{:S(2)}) %all-to-all-start.3) | async-done | bytes 524320 | tf_op jit(solution)/shard_map/all_to_all | solution.py:352
  154.6 72.4 %all_to_all.31.grads_ref = bf16[128,80,128]{2,1,0:T(8,128)(2,1)S(1)} all-to-all(bf16[128,80,128]{2,1,0:T(8,128)(2,1)S(1)} %constant_dynamic-update-slice_fusion), channel_id=1, replica_groups=mesh['dp_0'=8,'dp_1'=8,'dp_2'=2,'mp'=4] {'dp_0','dp_1','dp_2'}, dimensions={0} | all-to-all | bytes 5242880 | tf_op jit(solution)/shard_map/all_to_all | solution.py:352
  227.0 3.3 %collective-permute-start.7 = (bf16[64,2,16,128]{3,2,1,0:T(8,128)(2,1)S(1)}, bf16[64,2,16,128]{3,2,1,0:T(8,128)(2,1)S(1)}, u32[]{:S(2)}, u32[]{:S(2)}) collective-permute-start(bf16[64,2,16,128]{3,2,1,0:T(8,128)(2,1)S(1)} %bitcast.19), channel_id=1, source_target_pairs={{0,4},{4,0},{1,5},{5,1},{2,6},{6,2},{3,7},{7,3},{8,12},{12,8},{9,1... | collective-permute-start | bytes 1572872 | tf_op jit(solution)/shard_map/ppermute | solution.py:357
  230.3 2.4 wanted.1.wanted_ref
  233.3 8.2 %update.1 = (f32[4,512,128]{2,1,0:T(8,128)}, f32[4,512]{1,0:T(4,128)}) custom-call(bf16[128,80,128]{2,1,0:T(8,128)(2,1)S(1)} %all_to_all.31.grads_ref, f32[4,16,2048]{2,1,0:T(8,128)} %wanted.1.wanted_ref, f32[4,512,128]{2,1,0:T(8,128)} %emb_ref.3, s32[4,512]{1,0:T(4,128)S(1)} %copy-done.3, f32[4,512]{1,0:T(4,128)S(1)} %copy-done.4), custom_call_target="tpu_custom_call" | custom-call | flops 4294967296 | bytes 1048576 | tf_op jit(solution)/shard_map/update/pallas_call | solution.py:522
  (30 shorter events, 10.9 us)
Async XLA Ops:
  3.9 28.2 %all-to-all-start = ((s32[128,1,64]{2,1,0:T(1,128)}), s32[128,1,64]{2,1,0:T(1,128)S(1)}, u32[]{:S(2)}, u32[]{:S(2)}) async-start(s32[128,1,64]{2,1,0:T(1,128)} %bitcast.7), calls=%async_computation | async-start | bytes 131072 | tf_op jit(solution)/shard_map/all_to_all | solution.py:352
  21.6 0.7 copy-start.2
  38.3 59.8 %all-to-all-start.1 = ((bf16[128,64,128]{2,1,0:T(8,128)(2,1)}), bf16[128,64,128]{2,1,0:T(8,128)(2,1)S(1)}, u32[]{:S(2)}, u32[]{:S(2)}) async-start(bf16[128,64,128]{2,1,0:T(8,128)(2,1)} %fetch.1), calls=%async_computation.1 | async-start | bytes 4194304 | tf_op jit(solution)/shard_map/all_to_all | solution.py:352
  44.9 72.8 %collective-permute-start = (bf16[2048,256]{1,0:T(8,128)(2,1)}, bf16[2048,256]{1,0:T(8,128)(2,1)}, u32[]{:S(2)}, u32[]{:S(2)}) collective-permute-start(bf16[2048,256]{1,0:T(8,128)(2,1)} %w0.1), channel_id=1, source_target_pairs={{0,1},{1,2},{2,3},{3,0},{4,5},{5,6},{6,7},{7,4},{8,9},{9,10},{10,1... | collective-permute-start | bytes 3145736 | tf_op jit(solution)/shard_map/ppermute | solution.py:357
  47.0 70.7 %collective-permute-start.1 = (bf16[2048,256]{1,0:T(8,128)(2,1)}, bf16[2048,256]{1,0:T(8,128)(2,1)}, u32[]{:S(2)}, u32[]{:S(2)}) collective-permute-start(bf16[2048,256]{1,0:T(8,128)(2,1)} %w0.1), channel_id=1, source_target_pairs={{0,2},{1,3},{2,0},{3,1},{4,6},{5,7},{6,4},{7,5},{8,10},{9,11},{10,... | collective-permute-start | bytes 3145736 | tf_op jit(solution)/shard_map/ppermute | solution.py:357
  51.1 66.6 %collective-permute-start.2 = (bf16[2048,256]{1,0:T(8,128)(2,1)}, bf16[2048,256]{1,0:T(8,128)(2,1)}, u32[]{:S(2)}, u32[]{:S(2)}) collective-permute-start(bf16[2048,256]{1,0:T(8,128)(2,1)} %w0.1), channel_id=1, source_target_pairs={{0,3},{1,0},{2,1},{3,2},{4,7},{5,4},{6,5},{7,6},{8,11},{9,8},{10,9... | collective-permute-start | bytes 3145736 | tf_op jit(solution)/shard_map/ppermute | solution.py:357
  55.9 50.1 %copy-start = (f32[256]{0:T(256)S(1)}, f32[256]{0:T(256)}, u32[]{:S(2)}) copy-start(f32[256]{0:T(256)} %param.18) | copy-start | bytes 3076
  55.9 58.3 %copy-start.1 = (s32[128]{0:T(128)S(1)}, s32[128]{0:T(128)}, u32[]{:S(2)}) copy-start(s32[128]{0:T(128)} %param.19) | copy-start | bytes 1540
  101.8 16.0 %all-to-all-start.2 = ((bf16[4,128,512]{2,1,0:T(8,128)(2,1)}), bf16[4,128,512]{2,1,0:T(8,128)(2,1)S(1)}, u32[]{:S(2)}, u32[]{:S(2)}) async-start(bf16[4,128,512]{2,1,0:T(8,128)(2,1)} %pool.1), calls=%async_computation.2 | async-start | bytes 1048576 | tf_op jit(solution)/shard_map/all_to_all | solution.py:352
  106.0 6.2 %collective-permute-start.3 = (f32[1,256]{1,0:T(1,128)S(1)}, f32[1,256]{1,0:T(1,128)S(1)}, u32[]{:S(2)}, u32[]{:S(2)}) collective-permute-start(f32[1,256]{1,0:T(1,128)S(1)} %bitcast.23), channel_id=1, source_target_pairs={{0,1},{1,2},{2,3},{3,0},{4,5},{5,6},{6,7},{7,4},{8,9},{9,10},{10,1... | collective-permute-start | bytes 3080 | tf_op jit(solution)/shard_map/ppermute | solution.py:357
  107.9 6.4 %collective-permute-start.4 = (f32[1,256]{1,0:T(1,128)S(1)}, f32[1,256]{1,0:T(1,128)S(1)}, u32[]{:S(2)}, u32[]{:S(2)}) collective-permute-start(f32[1,256]{1,0:T(1,128)S(1)} %bitcast.24), channel_id=1, source_target_pairs={{0,2},{1,3},{2,0},{3,1},{4,6},{5,7},{6,4},{7,5},{8,10},{9,11},{10,... | collective-permute-start | bytes 3080 | tf_op jit(solution)/shard_map/ppermute | solution.py:357
  112.2 5.5 %collective-permute-start.5 = (f32[1,256]{1,0:T(1,128)S(1)}, f32[1,256]{1,0:T(1,128)S(1)}, u32[]{:S(2)}, u32[]{:S(2)}) collective-permute-start(f32[1,256]{1,0:T(1,128)S(1)} %bitcast.25), channel_id=1, source_target_pairs={{0,3},{1,0},{2,1},{3,2},{4,7},{5,4},{6,5},{7,6},{8,11},{9,8},{10,9... | collective-permute-start | bytes 3080 | tf_op jit(solution)/shard_map/ppermute | solution.py:357
  122.2 7.1 %collective-permute-start.6 = (bf16[2048,128]{1,0:T(8,128)(2,1)S(1)}, bf16[2048,128]{1,0:T(8,128)(2,1)S(1)}, u32[]{:S(2)}, u32[]{:S(2)}) collective-permute-start(bf16[2048,128]{1,0:T(8,128)(2,1)S(1)} %get-tuple-element.27), channel_id=1, source_target_pairs={{0,4},{4,0},{1,5},{5,1},{2,6},{6,2},{3,7},{7,3},{8,12},{12,8},{9,1... | collective-permute-start | bytes 1572872 | tf_op jit(solution)/shard_map/ppermute | solution.py:357
  130.2 23.1 %all-to-all-start.3 = ((bf16[64,2,16,128]{3,2,1,0:T(8,128)(2,1)}), bf16[64,2,16,128]{3,2,1,0:T(8,128)(2,1)}, u32[]{:S(2)}, u32[]{:S(2)}) async-start(bf16[64,2,16,128]{3,2,1,0:T(8,128)(2,1)} %bitcast.18), calls=%async_computation.3 | async-start | bytes 1048576 | tf_op jit(solution)/shard_map/all_to_all | solution.py:352
  227.0 6.3 %copy-start.3 = (s32[4,512]{1,0:T(4,128)S(1)}, s32[4,512]{1,0:T(4,128)}, u32[]{:S(2)}) copy-start(s32[4,512]{1,0:T(4,128)} %expired_ref.3) | copy-start | bytes 24580
  227.0 6.3 %copy-start.4 = (f32[4,512]{1,0:T(4,128)S(1)}, f32[4,512]{1,0:T(4,128)}, u32[]{:S(2)}) copy-start(f32[4,512]{1,0:T(4,128)} %acc_ref.1) | copy-start | bytes 24580
  227.0 14.4 %collective-permute-start.7 = (bf16[64,2,16,128]{3,2,1,0:T(8,128)(2,1)S(1)}, bf16[64,2,16,128]{3,2,1,0:T(8,128)(2,1)S(1)}, u32[]{:S(2)}, u32[]{:S(2)}) collective-permute-start(bf16[64,2,16,128]{3,2,1,0:T(8,128)(2,1)S(1)} %bitcast.19), channel_id=1, source_target_pairs={{0,4},{4,0},{1,5},{5,1},{2,6},{6,2},{3,7},{7,3},{8,12},{12,8},{9,1... | collective-permute-start | bytes 1572872 | tf_op jit(solution)/shard_map/ppermute | solution.py:357

commit v3 on v1

--- a/solution.py
+++ b/solution.py
@@ -1,3 +1,5 @@
+import functools
+
 import jax
 import jax.numpy as jnp
 from jax import lax
@@ -80,23 +82,35 @@
         inv_ref[t] = jnp.broadcast_to(column, (toks, toks))
 
 
-def spread_rows(length, groups, cap, start):
-    return flag((iota((length, groups), 0) + start) // cap == iota((length, groups), 1))
+def own_lines(table, slots):
+    groups, lanes = table.shape
+    cap = slots // groups
+    mine = iota((cap, lanes), 1) % cap == iota((cap, lanes), 0)
+    return jnp.concatenate(
+        [
+            jnp.where(mine, jnp.broadcast_to(table[o : o + 1], (cap, lanes)), 0.0)
+            for o in range(groups)
+        ],
+        axis=0,
+    ).astype(BF16)
+
+
+def of_table(shape, lane_dim, t, kind, width, cap):
+    lane = iota(shape, lane_dim)
+    return flag((lane // width == kind) & (lane % width // cap == t))
 
 
 def samples_kernel(sample_ref, pick_ref, row_ref):
     tabs, slots, toks = pick_ref.shape
-    groups, width = sample_ref.shape
+    width = sample_ref.shape[1]
     cap = width // tabs
-    spread = spread_rows(slots, groups, cap, 0)
-    every = dot(spread, sample_ref[...].astype(BF16))
-    place = iota((slots, width), 0) % cap
-    lane = iota((slots, width), 1)
+    own = own_lines(sample_ref[...], slots)
     wanted = (iota((slots, toks), 1) + 1).astype(F32)
     for t in range(tabs):
-        own = jnp.where(lane == place + t * cap, every, 0.0).astype(BF16)
-        pick_ref[t] = flag(dot(own, jnp.ones((width, toks), BF16)) == wanted)
-        row_ref[t] = dot(jnp.ones((8, width), BF16), own, NT)
+        mine = of_table((width, toks), 0, t, 0, width, cap)
+        pick_ref[t] = flag(dot(own, mine) == wanted)
+        row = dot(of_table((8, width), 1, t, 0, width, cap), own, NT)
+        row_ref[t : t + 1, :] = row[0:1]
 
 
 def labels_kernel(label_ref, out_ref):
@@ -108,61 +122,111 @@
     out_ref[...] = jnp.broadcast_to(column, dims)
 
 
-def halves_of(arrived):
+def rows_kernel(expired_ref, emb_ref, out_ref):
+    tabs, rows, emb = emb_ref.shape
+    diag = iota((emb, emb), 0) == iota((emb, emb), 1)
+    for t in range(tabs):
+        for j in range(0, rows, emb):
+            gone = expired_ref[t : t + 1, j : j + emb].astype(F32)
+            column = jnp.sum(jnp.where(diag, gone, 0.0), axis=1, keepdims=True)
+            out_ref[t, j : j + emb, :] = jnp.where(
+                column > 0.5, 0.0, emb_ref[t, j : j + emb, :]
+            ).astype(BF16)
+
+
+def halves_of(arrived, block_rows):
+    shift = block_rows.bit_length() - 1
     return jnp.concatenate(
-        [(arrived >> 4).astype(F32), (arrived & 15).astype(F32)], axis=1
-    ).astype(BF16)
-
-
-def fetch_kernel(arrived_ref, expired_ref, emb_ref, out_ref):
+        [(arrived >> shift).astype(F32), (arrived & (block_rows - 1)).astype(F32)], axis=1
+    )
+
+
+def fetch_kernel(arrived_ref, rows_ref, out_ref, table_ref, own_ref, sent_ref, in_sem, out_sem):
     groups, width = arrived_ref.shape
-    rows, emb = emb_ref.shape[1:]
-    cap = out_ref.shape[1]
-    t = pl.program_id(0)
-    halves = halves_of(arrived_ref[...])
-    table = emb_ref[0].astype(BF16)
-    scale = jnp.where(iota((2 * width, emb), 0) < width, 16.0, 1.0).astype(BF16)
-    gone = expired_ref[pl.ds(t, 1), :]
-    names = jnp.where(gone == 1, -1.0, iota((1, rows), 1).astype(F32))
-    part = 32
-    for c in range(groups // part):
-        length = part * cap
-        spread = spread_rows(length, groups, cap, c * length)
-        every = dot(spread, halves)
-        lane = iota((length, 2 * width), 1) & (width - 1)
-        own = jnp.where(
-            lane == iota((length, 2 * width), 0) % cap + t * cap, every, 0.0
-        ).astype(BF16)
-        wanted = dot(own, scale)
-        pick = jnp.concatenate(
-            [flag(wanted == names[:, j : j + emb]) for j in range(0, rows, emb)], axis=1
-        )
-        out_ref[c * part : (c + 1) * part] = (
-            dot(pick, table).astype(BF16).reshape(part, cap, emb)
-        )
+    tabs, rows, emb = rows_ref.shape
+    cap = width // tabs
+    slots = groups * cap
+    half = rows // 2
+    load = pltpu.make_async_copy(rows_ref, table_ref, in_sem)
+    load.start()
+    own_ref[...] = own_lines(halves_of(arrived_ref[...], half), slots)
+    lane = iota((16, emb), 1).astype(F32)
+    parts = out_sem.shape[0]
+    part = slots // parts
+    low = jnp.concatenate([lane.astype(BF16)] * (part // 16), axis=0)
+    high = jnp.concatenate([(lane + emb).astype(BF16)] * (part // 16), axis=0)
+    one, zero = jnp.ones((part, emb), BF16), jnp.zeros((part, emb), BF16)
+    lanes = (2 * width, emb)
+    stores = []
+    for c in range(parts):
+        own = own_ref[c * part : (c + 1) * part, :]
+        mine = slice(c * part // cap, (c + 1) * part // cap)
+        for t in range(tabs):
+            which = jnp.concatenate(
+                [of_table(lanes, 0, t, 1, width, cap), of_table(lanes, 0, t, 0, width, cap)],
+                axis=1,
+            )
+            found = dot(own, which)
+            at = found[:, :emb].astype(BF16)
+            pick = jnp.concatenate(
+                [jnp.where(at == low, one, zero), jnp.where(at == high, one, zero)], axis=1
+            )
+            if c == 0 and t == 0:
+                load.wait()
+            table = jnp.concatenate([table_ref[t, :half], table_ref[t, half:]], axis=1)
+            both = dot(pick, table).astype(BF16)
+            line = jnp.where(found[:, emb:].astype(BF16) == zero, both[:, :emb], both[:, emb:])
+            sent_ref[mine, t * cap : (t + 1) * cap, :] = line.reshape(part // cap, cap, emb)
+        store = pltpu.make_async_copy(sent_ref.at[mine], out_ref.at[mine], out_sem.at[c])
+        store.start()
+        stores.append(store)
+    for store in stores:
+        store.wait()
 
 
 def wanted_kernel(arrived_ref, row_ref):
-    groups, width = arrived_ref.shape
-    tabs, eight, slots = row_ref.shape
+    width = arrived_ref.shape[1]
+    tabs, _, slots = row_ref.shape
     cap = width // tabs
-    every = dot(spread_rows(slots, groups, cap, 0), halves_of(arrived_ref[...]))
-    place = iota((slots, 2 * width), 0) % cap
-    lane = iota((slots, 2 * width), 1) & (width - 1)
-    scale = jnp.where(iota((eight, 2 * width), 1) < width, 16.0, 1.0).astype(BF16)
+    own = own_lines(halves_of(arrived_ref[...], 128), slots)
     for t in range(tabs):
-        own = jnp.where(lane == place + t * cap, every, 0.0).astype(BF16)
-        row_ref[t] = dot(scale, own, NT)
-
-
-def pool_kernel(rows_ref, sample_ref, inv_ref, out_ref):
-    groups, cap, emb = rows_ref.shape
-    toks = inv_ref.shape[1]
+        for kind in range(2):
+            row_ref[t, 8 * kind : 8 * kind + 8, :] = dot(
+                of_table((8, 2 * width), 1, t, kind, width, cap), own, NT
+            )
+
+
+def sublanes(length, wide):
+    column = iota((length, 128), 0).astype(F32).astype(BF16)
+    return jnp.concatenate([column] * (wide // 128), axis=1)
+
+
+def down(row, length):
+    return jnp.concatenate([row] * (length // 8), axis=0).astype(BF16)
+
+
+def pool_kernel(rows_ref, sample_ref, inv_ref, out_ref, feature_ref, sem_ref):
+    groups, width, emb = rows_ref.shape
+    tabs, toks, _ = inv_ref.shape
+    cap = width // tabs
     slots = groups * cap
-    wanted = (iota((toks, slots), 0) + 1).astype(F32)
-    pick = flag(sample_ref[0, 0:1, :] == wanted)
-    pooled = dot(pick, rows_ref[...].reshape(slots, emb))
-    out_ref[...] = (pooled * inv_ref[0]).astype(BF16)
+    one, zero = jnp.ones((toks, slots), BF16), jnp.zeros((toks, slots), BF16)
+    samples = sublanes(toks, slots)
+    copies = []
+    for t in range(tabs):
+        row = jnp.broadcast_to(sample_ref[t : t + 1, :] - 1.0, (16, slots)).astype(BF16)
+        pick = jnp.where(jnp.concatenate([row] * (toks // 16), axis=0) == samples, one, zero)
+        pooled = dot(pick, rows_ref[:, t * cap : (t + 1) * cap, :].reshape(slots, emb))
+        cols = slice(t * emb, (t + 1) * emb)
+        feature_ref[:, cols] = (pooled * inv_ref[t]).astype(BF16)
+        for k in range(out_ref.shape[0]):
+            copy = pltpu.make_async_copy(
+                feature_ref.at[:, cols], out_ref.at[k, :, cols], sem_ref.at[t, k]
+            )
+            copy.start()
+            copies.append(copy)
+    for copy in copies:
+        copy.wait()
 
 
 def silu_slope(preact):
@@ -228,14 +292,18 @@
     slots = groups * cap
     t = pl.program_id(0)
     grads = grads_ref[...].reshape(slots, emb)
-    wanted = wanted_ref[0, 0:1, :]
+    at = down(wanted_ref[0, 0:8, :], 16)
+    low = down(wanted_ref[0, 8:16, :], 16)
+    low = jnp.concatenate([low] * (emb // 16), axis=0)
+    one, zero = jnp.ones((emb, slots), BF16), jnp.zeros((emb, slots), BF16)
+    hot = jnp.where(low == sublanes(emb, slots), one, zero)
     gone = expired_ref[pl.ds(t, 1), :]
     fresh_acc = jnp.where(gone == 1, ACC_RESET, acc_ref[pl.ds(t, 1), :])
     kept = jnp.where(gone == 1, 0.0, 1.0)
     diag = iota((emb, emb), 0) == iota((emb, emb), 1)
     for j in range(0, rows, emb):
-        names = (iota((emb, slots), 0) + j).astype(F32)
-        summed = dot(flag(wanted == names), grads)
+        here = jnp.concatenate([at == jnp.full_like(at, j // emb)] * (emb // 16), axis=0)
+        summed = dot(jnp.where(here, hot, zero), grads)
         cols = slice(j, j + emb)
         old = jnp.sum(jnp.where(diag, fresh_acc[:, cols], 0.0), axis=1, keepdims=True)
         keep = jnp.sum(jnp.where(diag, kept[:, cols], 0.0), axis=1, keepdims=True)
@@ -307,59 +375,77 @@
         compiler_params=params(24),
         name="slots",
     )(
-        bag_lengths,
-        owners[..., 0].swapaxes(1, 2),
-        row_slots.swapaxes(1, 2),
-        admit_mask.swapaxes(1, 2),
+        *map(
+            functools.partial(pltpu.with_memory_space_constraint, memory_space=pltpu.HBM),
+            (
+                bag_lengths,
+                owners[..., 0].swapaxes(1, 2),
+                row_slots.swapaxes(1, 2),
+                admit_mask.swapaxes(1, 2),
+            ),
+        )
     )
     arrived = a2a(request, DP)
     weight, _ = lax.optimization_barrier((hidden_weight, request))
     weights = [weight] + [ring(weight, "mp", k) for k in range(1, parts)]
     pick, sample_row = pl.pallas_call(
         samples_kernel,
-        out_shape=(shape((tabs, slots, toks), BF16), shape((tabs, 8, slots), F32)),
+        out_shape=(
+            pltpu.HBM((tabs, slots, toks), BF16),
+            shape((tabs, slots), F32),
+        ),
         compiler_params=params(24),
         cost_estimate=cost(4 << 30),
         name="samples",
     )(sample)
+    held = functools.partial(pltpu.with_memory_space_constraint, memory_space=pltpu.HBM)
+    sent = pl.pallas_call(
+        rows_kernel,
+        out_shape=pltpu.HBM((tabs, rows, emb), BF16),
+        compiler_params=params(8),
+        cost_estimate=cost(1 << 30),
+        name="rows",
+    )(expired, held(embeddings))
+    _, vmem, hbm = (
+        pl.BlockSpec(memory_space=space) for space in (pltpu.SMEM, pltpu.VMEM, pltpu.HBM)
+    )
+    dma = pltpu.SemaphoreType.DMA
     fetched = pl.pallas_call(
         fetch_kernel,
-        grid=(tabs,),
-        in_specs=[
-            block((groups, width)),
-            block((tabs, rows)),
-            block((1, rows, emb), lambda t: (t, 0, 0)),
+        in_specs=[vmem, hbm],
+        out_specs=hbm,
+        out_shape=pltpu.HBM((groups, width, emb), BF16),
+        scratch_shapes=[
+            pltpu.VMEM((tabs, rows, emb), BF16),
+            pltpu.VMEM((slots, 2 * width), BF16),
+            pltpu.VMEM((groups, width, emb), BF16),
+            dma,
+            dma((4,)),
         ],
-        out_specs=block((groups, cap, emb), lambda t: (0, t, 0)),
-        out_shape=pltpu.HBM((groups, width, emb), BF16),
         compiler_params=params(24),
         name="fetch",
-    )(arrived, expired, embeddings)
+    )(arrived, held(sent))
     returned = a2a(fetched, DP)
     unit, later = lax.optimization_barrier((output_weight, arrived))
     unit = unit.reshape(1, -1)
     units = [unit] + [ring(unit, "mp", k) for k in range(1, parts)]
     wanted = pl.pallas_call(
         wanted_kernel,
-        out_shape=shape((tabs, 8, slots), F32),
+        out_shape=pltpu.HBM((tabs, 16, slots), F32),
         compiler_params=params(24),
         cost_estimate=cost(4 << 30),
         name="wanted",
     )(later)
     features = pl.pallas_call(
         pool_kernel,
-        grid=(tabs,),
-        in_specs=[
-            block((groups, cap, emb), lambda t: (0, t, 0)),
-            block((1, 8, slots), lambda t: (t, 0, 0)),
-            block((1, toks, toks), lambda t: (t, 0, 0)),
-        ],
-        out_specs=block((toks, emb), lambda t: (0, t)),
-        out_shape=shape((toks, feats), BF16),
+        in_specs=[vmem, vmem, vmem],
+        out_specs=hbm,
+        out_shape=pltpu.HBM((parts, toks, feats), BF16),
+        scratch_shapes=[pltpu.VMEM((toks, feats), BF16), dma((tabs, parts))],
         compiler_params=params(24),
         name="pool",
     )(returned, sample_row, inv)
-    portion = from_everyone(features, "mp")
+    portion = a2a(features, "mp")
     label_column = pl.pallas_call(
         labels_kernel,
         out_shape=shape((toks, toks), F32),
@@ -416,7 +502,7 @@
         grid=(tabs,),
         in_specs=[
             block((groups, cap, emb), lambda t: (0, t, 0)),
-            block((1, 8, slots), lambda t: (t, 0, 0)),
+            block((1, 16, slots), lambda t: (t, 0, 0)),
             block((1, rows, emb), lambda t: (t, 0, 0)),
             block((tabs, rows)),
             block((tabs, rows)),
@@ -429,7 +515,7 @@
         compiler_params=params(24),
         cost_estimate=cost(4 << 30),
         name="update",
-    )(gradients, wanted, embeddings, expired, accumulator)
+    )(gradients, held(wanted), held(embeddings), expired, accumulator)
     return (new_rows, new_acc, weight_grad, logits[:, 0])
 
 

time: 244 us -> 240 us (0.984)
  blocking collectives: 98.2 us -> 68.5 us
  starting transfers between devices: 51.6 us -> 70.2 us
  waiting for transfers between devices: 56.1 us -> 64.6 us
  local copies, waits for them, and re-layouts: 10.2 us -> 3.81 us
  Pallas kernels: 24.4 us -> 29.4 us
    all_to_all x2 -> x1, blocking collectives: 98.2 us -> 68.5 us  [a2a(): return lax.all_to_all(value, axis, split_axis=0, concat_axis=0, tiled=True)]
    all_to_all x3 -> x4, starting transfers between devices: 19.1 us -> 37.6 us  [a2a(): return lax.all_to_all(value, axis, split_axis=0, concat_axis=0, tiled=True)]
    all_to_all x3 -> x4, waiting for transfers between devices: 54.6 us -> 63.3 us  [a2a(): return lax.all_to_all(value, axis, split_axis=0, concat_axis=0, tiled=True)]
    unnamed x32 -> x18, local copies, waits for them, and re-layouts: 7.72 us -> 2.18 us
    pallas_call x4 -> x5, Pallas kernels: 10.3 us -> 12.8 us  [the longest x1 4.34 us: shards(): pl.pallas_call(fetch_kernel, in_specs=[vmem, hbm], out_specs=hbm, out_sha...]
  transfers between devices with their start and end apart: 11 -> 12, of which waited for: 4 -> 5; matrix products, arithmetic and copies ran while one was open for 1% -> 0% of each run, Pallas kernels for 5% -> 8%
where the time goes in v3:
time: 240 us; the launch traced here: 239 us
  starting transfers between devices  70.2 us (29%)
  blocking collectives  68.5 us (29%)
  waiting for transfers between devices  64.6 us (27%)
  Pallas kernels  29.4 us (12%)
  local copies, waits for them, and re-layouts  3.81 us (2%)
    all_to_all x1, blocking collectives, a2a(): return lax.all_to_all(value, axis, split_axis=0, concat_axis=0, tiled=True)  68.5 us
    all_to_all x4, waiting for transfers between devices, a2a(): return lax.all_to_all(value, axis, split_axis=0, concat_axis=0, tiled=True)  63.3 us
    all_to_all x4, starting transfers between devices, a2a(): return lax.all_to_all(value, axis, split_axis=0, concat_axis=0, tiled=True)  37.6 us
    ppermute x8, starting transfers between devices, ring(): lax.ppermute(value, axis, [(i, (i + step) % size) for i in range(size)])  32.6 us
    pallas_call x1, Pallas kernels, shards(): pl.pallas_call(update_kernel, grid=(tabs,), in_specs=[block((groups, cap,...  8.17 us
  transfers between devices with their start and end apart: 12, of which 5 were waited for; matrix products, arithmetic and copies ran while one was open for 0% of the time, Pallas kernels for 8%

profile of v3, /device:TPU:1, one launch (start us, length us, event | category | flops | bytes accessed | tf_op | source)
XLA Modules:
  0.0 238.8 jit_solution(4694410536335323988)
XLA Ops:
  0.6 3.3 %slots.1 = (s32[128,64]{1,0:T(8,128)}, f32[128,64]{1,0:T(8,128)S(1)}, f32[4,128,128]{2,1,0:T(8,128)S(1)}) custom-call(s32[4,128]{1,0:T(4,128)} %len_ref.1, s32[4,8,128]{2,1,0:T(8,128)} %bitcast.35, s32[4,8,128]{2,1,0:T(8,128)} %bitcast.36, s32[4,8,128]{2,1,0:T(8,128)} %bitcast.37), custom_call_target="tpu_custom_call" | custom-call | tf_op jit(solution)/shard_map/slots/pallas_call | solution.py:368
  4.6 18.4 %all-to-all-start = ((s32[128,1,64]{2,1,0:T(1,128)}), s32[128,1,64]{2,1,0:T(1,128)S(1)}, u32[]{:S(2)}, u32[]{:S(2)}) async-start(s32[128,1,64]{2,1,0:T(1,128)} %bitcast.7), calls=%async_computation | async-start | bytes 131072 | tf_op jit(solution)/shard_map/all_to_all | solution.py:340
  23.7 2.4 rows.1.rows_ref
  26.0 8.4 %all-to-all-done = s32[128,1,64]{2,1,0:T(1,128)S(1)} async-done(((s32[128,1,64]{2,1,0:T(1,128)}), s32[128,1,64]{2,1,0:T(1,128)S(1)}, u32[]{:S(2)}, u32[]{:S(2)}) %all-to-all-start) | async-done | bytes 32800 | tf_op jit(solution)/shard_map/all_to_all | solution.py:340
  34.4 4.3 %fetch.1 = bf16[128,64,128]{2,1,0:T(8,128)(2,1)} custom-call(s32[128,64]{1,0:T(8,128)S(1)} %bitcast.22, bf16[4,512,128]{2,1,0:T(8,128)(2,1)} %rows.1.rows_ref), custom_call_target="tpu_custom_call" | custom-call | tf_op jit(solution)/shard_map/fetch/pallas_call | solution.py:413
  38.7 5.9 %all-to-all-start.1 = ((bf16[128,64,128]{2,1,0:T(8,128)(2,1)}), bf16[128,64,128]{2,1,0:T(8,128)(2,1)S(1)}, u32[]{:S(2)}, u32[]{:S(2)}) async-start(bf16[128,64,128]{2,1,0:T(8,128)(2,1)} %fetch.1), calls=%async_computation.1 | async-start | bytes 4194304 | tf_op jit(solution)/shard_map/all_to_all | solution.py:340
  44.7 3.1 %collective-permute-start = (bf16[2048,256]{1,0:T(8,128)(2,1)S(1)}, bf16[2048,256]{1,0:T(8,128)(2,1)}, u32[]{:S(2)}, u32[]{:S(2)}) collective-permute-start(bf16[2048,256]{1,0:T(8,128)(2,1)S(1)} %copy-done), channel_id=1, source_target_pairs={{0,1},{1,2},{2,3},{3,0},{4,5},{5,6},{6,7},{7,4},{8,9},{9,10},{10,1... | collective-permute-start | bytes 3145736 | tf_op jit(solution)/shard_map/ppermute | solution.py:350
  47.8 4.4 %collective-permute-start.1 = (bf16[2048,256]{1,0:T(8,128)(2,1)S(1)}, bf16[2048,256]{1,0:T(8,128)(2,1)}, u32[]{:S(2)}, u32[]{:S(2)}) collective-permute-start(bf16[2048,256]{1,0:T(8,128)(2,1)S(1)} %copy-done), channel_id=1, source_target_pairs={{0,2},{1,3},{2,0},{3,1},{4,6},{5,7},{6,4},{7,5},{8,10},{9,11},{10,... | collective-permute-start | bytes 3145736 | tf_op jit(solution)/shard_map/ppermute | solution.py:350
  52.2 3.1 %collective-permute-start.2 = (bf16[2048,256]{1,0:T(8,128)(2,1)S(1)}, bf16[2048,256]{1,0:T(8,128)(2,1)}, u32[]{:S(2)}, u32[]{:S(2)}) collective-permute-start(bf16[2048,256]{1,0:T(8,128)(2,1)S(1)} %copy-done), channel_id=1, source_target_pairs={{0,3},{1,0},{2,1},{3,2},{4,7},{5,4},{6,5},{7,6},{8,11},{9,8},{10,9... | collective-permute-start | bytes 3145736 | tf_op jit(solution)/shard_map/ppermute | solution.py:350
  56.1 2.5 %samples.1 = (bf16[4,2048,128]{2,1,0:T(8,128)(2,1)}, f32[4,2048]{1,0:T(4,128)S(1)}) custom-call(f32[128,64]{1,0:T(8,128)S(1)} %copy-done.4), custom_call_target="tpu_custom_call" | custom-call | flops 4294967296 | bytes 1048576 | tf_op jit(solution)/shard_map/samples/pallas_call | solution.py:391
  58.6 37.4 %all-to-all-done.1.rows_ref = bf16[128,64,128]{2,1,0:T(8,128)(2,1)S(1)} async-done(((bf16[128,64,128]{2,1,0:T(8,128)(2,1)}), bf16[128,64,128]{2,1,0:T(8,128)(2,1)S(1)}, u32[]{:S(2)}, u32[]{:S(2)}) %all-to-all-start.1) | async-done | bytes 2097184 | tf_op jit(solution)/shard_map/all_to_all | solution.py:340
  96.0 1.5 pool.1
  97.5 4.0 %all-to-all-start.2 = ((bf16[4,128,512]{2,1,0:T(8,128)(2,1)}), bf16[4,128,512]{2,1,0:T(8,128)(2,1)S(1)}, u32[]{:S(2)}, u32[]{:S(2)}) async-start(bf16[4,128,512]{2,1,0:T(8,128)(2,1)} %pool.1), calls=%async_computation.2 | async-start | bytes 1048576 | tf_op jit(solution)/shard_map/all_to_all | solution.py:340
  101.6 3.4 %collective-permute-start.3 = (f32[1,256]{1,0:T(1,128)S(1)}, f32[1,256]{1,0:T(1,128)S(1)}, u32[]{:S(2)}, u32[]{:S(2)}) collective-permute-start(f32[1,256]{1,0:T(1,128)S(1)} %bitcast.24), channel_id=1, source_target_pairs={{0,1},{1,2},{2,3},{3,0},{4,5},{5,6},{6,7},{7,4},{8,9},{9,10},{10,1... | collective-permute-start | bytes 3080 | tf_op jit(solution)/shard_map/ppermute | solution.py:350
  104.9 4.3 %collective-permute-start.4 = (f32[1,256]{1,0:T(1,128)S(1)}, f32[1,256]{1,0:T(1,128)S(1)}, u32[]{:S(2)}, u32[]{:S(2)}) collective-permute-start(f32[1,256]{1,0:T(1,128)S(1)} %bitcast.25), channel_id=1, source_target_pairs={{0,2},{1,3},{2,0},{3,1},{4,6},{5,7},{6,4},{7,5},{8,10},{9,11},{10,... | collective-permute-start | bytes 3080 | tf_op jit(solution)/shard_map/ppermute | solution.py:350
  109.3 3.3 %collective-permute-start.5 = (f32[1,256]{1,0:T(1,128)S(1)}, f32[1,256]{1,0:T(1,128)S(1)}, u32[]{:S(2)}, u32[]{:S(2)}) collective-permute-start(f32[1,256]{1,0:T(1,128)S(1)} %bitcast.26), channel_id=1, source_target_pairs={{0,3},{1,0},{2,1},{3,2},{4,7},{5,4},{6,5},{7,6},{8,11},{9,8},{10,9... | collective-permute-start | bytes 3080 | tf_op jit(solution)/shard_map/ppermute | solution.py:350
  113.9 3.7 %dense.1 = (f32[128,128]{1,0:T(8,128)S(1)}, f32[128,512]{1,0:T(8,128)S(1)}, bf16[2048,128]{1,0:T(8,128)(2,1)S(1)}, bf16[2048,128]{1,0:T(8,128)(2,1)S(1)}) custom-call(s32[2]{0:T(128)S(1)} %pad_add_fusion.at_ref, bf16[4,128,512]{2,1,0:T(8,128)(2,1)S(1)} %all-to-all-done.2.feat_ref, bf16[2048,256]{1,0:T(8,128)(2,1)S(1)} %copy-done, ...), custom_call_target="tpu_custom_call" | custom-call | tf_op jit(solution)/shard_map/dense/pallas_call | solution.py:457
  117.6 6.1 %collective-permute-start.6 = (bf16[2048,128]{1,0:T(8,128)(2,1)S(1)}, bf16[2048,128]{1,0:T(8,128)(2,1)S(1)}, u32[]{:S(2)}, u32[]{:S(2)}) collective-permute-start(bf16[2048,128]{1,0:T(8,128)(2,1)S(1)} %get-tuple-element.27), channel_id=1, source_target_pairs={{0,4},{4,0},{1,5},{5,1},{2,6},{6,2},{3,7},{7,3},{8,12},{12,8},{9,1... | collective-permute-start | bytes 1572872 | tf_op jit(solution)/shard_map/ppermute | solution.py:350
  125.4 68.5 %all_to_all.31.grads_ref = bf16[128,80,128]{2,1,0:T(8,128)(2,1)S(1)} all-to-all(bf16[128,80,128]{2,1,0:T(8,128)(2,1)S(1)} %constant_dynamic-update-slice_fusion), channel_id=1, replica_groups=mesh['dp_0'=8,'dp_1'=8,'dp_2'=2,'mp'=4] {'dp_0','dp_1','dp_2'}, dimensions={0} | all-to-all | bytes 5242880 | tf_op jit(solution)/shard_map/all_to_all | solution.py:340
  195.0 9.2 %all-to-all-start.4 = ((bf16[64,2,2,8,128]{4,3,2,1,0:T(8,128)(2,1)}), bf16[64,2,2,8,128]{4,3,2,1,0:T(8,128)(2,1)S(1)}, u32[]{:S(2)}, u32[]{:S(2)}) async-start(bf16[64,2,2,8,128]{4,3,2,1,0:T(8,128)(2,1)} %broadcast_in_dim.2), calls=%async_computation.4 | async-start | bytes 1048576 | tf_op jit(solution)/shard_map/all_to_all | solution.py:340
  204.2 17.5 %all-to-all-done.4 = bf16[64,2,2,8,128]{4,3,2,1,0:T(8,128)(2,1)S(1)} async-done(((bf16[64,2,2,8,128]{4,3,2,1,0:T(8,128)(2,1)}), bf16[64,2,2,8,128]{4,3,2,1,0:T(8,128)(2,1)S(1)}, u32[]{:S(2)}, u32[]{:S(2)}) %all-to-all-start.4) | async-done | bytes 524320 | tf_op jit(solution)/shard_map/all_to_all | solution.py:340
  221.7 5.1 %collective-permute-start.7 = (bf16[1024,256]{1,0:T(8,128)(2,1)S(1)}, bf16[1024,256]{1,0:T(8,128)(2,1)S(1)}, u32[]{:S(2)}, u32[]{:S(2)}) collective-permute-start(bf16[1024,256]{1,0:T(8,128)(2,1)S(1)} %bitcast.29), channel_id=1, source_target_pairs={{0,4},{4,0},{1,5},{5,1},{2,6},{6,2},{3,7},{7,3},{8,12},{12,8},{9,1... | collective-permute-start | bytes 1572872 | tf_op jit(solution)/shard_map/ppermute | solution.py:350
  226.8 2.1 wanted.1.wanted_ref
  229.5 8.2 %update.1 = (f32[4,512,128]{2,1,0:T(8,128)}, f32[4,512]{1,0:T(4,128)}) custom-call(bf16[128,80,128]{2,1,0:T(8,128)(2,1)S(1)} %all_to_all.31.grads_ref, f32[4,16,2048]{2,1,0:T(8,128)} %wanted.1.wanted_ref, f32[4,512,128]{2,1,0:T(8,128)} %emb_ref.3, s32[4,512]{1,0:T(4,128)S(1)} %copy-done.6, f32[4,512]{1,0:T(4,128)S(1)} %copy-done.7), custom_call_target="tpu_custom_call" | custom-call | flops 4294967296 | bytes 1048576 | tf_op jit(solution)/shard_map/update/pallas_call | solution.py:500
  (40 shorter events, 8.0 us)
Async XLA Ops:
  3.9 0.6 copy-start.3
  4.6 29.8 %all-to-all-start = ((s32[128,1,64]{2,1,0:T(1,128)}), s32[128,1,64]{2,1,0:T(1,128)S(1)}, u32[]{:S(2)}, u32[]{:S(2)}) async-start(s32[128,1,64]{2,1,0:T(1,128)} %bitcast.7), calls=%async_computation | async-start | bytes 131072 | tf_op jit(solution)/shard_map/all_to_all | solution.py:340
  23.0 0.7 copy-start.5
  38.7 5.9 %copy-start = (bf16[2048,256]{1,0:T(8,128)(2,1)S(1)}, bf16[2048,256]{1,0:T(8,128)(2,1)}, u32[]{:S(2)}) copy-start(bf16[2048,256]{1,0:T(8,128)(2,1)} %w0) | copy-start | bytes 3145732
  38.7 57.3 %all-to-all-start.1 = ((bf16[128,64,128]{2,1,0:T(8,128)(2,1)}), bf16[128,64,128]{2,1,0:T(8,128)(2,1)S(1)}, u32[]{:S(2)}, u32[]{:S(2)}) async-start(bf16[128,64,128]{2,1,0:T(8,128)(2,1)} %fetch.1), calls=%async_computation.1 | async-start | bytes 4194304 | tf_op jit(solution)/shard_map/all_to_all | solution.py:340
  44.7 69.2 %collective-permute-start = (bf16[2048,256]{1,0:T(8,128)(2,1)S(1)}, bf16[2048,256]{1,0:T(8,128)(2,1)}, u32[]{:S(2)}, u32[]{:S(2)}) collective-permute-start(bf16[2048,256]{1,0:T(8,128)(2,1)S(1)} %copy-done), channel_id=1, source_target_pairs={{0,1},{1,2},{2,3},{3,0},{4,5},{5,6},{6,7},{7,4},{8,9},{9,10},{10,1... | collective-permute-start | bytes 3145736 | tf_op jit(solution)/shard_map/ppermute | solution.py:350
  47.8 66.1 %collective-permute-start.1 = (bf16[2048,256]{1,0:T(8,128)(2,1)S(1)}, bf16[2048,256]{1,0:T(8,128)(2,1)}, u32[]{:S(2)}, u32[]{:S(2)}) collective-permute-start(bf16[2048,256]{1,0:T(8,128)(2,1)S(1)} %copy-done), channel_id=1, source_target_pairs={{0,2},{1,3},{2,0},{3,1},{4,6},{5,7},{6,4},{7,5},{8,10},{9,11},{10,... | collective-permute-start | bytes 3145736 | tf_op jit(solution)/shard_map/ppermute | solution.py:350
  52.2 61.7 %collective-permute-start.2 = (bf16[2048,256]{1,0:T(8,128)(2,1)S(1)}, bf16[2048,256]{1,0:T(8,128)(2,1)}, u32[]{:S(2)}, u32[]{:S(2)}) collective-permute-start(bf16[2048,256]{1,0:T(8,128)(2,1)S(1)} %copy-done), channel_id=1, source_target_pairs={{0,3},{1,0},{2,1},{3,2},{4,7},{5,4},{6,5},{7,6},{8,11},{9,8},{10,9... | collective-permute-start | bytes 3145736 | tf_op jit(solution)/shard_map/ppermute | solution.py:350
  55.2 0.8 copy-start.4
  58.6 43.0 %copy-start.1 = (f32[256]{0:T(256)S(1)}, f32[256]{0:T(256)}, u32[]{:S(2)}) copy-start(f32[256]{0:T(256)} %param.18) | copy-start | bytes 3076
  58.6 54.0 %copy-start.2 = (s32[128]{0:T(128)S(1)}, s32[128]{0:T(128)}, u32[]{:S(2)}) copy-start(s32[128]{0:T(128)} %param.19) | copy-start | bytes 1540
  97.5 16.4 %all-to-all-start.2 = ((bf16[4,128,512]{2,1,0:T(8,128)(2,1)}), bf16[4,128,512]{2,1,0:T(8,128)(2,1)S(1)}, u32[]{:S(2)}, u32[]{:S(2)}) async-start(bf16[4,128,512]{2,1,0:T(8,128)(2,1)} %pool.1), calls=%async_computation.2 | async-start | bytes 1048576 | tf_op jit(solution)/shard_map/all_to_all | solution.py:340
  101.6 7.7 %collective-permute-start.3 = (f32[1,256]{1,0:T(1,128)S(1)}, f32[1,256]{1,0:T(1,128)S(1)}, u32[]{:S(2)}, u32[]{:S(2)}) collective-permute-start(f32[1,256]{1,0:T(1,128)S(1)} %bitcast.24), channel_id=1, source_target_pairs={{0,1},{1,2},{2,3},{3,0},{4,5},{5,6},{6,7},{7,4},{8,9},{9,10},{10,1... | collective-permute-start | bytes 3080 | tf_op jit(solution)/shard_map/ppermute | solution.py:350
  104.9 7.8 %collective-permute-start.4 = (f32[1,256]{1,0:T(1,128)S(1)}, f32[1,256]{1,0:T(1,128)S(1)}, u32[]{:S(2)}, u32[]{:S(2)}) collective-permute-start(f32[1,256]{1,0:T(1,128)S(1)} %bitcast.25), channel_id=1, source_target_pairs={{0,2},{1,3},{2,0},{3,1},{4,6},{5,7},{6,4},{7,5},{8,10},{9,11},{10,... | collective-permute-start | bytes 3080 | tf_op jit(solution)/shard_map/ppermute | solution.py:350
  109.3 4.6 %collective-permute-start.5 = (f32[1,256]{1,0:T(1,128)S(1)}, f32[1,256]{1,0:T(1,128)S(1)}, u32[]{:S(2)}, u32[]{:S(2)}) collective-permute-start(f32[1,256]{1,0:T(1,128)S(1)} %bitcast.26), channel_id=1, source_target_pairs={{0,3},{1,0},{2,1},{3,2},{4,7},{5,4},{6,5},{7,6},{8,11},{9,8},{10,9... | collective-permute-start | bytes 3080 | tf_op jit(solution)/shard_map/ppermute | solution.py:350
  113.9 9.8 %copy-start.8 = (bf16[4,2048,128]{2,1,0:T(8,128)(2,1)S(1)}, bf16[4,2048,128]{2,1,0:T(8,128)(2,1)}, u32[]{:S(2)}) copy-start(bf16[4,2048,128]{2,1,0:T(8,128)(2,1)} %get-tuple-element.25.pick_ref) | copy-start | bytes 6291460
  117.6 7.6 %collective-permute-start.6 = (bf16[2048,128]{1,0:T(8,128)(2,1)S(1)}, bf16[2048,128]{1,0:T(8,128)(2,1)S(1)}, u32[]{:S(2)}, u32[]{:S(2)}) collective-permute-start(bf16[2048,128]{1,0:T(8,128)(2,1)S(1)} %get-tuple-element.27), channel_id=1, source_target_pairs={{0,4},{4,0},{1,5},{5,1},{2,6},{6,2},{3,7},{7,3},{8,12},{12,8},{9,1... | collective-permute-start | bytes 1572872 | tf_op jit(solution)/shard_map/ppermute | solution.py:350
  195.0 26.8 %all-to-all-start.4 = ((bf16[64,2,2,8,128]{4,3,2,1,0:T(8,128)(2,1)}), bf16[64,2,2,8,128]{4,3,2,1,0:T(8,128)(2,1)S(1)}, u32[]{:S(2)}, u32[]{:S(2)}) async-start(bf16[64,2,2,8,128]{4,3,2,1,0:T(8,128)(2,1)} %broadcast_in_dim.2), calls=%async_computation.4 | async-start | bytes 1048576 | tf_op jit(solution)/shard_map/all_to_all | solution.py:340
  221.7 7.8 %copy-start.6 = (s32[4,512]{1,0:T(4,128)S(1)}, s32[4,512]{1,0:T(4,128)}, u32[]{:S(2)}) copy-start(s32[4,512]{1,0:T(4,128)} %expired_ref.3) | copy-start | bytes 24580
  221.7 7.8 %copy-start.7 = (f32[4,512]{1,0:T(4,128)S(1)}, f32[4,512]{1,0:T(4,128)}, u32[]{:S(2)}) copy-start(f32[4,512]{1,0:T(4,128)} %acc_ref.1) | copy-start | bytes 24580
  221.7 16.0 %collective-permute-start.7 = (bf16[1024,256]{1,0:T(8,128)(2,1)S(1)}, bf16[1024,256]{1,0:T(8,128)(2,1)S(1)}, u32[]{:S(2)}, u32[]{:S(2)}) collective-permute-start(bf16[1024,256]{1,0:T(8,128)(2,1)S(1)} %bitcast.29), channel_id=1, source_target_pairs={{0,4},{4,0},{1,5},{5,1},{2,6},{6,2},{3,7},{7,3},{8,12},{12,8},{9,1... | collective-permute-start | bytes 1572872 | tf_op jit(solution)/shard_map/ppermute | solution.py:350

commit v4 on v3

--- a/solution.py
+++ b/solution.py
@@ -122,18 +122,6 @@
     out_ref[...] = jnp.broadcast_to(column, dims)
 
 
-def rows_kernel(expired_ref, emb_ref, out_ref):
-    tabs, rows, emb = emb_ref.shape
-    diag = iota((emb, emb), 0) == iota((emb, emb), 1)
-    for t in range(tabs):
-        for j in range(0, rows, emb):
-            gone = expired_ref[t : t + 1, j : j + emb].astype(F32)
-            column = jnp.sum(jnp.where(diag, gone, 0.0), axis=1, keepdims=True)
-            out_ref[t, j : j + emb, :] = jnp.where(
-                column > 0.5, 0.0, emb_ref[t, j : j + emb, :]
-            ).astype(BF16)
-
-
 def halves_of(arrived, block_rows):
     shift = block_rows.bit_length() - 1
     return jnp.concatenate(
@@ -141,42 +129,56 @@
     )
 
 
-def fetch_kernel(arrived_ref, rows_ref, out_ref, table_ref, own_ref, sent_ref, in_sem, out_sem):
+def fetch_kernel(
+    arrived_ref, expired_ref, emb_ref, out_ref,
+    gone_ref, held_ref, table_ref, sent_ref, in_sem, out_sem,
+):
     groups, width = arrived_ref.shape
-    tabs, rows, emb = rows_ref.shape
+    tabs, rows, emb = emb_ref.shape
     cap = width // tabs
-    slots = groups * cap
     half = rows // 2
-    load = pltpu.make_async_copy(rows_ref, table_ref, in_sem)
-    load.start()
-    own_ref[...] = own_lines(halves_of(arrived_ref[...], half), slots)
+    loads = [pltpu.make_async_copy(expired_ref, gone_ref, in_sem.at[tabs])] + [
+        pltpu.make_async_copy(emb_ref.at[t], held_ref.at[t], in_sem.at[t]) for t in range(tabs)
+    ]
+    for load in loads:
+        load.start()
+    halves = halves_of(arrived_ref[...], half)
     lane = iota((16, emb), 1).astype(F32)
+    diag = iota((emb, emb), 0) == iota((emb, emb), 1)
     parts = out_sem.shape[0]
-    part = slots // parts
-    low = jnp.concatenate([lane.astype(BF16)] * (part // 16), axis=0)
-    high = jnp.concatenate([(lane + emb).astype(BF16)] * (part // 16), axis=0)
-    one, zero = jnp.ones((part, emb), BF16), jnp.zeros((part, emb), BF16)
+    part = groups // parts
+    low = jnp.concatenate([lane.astype(BF16)] * (part * cap // 16), axis=0)
+    high = jnp.concatenate([(lane + emb).astype(BF16)] * (part * cap // 16), axis=0)
+    one, zero = jnp.ones((part * cap, emb), BF16), jnp.zeros((part * cap, emb), BF16)
     lanes = (2 * width, emb)
+    which = [
+        jnp.concatenate([of_table(lanes, 0, t, kind, width, cap) for kind in (1, 0)], axis=1)
+        for t in range(tabs)
+    ]
     stores = []
     for c in range(parts):
-        own = own_ref[c * part : (c + 1) * part, :]
-        mine = slice(c * part // cap, (c + 1) * part // cap)
+        mine = slice(c * part, (c + 1) * part)
+        own = own_lines(halves[mine], part * cap)
         for t in range(tabs):
-            which = jnp.concatenate(
-                [of_table(lanes, 0, t, 1, width, cap), of_table(lanes, 0, t, 0, width, cap)],
-                axis=1,
-            )
-            found = dot(own, which)
+            if c == 0:
+                if t == 0:
+                    loads[0].wait()
+                loads[t + 1].wait()
+                for j in range(0, rows, emb):
+                    gone = gone_ref[t : t + 1, j : j + emb].astype(F32)
+                    column = jnp.sum(jnp.where(diag, gone, 0.0), axis=1, keepdims=True)
+                    side = j // half * emb
+                    table_ref[t, j % half : j % half + emb, side : side + emb] = jnp.where(
+                        column > 0.5, 0.0, held_ref[t, j : j + emb, :]
+                    ).astype(BF16)
+            found = dot(own, which[t])
             at = found[:, :emb].astype(BF16)
             pick = jnp.concatenate(
                 [jnp.where(at == low, one, zero), jnp.where(at == high, one, zero)], axis=1
             )
-            if c == 0 and t == 0:
-                load.wait()
-            table = jnp.concatenate([table_ref[t, :half], table_ref[t, half:]], axis=1)
-            both = dot(pick, table).astype(BF16)
+            both = dot(pick, table_ref[t]).astype(BF16)
             line = jnp.where(found[:, emb:].astype(BF16) == zero, both[:, :emb], both[:, emb:])
-            sent_ref[mine, t * cap : (t + 1) * cap, :] = line.reshape(part // cap, cap, emb)
+            sent_ref[mine, t * cap : (t + 1) * cap, :] = line.reshape(part, cap, emb)
         store = pltpu.make_async_copy(sent_ref.at[mine], out_ref.at[mine], out_sem.at[c])
         store.start()
         stores.append(store)
@@ -318,6 +320,18 @@
                 new_acc_ref[table : table + 1, cols] = line
 
 
+def near_kernel(at_ref, piece_ref, out_ref, sem):
+    copy = pltpu.make_async_copy(piece_ref, out_ref.at[at_ref[1]], sem)
+    copy.start()
+    copy.wait()
+
+
+def far_kernel(at_ref, piece_ref, begun_ref, out_ref, sem):
+    copy = pltpu.make_async_copy(piece_ref, out_ref.at[1 - at_ref[1]], sem)
+    copy.start()
+    copy.wait()
+
+
 def shape(dims, dtype):
     return jax.ShapeDtypeStruct(dims, dtype)
 
@@ -399,32 +413,26 @@
         name="samples",
     )(sample)
     held = functools.partial(pltpu.with_memory_space_constraint, memory_space=pltpu.HBM)
-    sent = pl.pallas_call(
-        rows_kernel,
-        out_shape=pltpu.HBM((tabs, rows, emb), BF16),
-        compiler_params=params(8),
-        cost_estimate=cost(1 << 30),
-        name="rows",
-    )(expired, held(embeddings))
-    _, vmem, hbm = (
+    smem, vmem, hbm = (
         pl.BlockSpec(memory_space=space) for space in (pltpu.SMEM, pltpu.VMEM, pltpu.HBM)
     )
     dma = pltpu.SemaphoreType.DMA
     fetched = pl.pallas_call(
         fetch_kernel,
-        in_specs=[vmem, hbm],
+        in_specs=[vmem, hbm, hbm],
         out_specs=hbm,
         out_shape=pltpu.HBM((groups, width, emb), BF16),
         scratch_shapes=[
-            pltpu.VMEM((tabs, rows, emb), BF16),
-            pltpu.VMEM((slots, 2 * width), BF16),
+            pltpu.VMEM((tabs, rows), I32),
+            pltpu.VMEM((tabs, rows, emb), F32),
+            pltpu.VMEM((tabs, rows // 2, 2 * emb), BF16),
             pltpu.VMEM((groups, width, emb), BF16),
-            dma,
+            dma((tabs + 1,)),
             dma((4,)),
         ],
         compiler_params=params(24),
         name="fetch",
-    )(arrived, held(sent))
+    )(arrived, held(expired), held(embeddings))
     returned = a2a(fetched, DP)
     unit, later = lax.optimization_barrier((output_weight, arrived))
     unit = unit.reshape(1, -1)
@@ -494,9 +502,20 @@
     near = from_everyone(own, FAR)
     near = near.transpose(0, 1, 3, 2, 4).reshape(lines // 2, units_dev)
     far = ring(near, NEAR, 1)
-    weight_grad = jnp.concatenate(
-        [jnp.where(core == 0, near, far), jnp.where(core == 0, far, near)]
-    )
+    weight_grad = None
+    for kernel, piece in ((near_kernel, near), (far_kernel, far)):
+        begun = [] if weight_grad is None else [weight_grad]
+        weight_grad = pl.pallas_call(
+            kernel,
+            in_specs=[smem, vmem] + [hbm] * len(begun),
+            out_specs=hbm,
+            out_shape=pltpu.HBM((2, lines // 2, units_dev), BF16),
+            input_output_aliases={2: 0} if begun else {},
+            scratch_shapes=[dma],
+            compiler_params=params(4),
+            name="near" if weight_grad is None else "far",
+        )(place, piece, *begun)
+    weight_grad = weight_grad.reshape(lines, units_dev)
     new_rows, new_acc = pl.pallas_call(
         update_kernel,
         grid=(tabs,),

time: 240 us -> 240 us (level)
  blocking collectives: 68.5 us -> 125 us
  starting transfers between devices: 70.2 us -> 42.6 us
  waiting for transfers between devices: 64.6 us -> 38.7 us
    all_to_all x1 -> x3, blocking collectives: 68.5 us -> 125 us  [a2a(): return lax.all_to_all(value, axis, split_axis=0, concat_axis=0, tiled=True)]
    all_to_all x4 -> x2, starting transfers between devices: 37.6 us -> 9.94 us  [a2a(): return lax.all_to_all(value, axis, split_axis=0, concat_axis=0, tiled=True)]
    all_to_all x4 -> x2, waiting for transfers between devices: 63.3 us -> 37.4 us  [a2a(): return lax.all_to_all(value, axis, split_axis=0, concat_axis=0, tiled=True)]
    pallas_call x2 -> x3, Pallas kernels: 6.7 us -> 7.92 us  [the longest x1 5.23 us: shards(): pl.pallas_call(fetch_kernel, in_specs=[vmem, hbm, hbm], out_specs=hbm, ou...]
  transfers between devices with their start and end apart: 12 -> 10, of which waited for: 5 -> 3; matrix products, arithmetic and copies ran while one was open for 0% -> 0% of each run, Pallas kernels for 8% -> 7%
where the time goes in v4:
time: 240 us; the launch traced here: 239 us
  blocking collectives  125 us (52%)
  starting transfers between devices  42.6 us (18%)
  waiting for transfers between devices  38.7 us (16%)
  Pallas kernels  30 us (12%)
    all_to_all x3, blocking collectives, a2a(): return lax.all_to_all(value, axis, split_axis=0, concat_axis=0, tiled=True)  125 us
    all_to_all x2, waiting for transfers between devices, a2a(): return lax.all_to_all(value, axis, split_axis=0, concat_axis=0, tiled=True)  37.4 us
    ppermute x8, starting transfers between devices, ring(): lax.ppermute(value, axis, [(i, (i + step) % size) for i in range(size)])  32.6 us
    all_to_all x2, starting transfers between devices, a2a(): return lax.all_to_all(value, axis, split_axis=0, concat_axis=0, tiled=True)  9.94 us
    pallas_call x1, Pallas kernels, shards(): pl.pallas_call(update_kernel, grid=(tabs,), in_specs=[block((groups, cap,...  8.17 us
    pallas_call x1, Pallas kernels, shards(): pl.pallas_call(fetch_kernel, in_specs=[vmem, hbm, hbm], out_specs=hbm, ou...  5.23 us
  transfers between devices with their start and end apart: 10, of which 3 were waited for; matrix products, arithmetic and copies ran while one was open for 0% of the time, Pallas kernels for 7%

profile of v4, /device:TPU:1, one launch (start us, length us, event | category | flops | bytes accessed | tf_op | source)
XLA Modules:
  0.0 239.1 jit_solution(9842148262575225426)
XLA Ops:
  0.6 2.7 %slots.1 = (s32[128,64]{1,0:T(8,128)S(1)}, f32[128,64]{1,0:T(8,128)S(1)}, f32[4,128,128]{2,1,0:T(8,128)S(1)}) custom-call(s32[4,128]{1,0:T(4,128)} %len_ref.1, s32[4,8,128]{2,1,0:T(8,128)} %bitcast.38, s32[4,8,128]{2,1,0:T(8,128)} %bitcast.39, s32[4,8,128]{2,1,0:T(8,128)} %bitcast.40), custom_call_target="tpu_custom_call" | custom-call | tf_op jit(solution)/shard_map/slots/pallas_call | solution.py:382
  3.3 29.7 %all_to_all.31 = s32[128,1,64]{2,1,0:T(1,128)S(1)} all-to-all(s32[128,1,64]{2,1,0:T(1,128)S(1)} %bitcast.27), channel_id=1, replica_groups=mesh['dp_0'=8,'dp_1'=8,'dp_2'=2,'mp'=4] {'dp_0','dp_1','dp_2'}, dimensions={0} | all-to-all | bytes 65536 | tf_op jit(solution)/shard_map/all_to_all | solution.py:354
  33.0 5.2 %fetch.1 = bf16[128,64,128]{2,1,0:T(8,128)(2,1)} custom-call(s32[128,64]{1,0:T(8,128)S(1)} %bitcast.25, s32[4,512]{1,0:T(4,128)} %expired_ref.3, f32[4,512,128]{2,1,0:T(8,128)} %emb_ref.3), custom_call_target="tpu_custom_call" | custom-call | tf_op jit(solution)/shard_map/fetch/pallas_call | solution.py:420
  38.3 5.9 %all-to-all-start.1 = ((bf16[128,64,128]{2,1,0:T(8,128)(2,1)}), bf16[128,64,128]{2,1,0:T(8,128)(2,1)S(1)}, u32[]{:S(2)}, u32[]{:S(2)}) async-start(bf16[128,64,128]{2,1,0:T(8,128)(2,1)} %fetch.1), calls=%async_computation.1 | async-start | bytes 4194304 | tf_op jit(solution)/shard_map/all_to_all | solution.py:354
  44.2 3.1 %collective-permute-start = (bf16[2048,256]{1,0:T(8,128)(2,1)S(1)}, bf16[2048,256]{1,0:T(8,128)(2,1)}, u32[]{:S(2)}, u32[]{:S(2)}) collective-permute-start(bf16[2048,256]{1,0:T(8,128)(2,1)S(1)} %copy-done), channel_id=1, source_target_pairs={{0,1},{1,2},{2,3},{3,0},{4,5},{5,6},{6,7},{7,4},{8,9},{9,10},{10,1... | collective-permute-start | bytes 3145736 | tf_op jit(solution)/shard_map/ppermute | solution.py:364
  47.3 4.4 %collective-permute-start.1 = (bf16[2048,256]{1,0:T(8,128)(2,1)S(1)}, bf16[2048,256]{1,0:T(8,128)(2,1)}, u32[]{:S(2)}, u32[]{:S(2)}) collective-permute-start(bf16[2048,256]{1,0:T(8,128)(2,1)S(1)} %copy-done), channel_id=1, source_target_pairs={{0,2},{1,3},{2,0},{3,1},{4,6},{5,7},{6,4},{7,5},{8,10},{9,11},{10,... | collective-permute-start | bytes 3145736 | tf_op jit(solution)/shard_map/ppermute | solution.py:364
  51.7 3.1 %collective-permute-start.2 = (bf16[2048,256]{1,0:T(8,128)(2,1)S(1)}, bf16[2048,256]{1,0:T(8,128)(2,1)}, u32[]{:S(2)}, u32[]{:S(2)}) collective-permute-start(bf16[2048,256]{1,0:T(8,128)(2,1)S(1)} %copy-done), channel_id=1, source_target_pairs={{0,3},{1,0},{2,1},{3,2},{4,7},{5,4},{6,5},{7,6},{8,11},{9,8},{10,9... | collective-permute-start | bytes 3145736 | tf_op jit(solution)/shard_map/ppermute | solution.py:364
  55.6 2.5 %samples.1 = (bf16[4,2048,128]{2,1,0:T(8,128)(2,1)}, f32[4,2048]{1,0:T(4,128)S(1)}) custom-call(f32[128,64]{1,0:T(8,128)S(1)} %copy-done.5), custom_call_target="tpu_custom_call" | custom-call | flops 4294967296 | bytes 1048576 | tf_op jit(solution)/shard_map/samples/pallas_call | solution.py:405
  58.1 37.4 %all-to-all-done.1.rows_ref = bf16[128,64,128]{2,1,0:T(8,128)(2,1)S(1)} async-done(((bf16[128,64,128]{2,1,0:T(8,128)(2,1)}), bf16[128,64,128]{2,1,0:T(8,128)(2,1)S(1)}, u32[]{:S(2)}, u32[]{:S(2)}) %all-to-all-start.1) | async-done | bytes 2097184 | tf_op jit(solution)/shard_map/all_to_all | solution.py:354
  95.6 1.5 pool.1
  97.1 4.0 %all-to-all-start.2 = ((bf16[4,128,512]{2,1,0:T(8,128)(2,1)}), bf16[4,128,512]{2,1,0:T(8,128)(2,1)S(1)}, u32[]{:S(2)}, u32[]{:S(2)}) async-start(bf16[4,128,512]{2,1,0:T(8,128)(2,1)} %pool.1), calls=%async_computation.2 | async-start | bytes 1048576 | tf_op jit(solution)/shard_map/all_to_all | solution.py:354
  101.1 3.4 %collective-permute-start.3 = (f32[1,256]{1,0:T(1,128)S(1)}, f32[1,256]{1,0:T(1,128)S(1)}, u32[]{:S(2)}, u32[]{:S(2)}) collective-permute-start(f32[1,256]{1,0:T(1,128)S(1)} %bitcast.28), channel_id=1, source_target_pairs={{0,1},{1,2},{2,3},{3,0},{4,5},{5,6},{6,7},{7,4},{8,9},{9,10},{10,1... | collective-permute-start | bytes 3080 | tf_op jit(solution)/shard_map/ppermute | solution.py:364
  104.5 4.3 %collective-permute-start.4 = (f32[1,256]{1,0:T(1,128)S(1)}, f32[1,256]{1,0:T(1,128)S(1)}, u32[]{:S(2)}, u32[]{:S(2)}) collective-permute-start(f32[1,256]{1,0:T(1,128)S(1)} %bitcast.29), channel_id=1, source_target_pairs={{0,2},{1,3},{2,0},{3,1},{4,6},{5,7},{6,4},{7,5},{8,10},{9,11},{10,... | collective-permute-start | bytes 3080 | tf_op jit(solution)/shard_map/ppermute | solution.py:364
  108.8 3.3 %collective-permute-start.5 = (f32[1,256]{1,0:T(1,128)S(1)}, f32[1,256]{1,0:T(1,128)S(1)}, u32[]{:S(2)}, u32[]{:S(2)}) collective-permute-start(f32[1,256]{1,0:T(1,128)S(1)} %bitcast.30), channel_id=1, source_target_pairs={{0,3},{1,0},{2,1},{3,2},{4,7},{5,4},{6,5},{7,6},{8,11},{9,8},{10,9... | collective-permute-start | bytes 3080 | tf_op jit(solution)/shard_map/ppermute | solution.py:364
  113.4 3.7 %dense.1 = (f32[128,128]{1,0:T(8,128)S(1)}, f32[128,512]{1,0:T(8,128)S(1)}, bf16[2048,128]{1,0:T(8,128)(2,1)S(1)}, bf16[2048,128]{1,0:T(8,128)(2,1)S(1)}) custom-call(s32[2]{0:T(128)S(1)} %pad_add_fusion.at_ref, bf16[4,128,512]{2,1,0:T(8,128)(2,1)S(1)} %all-to-all-done.2.feat_ref, bf16[2048,256]{1,0:T(8,128)(2,1)S(1)} %copy-done, ...), custom_call_target="tpu_custom_call" | custom-call | tf_op jit(solution)/shard_map/dense/pallas_call | solution.py:465
  117.1 6.1 %collective-permute-start.6 = (bf16[2048,128]{1,0:T(8,128)(2,1)S(1)}, bf16[2048,128]{1,0:T(8,128)(2,1)S(1)}, u32[]{:S(2)}, u32[]{:S(2)}) collective-permute-start(bf16[2048,128]{1,0:T(8,128)(2,1)S(1)} %get-tuple-element.27), channel_id=1, source_target_pairs={{0,4},{4,0},{1,5},{5,1},{2,6},{6,2},{3,7},{7,3},{8,12},{12,8},{9,1... | collective-permute-start | bytes 1572872 | tf_op jit(solution)/shard_map/ppermute | solution.py:364
  123.2 1.4 spread.1
  125.0 68.5 %all_to_all.32.grads_ref = bf16[128,80,128]{2,1,0:T(8,128)(2,1)S(1)} all-to-all(bf16[128,80,128]{2,1,0:T(8,128)(2,1)S(1)} %constant_dynamic-update-slice_fusion), channel_id=1, replica_groups=mesh['dp_0'=8,'dp_1'=8,'dp_2'=2,'mp'=4] {'dp_0','dp_1','dp_2'}, dimensions={0} | all-to-all | bytes 5242880 | tf_op jit(solution)/shard_map/all_to_all | solution.py:354
  193.7 26.6 %all_to_all.33 = bf16[64,2,2,8,128]{4,3,2,1,0:T(8,128)(2,1)S(1)} all-to-all(bf16[64,2,2,8,128]{4,3,2,1,0:T(8,128)(2,1)S(1)} %broadcast_in_dim.2), channel_id=1, replica_groups=mesh['dp_0'=8,'dp_1'=8,'dp_2'=2,'mp'=4] {'dp_0','dp_1'}, dimensions={0} | all-to-all | bytes 1048576 | tf_op jit(solution)/shard_map/all_to_all | solution.py:354
  220.3 5.1 %collective-permute-start.7 = (bf16[1024,256]{1,0:T(8,128)(2,1)S(1)}, bf16[1024,256]{1,0:T(8,128)(2,1)S(1)}, u32[]{:S(2)}, u32[]{:S(2)}) collective-permute-start(bf16[1024,256]{1,0:T(8,128)(2,1)S(1)} %bitcast.23), channel_id=1, source_target_pairs={{0,4},{4,0},{1,5},{5,1},{2,6},{6,2},{3,7},{7,3},{8,12},{12,8},{9,1... | collective-permute-start | bytes 1572872 | tf_op jit(solution)/shard_map/ppermute | solution.py:364
  225.4 2.1 wanted.1.wanted_ref
  228.1 8.2 %update.1 = (f32[4,512,128]{2,1,0:T(8,128)}, f32[4,512]{1,0:T(4,128)}) custom-call(bf16[128,80,128]{2,1,0:T(8,128)(2,1)S(1)} %all_to_all.32.grads_ref, f32[4,16,2048]{2,1,0:T(8,128)} %wanted.1.wanted_ref, f32[4,512,128]{2,1,0:T(8,128)} %emb_ref.3, s32[4,512]{1,0:T(4,128)S(1)} %copy-done.1, f32[4,512]{1,0:T(4,128)S(1)} %copy-done.6), custom_call_target="tpu_custom_call" | custom-call | flops 4294967296 | bytes 1048576 | tf_op jit(solution)/shard_map/update/pallas_call | solution.py:519
  236.2 1.3 near.1.begun_ref
  237.6 1.3 far.1
  (35 shorter events, 3.4 us)
Async XLA Ops:
  3.3 29.7 %copy-start.4 = (f32[128,64]{1,0:T(8,128)}, f32[128,64]{1,0:T(8,128)S(1)}, u32[]{:S(2)}) copy-start(f32[128,64]{1,0:T(8,128)S(1)} %get-tuple-element.19.sample_ref) | copy-start | bytes 98308
  38.3 5.9 %copy-start = (bf16[2048,256]{1,0:T(8,128)(2,1)S(1)}, bf16[2048,256]{1,0:T(8,128)(2,1)}, u32[]{:S(2)}) copy-start(bf16[2048,256]{1,0:T(8,128)(2,1)} %w0) | copy-start | bytes 3145732
  38.3 57.3 %all-to-all-start.1 = ((bf16[128,64,128]{2,1,0:T(8,128)(2,1)}), bf16[128,64,128]{2,1,0:T(8,128)(2,1)S(1)}, u32[]{:S(2)}, u32[]{:S(2)}) async-start(bf16[128,64,128]{2,1,0:T(8,128)(2,1)} %fetch.1), calls=%async_computation.1 | async-start | bytes 4194304 | tf_op jit(solution)/shard_map/all_to_all | solution.py:354
  44.2 69.2 %collective-permute-start = (bf16[2048,256]{1,0:T(8,128)(2,1)S(1)}, bf16[2048,256]{1,0:T(8,128)(2,1)}, u32[]{:S(2)}, u32[]{:S(2)}) collective-permute-start(bf16[2048,256]{1,0:T(8,128)(2,1)S(1)} %copy-done), channel_id=1, source_target_pairs={{0,1},{1,2},{2,3},{3,0},{4,5},{5,6},{6,7},{7,4},{8,9},{9,10},{10,1... | collective-permute-start | bytes 3145736 | tf_op jit(solution)/shard_map/ppermute | solution.py:364
  47.3 66.1 %collective-permute-start.1 = (bf16[2048,256]{1,0:T(8,128)(2,1)S(1)}, bf16[2048,256]{1,0:T(8,128)(2,1)}, u32[]{:S(2)}, u32[]{:S(2)}) collective-permute-start(bf16[2048,256]{1,0:T(8,128)(2,1)S(1)} %copy-done), channel_id=1, source_target_pairs={{0,2},{1,3},{2,0},{3,1},{4,6},{5,7},{6,4},{7,5},{8,10},{9,11},{10,... | collective-permute-start | bytes 3145736 | tf_op jit(solution)/shard_map/ppermute | solution.py:364
  51.7 61.7 %collective-permute-start.2 = (bf16[2048,256]{1,0:T(8,128)(2,1)S(1)}, bf16[2048,256]{1,0:T(8,128)(2,1)}, u32[]{:S(2)}, u32[]{:S(2)}) collective-permute-start(bf16[2048,256]{1,0:T(8,128)(2,1)S(1)} %copy-done), channel_id=1, source_target_pairs={{0,3},{1,0},{2,1},{3,2},{4,7},{5,4},{6,5},{7,6},{8,11},{9,8},{10,9... | collective-permute-start | bytes 3145736 | tf_op jit(solution)/shard_map/ppermute | solution.py:364
  54.8 0.8 copy-start.5
  58.1 42.9 %copy-start.2 = (f32[256]{0:T(256)S(1)}, f32[256]{0:T(256)}, u32[]{:S(2)}) copy-start(f32[256]{0:T(256)} %param.18) | copy-start | bytes 3076
  58.1 54.0 %copy-start.3 = (s32[128]{0:T(128)S(1)}, s32[128]{0:T(128)}, u32[]{:S(2)}) copy-start(s32[128]{0:T(128)} %param.19) | copy-start | bytes 1540
  97.1 16.4 %all-to-all-start.2 = ((bf16[4,128,512]{2,1,0:T(8,128)(2,1)}), bf16[4,128,512]{2,1,0:T(8,128)(2,1)S(1)}, u32[]{:S(2)}, u32[]{:S(2)}) async-start(bf16[4,128,512]{2,1,0:T(8,128)(2,1)} %pool.1), calls=%async_computation.2 | async-start | bytes 1048576 | tf_op jit(solution)/shard_map/all_to_all | solution.py:354
  101.1 7.7 %collective-permute-start.3 = (f32[1,256]{1,0:T(1,128)S(1)}, f32[1,256]{1,0:T(1,128)S(1)}, u32[]{:S(2)}, u32[]{:S(2)}) collective-permute-start(f32[1,256]{1,0:T(1,128)S(1)} %bitcast.28), channel_id=1, source_target_pairs={{0,1},{1,2},{2,3},{3,0},{4,5},{5,6},{6,7},{7,4},{8,9},{9,10},{10,1... | collective-permute-start | bytes 3080 | tf_op jit(solution)/shard_map/ppermute | solution.py:364
  104.5 7.8 %collective-permute-start.4 = (f32[1,256]{1,0:T(1,128)S(1)}, f32[1,256]{1,0:T(1,128)S(1)}, u32[]{:S(2)}, u32[]{:S(2)}) collective-permute-start(f32[1,256]{1,0:T(1,128)S(1)} %bitcast.29), channel_id=1, source_target_pairs={{0,2},{1,3},{2,0},{3,1},{4,6},{5,7},{6,4},{7,5},{8,10},{9,11},{10,... | collective-permute-start | bytes 3080 | tf_op jit(solution)/shard_map/ppermute | solution.py:364
  108.8 4.6 %collective-permute-start.5 = (f32[1,256]{1,0:T(1,128)S(1)}, f32[1,256]{1,0:T(1,128)S(1)}, u32[]{:S(2)}, u32[]{:S(2)}) collective-permute-start(f32[1,256]{1,0:T(1,128)S(1)} %bitcast.30), channel_id=1, source_target_pairs={{0,3},{1,0},{2,1},{3,2},{4,7},{5,4},{6,5},{7,6},{8,11},{9,8},{10,9... | collective-permute-start | bytes 3080 | tf_op jit(solution)/shard_map/ppermute | solution.py:364
  113.4 9.8 %copy-start.7 = (bf16[4,2048,128]{2,1,0:T(8,128)(2,1)S(1)}, bf16[4,2048,128]{2,1,0:T(8,128)(2,1)}, u32[]{:S(2)}) copy-start(bf16[4,2048,128]{2,1,0:T(8,128)(2,1)} %get-tuple-element.25.pick_ref) | copy-start | bytes 6291460
  117.1 7.6 %collective-permute-start.6 = (bf16[2048,128]{1,0:T(8,128)(2,1)S(1)}, bf16[2048,128]{1,0:T(8,128)(2,1)S(1)}, u32[]{:S(2)}, u32[]{:S(2)}) collective-permute-start(bf16[2048,128]{1,0:T(8,128)(2,1)S(1)} %get-tuple-element.27), channel_id=1, source_target_pairs={{0,4},{4,0},{1,5},{5,1},{2,6},{6,2},{3,7},{7,3},{8,12},{12,8},{9,1... | collective-permute-start | bytes 1572872 | tf_op jit(solution)/shard_map/ppermute | solution.py:364
  220.2 7.8 %copy-start.1 = (s32[4,512]{1,0:T(4,128)S(1)}, s32[4,512]{1,0:T(4,128)}, u32[]{:S(2)}) copy-start(s32[4,512]{1,0:T(4,128)} %expired_ref.3) | copy-start | bytes 24580
  220.2 7.8 %copy-start.6 = (f32[4,512]{1,0:T(4,128)S(1)}, f32[4,512]{1,0:T(4,128)}, u32[]{:S(2)}) copy-start(f32[4,512]{1,0:T(4,128)} %acc_ref.1) | copy-start | bytes 24580
  220.3 17.3 %collective-permute-start.7 = (bf16[1024,256]{1,0:T(8,128)(2,1)S(1)}, bf16[1024,256]{1,0:T(8,128)(2,1)S(1)}, u32[]{:S(2)}, u32[]{:S(2)}) collective-permute-start(bf16[1024,256]{1,0:T(8,128)(2,1)S(1)} %bitcast.23), channel_id=1, source_target_pairs={{0,4},{4,0},{1,5},{5,1},{2,6},{6,2},{3,7},{7,3},{8,12},{12,8},{9,1... | collective-permute-start | bytes 1572872 | tf_op jit(solution)/shard_map/ppermute | solution.py:364

commit v5 on v4

--- a/solution.py
+++ b/solution.py
@@ -142,23 +142,18 @@
     ]
     for load in loads:
         load.start()
-    halves = halves_of(arrived_ref[...], half)
-    lane = iota((16, emb), 1).astype(F32)
+    arrived = arrived_ref[...]
+    low = (arrived & (half - 1)).astype(F32).T.astype(BF16)
+    side = (arrived >> (half.bit_length() - 1)).astype(F32).T.astype(BF16)
     diag = iota((emb, emb), 0) == iota((emb, emb), 1)
     parts = out_sem.shape[0]
     part = groups // parts
-    low = jnp.concatenate([lane.astype(BF16)] * (part * cap // 16), axis=0)
-    high = jnp.concatenate([(lane + emb).astype(BF16)] * (part * cap // 16), axis=0)
-    one, zero = jnp.ones((part * cap, emb), BF16), jnp.zeros((part * cap, emb), BF16)
-    lanes = (2 * width, emb)
-    which = [
-        jnp.concatenate([of_table(lanes, 0, t, kind, width, cap) for kind in (1, 0)], axis=1)
-        for t in range(tabs)
-    ]
+    lane = iota((cap, emb), 1).astype(F32)
+    names = lane.astype(BF16), (lane + emb).astype(BF16)
+    one, zero = jnp.ones((cap, emb), BF16), jnp.zeros((cap, emb), BF16)
     stores = []
     for c in range(parts):
         mine = slice(c * part, (c + 1) * part)
-        own = own_lines(halves[mine], part * cap)
         for t in range(tabs):
             if c == 0:
                 if t == 0:
@@ -167,18 +162,21 @@
                 for j in range(0, rows, emb):
                     gone = gone_ref[t : t + 1, j : j + emb].astype(F32)
                     column = jnp.sum(jnp.where(diag, gone, 0.0), axis=1, keepdims=True)
-                    side = j // half * emb
-                    table_ref[t, j % half : j % half + emb, side : side + emb] = jnp.where(
+                    at = j // half * emb
+                    table_ref[t, j % half : j % half + emb, at : at + emb] = jnp.where(
                         column > 0.5, 0.0, held_ref[t, j : j + emb, :]
                     ).astype(BF16)
-            found = dot(own, which[t])
-            at = found[:, :emb].astype(BF16)
-            pick = jnp.concatenate(
-                [jnp.where(at == low, one, zero), jnp.where(at == high, one, zero)], axis=1
-            )
-            both = dot(pick, table_ref[t]).astype(BF16)
-            line = jnp.where(found[:, emb:].astype(BF16) == zero, both[:, :emb], both[:, emb:])
-            sent_ref[mine, t * cap : (t + 1) * cap, :] = line.reshape(part, cap, emb)
+            lines = slice(t * cap, (t + 1) * cap)
+            picks, first = [], []
+            for o in range(c * part, (c + 1) * part):
+                row = jnp.broadcast_to(low[lines, o : o + 1], (cap, emb))
+                picks.append(
+                    jnp.concatenate([jnp.where(row == n, one, zero) for n in names], axis=1)
+                )
+                first.append(jnp.broadcast_to(side[lines, o : o + 1], (cap, emb)) == zero)
+            both = dot(jnp.concatenate(picks, axis=0), table_ref[t]).astype(BF16)
+            line = jnp.where(jnp.concatenate(first, axis=0), both[:, :emb], both[:, emb:])
+            sent_ref[mine, lines, :] = line.reshape(part, cap, emb)
         store = pltpu.make_async_copy(sent_ref.at[mine], out_ref.at[mine], out_sem.at[c])
         store.start()
         stores.append(store)
@@ -207,28 +205,20 @@
     return jnp.concatenate([row] * (length // 8), axis=0).astype(BF16)
 
 
-def pool_kernel(rows_ref, sample_ref, inv_ref, out_ref, feature_ref, sem_ref):
+def pool_kernel(rows_ref, sample_ref, inv_ref, out_ref):
     groups, width, emb = rows_ref.shape
     tabs, toks, _ = inv_ref.shape
     cap = width // tabs
     slots = groups * cap
     one, zero = jnp.ones((toks, slots), BF16), jnp.zeros((toks, slots), BF16)
     samples = sublanes(toks, slots)
-    copies = []
     for t in range(tabs):
         row = jnp.broadcast_to(sample_ref[t : t + 1, :] - 1.0, (16, slots)).astype(BF16)
         pick = jnp.where(jnp.concatenate([row] * (toks // 16), axis=0) == samples, one, zero)
         pooled = dot(pick, rows_ref[:, t * cap : (t + 1) * cap, :].reshape(slots, emb))
-        cols = slice(t * emb, (t + 1) * emb)
-        feature_ref[:, cols] = (pooled * inv_ref[t]).astype(BF16)
+        feature = (pooled * inv_ref[t]).astype(BF16)
         for k in range(out_ref.shape[0]):
-            copy = pltpu.make_async_copy(
-                feature_ref.at[:, cols], out_ref.at[k, :, cols], sem_ref.at[t, k]
-            )
-            copy.start()
-            copies.append(copy)
-    for copy in copies:
-        copy.wait()
+            out_ref[k, :, t * emb : (t + 1) * emb] = feature
 
 
 def silu_slope(preact):
@@ -238,13 +228,22 @@
 
 def dense_kernel(
     at_ref, feat_ref, w0, w1, w2, w3, u0, u1, u2, u3, labels_ref,
-    logits_ref, grad_ref, mine_ref, other_ref,
+    logits_ref, grad_ref, mine_ref, other_ref, held_ref, sem_ref,
 ):
     parts, toks, feats = feat_ref.shape
-    weights, units = (w0, w1, w2, w3), (u0, u1, u2, u3)
+    units = (u0, u1, u2, u3)
+    loads = [
+        pltpu.make_async_copy(w, held_ref.at[k], sem_ref.at[k])
+        for k, w in enumerate((w1, w2, w3))
+    ]
+    for load in loads:
+        load.start()
+    weights = [w0] + [held_ref.at[k] for k in range(parts - 1)]
     me, core = at_ref[0], at_ref[1]
     preacts, scores = [], []
-    for w, u in zip(weights, units):
+    for k, (w, u) in enumerate(zip(weights, units)):
+        if k > 0:
+            loads[k - 1].wait()
         pre = sum(
             dot(feat_ref[q], w[q * feats : (q + 1) * feats, :]) for q in range(parts)
         )
@@ -428,7 +427,7 @@
             pltpu.VMEM((tabs, rows // 2, 2 * emb), BF16),
             pltpu.VMEM((groups, width, emb), BF16),
             dma((tabs + 1,)),
-            dma((4,)),
+            dma((8,)),
         ],
         compiler_params=params(24),
         name="fetch",
@@ -446,13 +445,13 @@
     )(later)
     features = pl.pallas_call(
         pool_kernel,
-        in_specs=[vmem, vmem, vmem],
-        out_specs=hbm,
-        out_shape=pltpu.HBM((parts, toks, feats), BF16),
-        scratch_shapes=[pltpu.VMEM((toks, feats), BF16), dma((tabs, parts))],
+        out_shape=shape((parts, toks, feats), BF16),
         compiler_params=params(24),
         name="pool",
     )(returned, sample_row, inv)
+    features, place, weights, units = lax.optimization_barrier(
+        (features, place, weights, units)
+    )
     portion = a2a(features, "mp")
     label_column = pl.pallas_call(
         labels_kernel,
@@ -464,17 +463,20 @@
     lines, half = hidden_weight.shape[0], units_dev // 2
     logits, grad, mine, other = pl.pallas_call(
         dense_kernel,
-        in_specs=[pl.BlockSpec(memory_space=pltpu.SMEM)]
-        + [pl.BlockSpec(memory_space=pltpu.VMEM)] * (2 * parts + 2),
+        in_specs=[smem, vmem, vmem] + [hbm] * (parts - 1) + [vmem] * (parts + 1),
         out_shape=(
             shape((toks, toks), F32),
             shape((toks, feats), F32),
             shape((lines, half), BF16),
             shape((lines, half), BF16),
         ),
+        scratch_shapes=[
+            pltpu.VMEM((parts - 1, lines, units_dev), BF16),
+            dma((parts - 1,)),
+        ],
         compiler_params=params(24),
         name="dense",
-    )(place, portion, *weights, *units, label_column)
+    )(place, portion, weights[0], *map(held, weights[1:]), *units, label_column)
     joined = ring(other, NEAR, 1)
     share = lines // groups
     outgoing = pl.pallas_call(

time: 240 us -> 243 us (1.012)
  blocking collectives: 125 us -> 132 us
  waiting for transfers between devices: 38.7 us -> 34.8 us
    all_to_all x2, waiting for transfers between devices: 37.4 us -> 6.6 us  [a2a(): return lax.all_to_all(value, axis, split_axis=0, concat_axis=0, tiled=True)]
    ppermute x8, waiting for transfers between devices: 1.31 us -> 28.2 us  [ring(): lax.ppermute(value, axis, [(i, (i + step) % size) for i in range(size)])]
    all_to_all x3, blocking collectives: 125 us -> 132 us  [a2a(): return lax.all_to_all(value, axis, split_axis=0, concat_axis=0, tiled=True)]
where the time goes in v5:
time: 243 us; the launch traced here: 242 us
  blocking collectives  132 us (54%)
  starting transfers between devices  41.9 us (17%)
  waiting for transfers between devices  34.8 us (14%)
  Pallas kernels  30 us (12%)
    all_to_all x3, blocking collectives, a2a(): return lax.all_to_all(value, axis, split_axis=0, concat_axis=0, tiled=True)  132 us
    ppermute x8, starting transfers between devices, ring(): lax.ppermute(value, axis, [(i, (i + step) % size) for i in range(size)])  32.3 us
    ppermute x8, waiting for transfers between devices, ring(): lax.ppermute(value, axis, [(i, (i + step) % size) for i in range(size)])  28.2 us
    all_to_all x2, starting transfers between devices, a2a(): return lax.all_to_all(value, axis, split_axis=0, concat_axis=0, tiled=True)  9.58 us
    pallas_call x1, Pallas kernels, shards(): pl.pallas_call(update_kernel, grid=(tabs,), in_specs=[block((groups, cap,...  8.18 us
    all_to_all x2, waiting for transfers between devices, a2a(): return lax.all_to_all(value, axis, split_axis=0, concat_axis=0, tiled=True)  6.6 us
  transfers between devices with their start and end apart: 10, of which 3 were waited for; matrix products, arithmetic and copies ran while one was open for 0% of the time, Pallas kernels for 7%

profile of v5, /device:TPU:1, one launch (start us, length us, event | category | flops | bytes accessed | tf_op | source)
XLA Modules:
  0.0 242.1 jit_solution(109709280646590580)
XLA Ops:
  0.6 2.7 %slots.1 = (s32[128,64]{1,0:T(8,128)S(1)}, f32[128,64]{1,0:T(8,128)S(1)}, f32[4,128,128]{2,1,0:T(8,128)S(1)}) custom-call(s32[4,128]{1,0:T(4,128)} %len_ref.1, s32[4,8,128]{2,1,0:T(8,128)} %bitcast.38, s32[4,8,128]{2,1,0:T(8,128)} %bitcast.39, s32[4,8,128]{2,1,0:T(8,128)} %bitcast.40), custom_call_target="tpu_custom_call" | custom-call | tf_op jit(solution)/shard_map/slots/pallas_call | solution.py:381
  3.3 29.7 %all_to_all.31 = s32[128,1,64]{2,1,0:T(1,128)S(1)} all-to-all(s32[128,1,64]{2,1,0:T(1,128)S(1)} %bitcast.27), channel_id=1, replica_groups=mesh['dp_0'=8,'dp_1'=8,'dp_2'=2,'mp'=4] {'dp_0','dp_1','dp_2'}, dimensions={0} | all-to-all | bytes 65536 | tf_op jit(solution)/shard_map/all_to_all | solution.py:353
  33.0 4.7 %fetch.1 = bf16[128,64,128]{2,1,0:T(8,128)(2,1)} custom-call(s32[128,64]{1,0:T(8,128)S(1)} %bitcast.25, s32[4,512]{1,0:T(4,128)} %expired_ref.3, f32[4,512,128]{2,1,0:T(8,128)} %emb_ref.3), custom_call_target="tpu_custom_call" | custom-call | tf_op jit(solution)/shard_map/fetch/pallas_call | solution.py:419
  37.8 5.9 %all-to-all-start.1 = ((bf16[128,64,128]{2,1,0:T(8,128)(2,1)}), bf16[128,64,128]{2,1,0:T(8,128)(2,1)S(1)}, u32[]{:S(2)}, u32[]{:S(2)}) async-start(bf16[128,64,128]{2,1,0:T(8,128)(2,1)} %fetch.1), calls=%async_computation.1 | async-start | bytes 4194304 | tf_op jit(solution)/shard_map/all_to_all | solution.py:353
  43.7 3.1 %collective-permute-start = (bf16[2048,256]{1,0:T(8,128)(2,1)S(1)}, bf16[2048,256]{1,0:T(8,128)(2,1)}, u32[]{:S(2)}, u32[]{:S(2)}) collective-permute-start(bf16[2048,256]{1,0:T(8,128)(2,1)S(1)} %copy-done), channel_id=1, source_target_pairs={{0,1},{1,2},{2,3},{3,0},{4,5},{5,6},{6,7},{7,4},{8,9},{9,10},{10,1... | collective-permute-start | bytes 3145736 | tf_op jit(solution)/shard_map/ppermute | solution.py:363
  46.9 4.4 %collective-permute-start.1 = (bf16[2048,256]{1,0:T(8,128)(2,1)S(1)}, bf16[2048,256]{1,0:T(8,128)(2,1)}, u32[]{:S(2)}, u32[]{:S(2)}) collective-permute-start(bf16[2048,256]{1,0:T(8,128)(2,1)S(1)} %copy-done), channel_id=1, source_target_pairs={{0,2},{1,3},{2,0},{3,1},{4,6},{5,7},{6,4},{7,5},{8,10},{9,11},{10,... | collective-permute-start | bytes 3145736 | tf_op jit(solution)/shard_map/ppermute | solution.py:363
  51.2 3.1 %collective-permute-start.2 = (bf16[2048,256]{1,0:T(8,128)(2,1)S(1)}, bf16[2048,256]{1,0:T(8,128)(2,1)}, u32[]{:S(2)}, u32[]{:S(2)}) collective-permute-start(bf16[2048,256]{1,0:T(8,128)(2,1)S(1)} %copy-done), channel_id=1, source_target_pairs={{0,3},{1,0},{2,1},{3,2},{4,7},{5,4},{6,5},{7,6},{8,11},{9,8},{10,9... | collective-permute-start | bytes 3145736 | tf_op jit(solution)/shard_map/ppermute | solution.py:363
  54.3 2.2 collective-permute-start.3
  57.4 2.5 %samples.1 = (bf16[4,2048,128]{2,1,0:T(8,128)(2,1)}, f32[4,2048]{1,0:T(4,128)S(1)}) custom-call(f32[128,64]{1,0:T(8,128)S(1)} %copy-done.7), custom_call_target="tpu_custom_call" | custom-call | flops 4294967296 | bytes 1048576 | tf_op jit(solution)/shard_map/samples/pallas_call | solution.py:404
  59.9 2.9 %collective-permute-start.4 = (f32[1,256]{1,0:T(1,128)S(1)}, f32[1,256]{1,0:T(1,128)S(1)}, u32[]{:S(2)}, u32[]{:S(2)}) collective-permute-start(f32[1,256]{1,0:T(1,128)S(1)} %bitcast.29), channel_id=1, source_target_pairs={{0,2},{1,3},{2,0},{3,1},{4,6},{5,7},{6,4},{7,5},{8,10},{9,11},{10,... | collective-permute-start | bytes 3080 | tf_op jit(solution)/shard_map/ppermute | solution.py:363
  62.8 28.0 %collective-permute-done.3.u1 = f32[1,256]{1,0:T(1,128)S(1)} collective-permute-done((f32[1,256]{1,0:T(1,128)S(1)}, f32[1,256]{1,0:T(1,128)S(1)}, u32[]{:S(2)}, u32[]{:S(2)}) %collective-permute-start.3) | collective-permute-done | bytes 1056 | tf_op jit(solution)/shard_map/ppermute | solution.py:363
  90.8 5.5 %collective-permute-start.5 = (f32[1,256]{1,0:T(1,128)S(1)}, f32[1,256]{1,0:T(1,128)S(1)}, u32[]{:S(2)}, u32[]{:S(2)}) collective-permute-start(f32[1,256]{1,0:T(1,128)S(1)} %bitcast.30), channel_id=1, source_target_pairs={{0,3},{1,0},{2,1},{3,2},{4,7},{5,4},{6,5},{7,6},{8,11},{9,8},{10,9... | collective-permute-start | bytes 3080 | tf_op jit(solution)/shard_map/ppermute | solution.py:363
  96.4 1.5 pool.1
  97.9 3.7 %all-to-all-start.2 = ((bf16[4,128,512]{2,1,0:T(8,128)(2,1)}), bf16[4,128,512]{2,1,0:T(8,128)(2,1)S(1)}, u32[]{:S(2)}, u32[]{:S(2)}) async-start(bf16[4,128,512]{2,1,0:T(8,128)(2,1)} %pool.1), calls=%async_computation.2 | async-start | bytes 1048576 | tf_op jit(solution)/shard_map/all_to_all | solution.py:353
  101.7 6.6 %all-to-all-done.2.feat_ref = bf16[4,128,512]{2,1,0:T(8,128)(2,1)S(1)} async-done(((bf16[4,128,512]{2,1,0:T(8,128)(2,1)}), bf16[4,128,512]{2,1,0:T(8,128)(2,1)S(1)}, u32[]{:S(2)}, u32[]{:S(2)}) %all-to-all-start.2) | async-done | bytes 524320 | tf_op jit(solution)/shard_map/all_to_all | solution.py:353
  109.0 4.2 %dense.1 = (f32[128,128]{1,0:T(8,128)S(1)}, f32[128,512]{1,0:T(8,128)S(1)}, bf16[2048,128]{1,0:T(8,128)(2,1)S(1)}, bf16[2048,128]{1,0:T(8,128)(2,1)S(1)}) custom-call(s32[2]{0:T(128)S(1)} %pad_add_fusion.at_ref, bf16[4,128,512]{2,1,0:T(8,128)(2,1)S(1)} %all-to-all-done.2.feat_ref, bf16[2048,256]{1,0:T(8,128)(2,1)S(1)} %copy-done, ...), custom_call_target="tpu_custom_call" | custom-call | tf_op jit(solution)/shard_map/dense/pallas_call | solution.py:464
  113.2 6.1 %collective-permute-start.6 = (bf16[2048,128]{1,0:T(8,128)(2,1)S(1)}, bf16[2048,128]{1,0:T(8,128)(2,1)S(1)}, u32[]{:S(2)}, u32[]{:S(2)}) collective-permute-start(bf16[2048,128]{1,0:T(8,128)(2,1)S(1)} %get-tuple-element.47), channel_id=1, source_target_pairs={{0,4},{4,0},{1,5},{5,1},{2,6},{6,2},{3,7},{7,3},{8,12},{12,8},{9,1... | collective-permute-start | bytes 1572872 | tf_op jit(solution)/shard_map/ppermute | solution.py:363
  121.1 75.3 %all_to_all.32.grads_ref = bf16[128,80,128]{2,1,0:T(8,128)(2,1)S(1)} all-to-all(bf16[128,80,128]{2,1,0:T(8,128)(2,1)S(1)} %constant_dynamic-update-slice_fusion), channel_id=1, replica_groups=mesh['dp_0'=8,'dp_1'=8,'dp_2'=2,'mp'=4] {'dp_0','dp_1','dp_2'}, dimensions={0} | all-to-all | bytes 5242880 | tf_op jit(solution)/shard_map/all_to_all | solution.py:353
  196.7 26.6 %all_to_all.33 = bf16[64,2,2,8,128]{4,3,2,1,0:T(8,128)(2,1)S(1)} all-to-all(bf16[64,2,2,8,128]{4,3,2,1,0:T(8,128)(2,1)S(1)} %broadcast_in_dim.2), channel_id=1, replica_groups=mesh['dp_0'=8,'dp_1'=8,'dp_2'=2,'mp'=4] {'dp_0','dp_1'}, dimensions={0} | all-to-all | bytes 1048576 | tf_op jit(solution)/shard_map/all_to_all | solution.py:353
  223.2 5.1 %collective-permute-start.7 = (bf16[1024,256]{1,0:T(8,128)(2,1)S(1)}, bf16[1024,256]{1,0:T(8,128)(2,1)S(1)}, u32[]{:S(2)}, u32[]{:S(2)}) collective-permute-start(bf16[1024,256]{1,0:T(8,128)(2,1)S(1)} %bitcast.23), channel_id=1, source_target_pairs={{0,4},{4,0},{1,5},{5,1},{2,6},{6,2},{3,7},{7,3},{8,12},{12,8},{9,1... | collective-permute-start | bytes 1572872 | tf_op jit(solution)/shard_map/ppermute | solution.py:363
  228.3 2.1 wanted.1.wanted_ref
  231.0 8.2 %update.1 = (f32[4,512,128]{2,1,0:T(8,128)}, f32[4,512]{1,0:T(4,128)}) custom-call(bf16[128,80,128]{2,1,0:T(8,128)(2,1)S(1)} %all_to_all.32.grads_ref, f32[4,16,2048]{2,1,0:T(8,128)} %wanted.1.wanted_ref, f32[4,512,128]{2,1,0:T(8,128)} %emb_ref.3, s32[4,512]{1,0:T(4,128)S(1)} %copy-done.1, f32[4,512]{1,0:T(4,128)S(1)} %copy-done.8), custom_call_target="tpu_custom_call" | custom-call | flops 4294967296 | bytes 1048576 | tf_op jit(solution)/shard_map/update/pallas_call | solution.py:521
  239.2 1.3 near.1.begun_ref
  240.6 1.3 far.1
  (39 shorter events, 4.3 us)
Async XLA Ops:
  3.3 29.7 %copy-start.6 = (f32[128,64]{1,0:T(8,128)}, f32[128,64]{1,0:T(8,128)S(1)}, u32[]{:S(2)}) copy-start(f32[128,64]{1,0:T(8,128)S(1)} %get-tuple-element.29.sample_ref) | copy-start | bytes 98308
  37.8 5.9 %copy-start = (bf16[2048,256]{1,0:T(8,128)(2,1)S(1)}, bf16[2048,256]{1,0:T(8,128)(2,1)}, u32[]{:S(2)}) copy-start(bf16[2048,256]{1,0:T(8,128)(2,1)} %w0) | copy-start | bytes 3145732
  37.8 16.5 %copy-start.2 = (f32[256]{0:T(256)S(1)}, f32[256]{0:T(256)}, u32[]{:S(2)}) copy-start(f32[256]{0:T(256)} %param.18) | copy-start | bytes 3076
  37.8 58.6 %all-to-all-start.1 = ((bf16[128,64,128]{2,1,0:T(8,128)(2,1)}), bf16[128,64,128]{2,1,0:T(8,128)(2,1)S(1)}, u32[]{:S(2)}, u32[]{:S(2)}) async-start(bf16[128,64,128]{2,1,0:T(8,128)(2,1)} %fetch.1), calls=%async_computation.1 | async-start | bytes 4194304 | tf_op jit(solution)/shard_map/all_to_all | solution.py:353
  43.7 54.2 %collective-permute-start = (bf16[2048,256]{1,0:T(8,128)(2,1)S(1)}, bf16[2048,256]{1,0:T(8,128)(2,1)}, u32[]{:S(2)}, u32[]{:S(2)}) collective-permute-start(bf16[2048,256]{1,0:T(8,128)(2,1)S(1)} %copy-done), channel_id=1, source_target_pairs={{0,1},{1,2},{2,3},{3,0},{4,5},{5,6},{6,7},{7,4},{8,9},{9,10},{10,1... | collective-permute-start | bytes 3145736 | tf_op jit(solution)/shard_map/ppermute | solution.py:363
  46.9 51.1 %collective-permute-start.1 = (bf16[2048,256]{1,0:T(8,128)(2,1)S(1)}, bf16[2048,256]{1,0:T(8,128)(2,1)}, u32[]{:S(2)}, u32[]{:S(2)}) collective-permute-start(bf16[2048,256]{1,0:T(8,128)(2,1)S(1)} %copy-done), channel_id=1, source_target_pairs={{0,2},{1,3},{2,0},{3,1},{4,6},{5,7},{6,4},{7,5},{8,10},{9,11},{10,... | collective-permute-start | bytes 3145736 | tf_op jit(solution)/shard_map/ppermute | solution.py:363
  51.2 46.7 %collective-permute-start.2 = (bf16[2048,256]{1,0:T(8,128)(2,1)S(1)}, bf16[2048,256]{1,0:T(8,128)(2,1)}, u32[]{:S(2)}, u32[]{:S(2)}) collective-permute-start(bf16[2048,256]{1,0:T(8,128)(2,1)S(1)} %copy-done), channel_id=1, source_target_pairs={{0,3},{1,0},{2,1},{3,2},{4,7},{5,4},{6,5},{7,6},{8,11},{9,8},{10,9... | collective-permute-start | bytes 3145736 | tf_op jit(solution)/shard_map/ppermute | solution.py:363
  54.3 36.5 %collective-permute-start.3 = (f32[1,256]{1,0:T(1,128)S(1)}, f32[1,256]{1,0:T(1,128)S(1)}, u32[]{:S(2)}, u32[]{:S(2)}) collective-permute-start(f32[1,256]{1,0:T(1,128)S(1)} %bitcast.28), channel_id=1, source_target_pairs={{0,1},{1,2},{2,3},{3,0},{4,5},{5,6},{6,7},{7,4},{8,9},{9,10},{10,1... | collective-permute-start | bytes 3080 | tf_op jit(solution)/shard_map/ppermute | solution.py:363
  56.5 0.8 copy-start.7
  59.9 41.7 %copy-start.5 = (s32[128]{0:T(128)S(1)}, s32[128]{0:T(128)}, u32[]{:S(2)}) copy-start(s32[128]{0:T(128)} %param.19) | copy-start | bytes 1540
  59.9 38.0 %collective-permute-start.4 = (f32[1,256]{1,0:T(1,128)S(1)}, f32[1,256]{1,0:T(1,128)S(1)}, u32[]{:S(2)}, u32[]{:S(2)}) collective-permute-start(f32[1,256]{1,0:T(1,128)S(1)} %bitcast.29), channel_id=1, source_target_pairs={{0,2},{1,3},{2,0},{3,1},{4,6},{5,7},{6,4},{7,5},{8,10},{9,11},{10,... | collective-permute-start | bytes 3080 | tf_op jit(solution)/shard_map/ppermute | solution.py:363
  90.8 7.1 %collective-permute-start.5 = (f32[1,256]{1,0:T(1,128)S(1)}, f32[1,256]{1,0:T(1,128)S(1)}, u32[]{:S(2)}, u32[]{:S(2)}) collective-permute-start(f32[1,256]{1,0:T(1,128)S(1)} %bitcast.30), channel_id=1, source_target_pairs={{0,3},{1,0},{2,1},{3,2},{4,7},{5,4},{6,5},{7,6},{8,11},{9,8},{10,9... | collective-permute-start | bytes 3080 | tf_op jit(solution)/shard_map/ppermute | solution.py:363
  97.9 3.8 %copy-start.3 = (f32[1,256]{1,0:T(1,128)}, f32[1,256]{1,0:T(1,128)S(1)}, u32[]{:S(2)}) copy-start(f32[1,256]{1,0:T(1,128)S(1)} %collective-permute-done.5.u3) | copy-start | bytes 3076
  97.9 10.4 %all-to-all-start.2 = ((bf16[4,128,512]{2,1,0:T(8,128)(2,1)}), bf16[4,128,512]{2,1,0:T(8,128)(2,1)S(1)}, u32[]{:S(2)}, u32[]{:S(2)}) async-start(bf16[4,128,512]{2,1,0:T(8,128)(2,1)} %pool.1), calls=%async_computation.2 | async-start | bytes 1048576 | tf_op jit(solution)/shard_map/all_to_all | solution.py:353
  108.3 0.7 copy-start.4
  109.0 10.4 %copy-start.9 = (bf16[4,2048,128]{2,1,0:T(8,128)(2,1)S(1)}, bf16[4,2048,128]{2,1,0:T(8,128)(2,1)}, u32[]{:S(2)}) copy-start(bf16[4,2048,128]{2,1,0:T(8,128)(2,1)} %get-tuple-element.45.pick_ref) | copy-start | bytes 6291460
  113.2 7.6 %collective-permute-start.6 = (bf16[2048,128]{1,0:T(8,128)(2,1)S(1)}, bf16[2048,128]{1,0:T(8,128)(2,1)S(1)}, u32[]{:S(2)}, u32[]{:S(2)}) collective-permute-start(bf16[2048,128]{1,0:T(8,128)(2,1)S(1)} %get-tuple-element.47), channel_id=1, source_target_pairs={{0,4},{4,0},{1,5},{5,1},{2,6},{6,2},{3,7},{7,3},{8,12},{12,8},{9,1... | collective-permute-start | bytes 1572872 | tf_op jit(solution)/shard_map/ppermute | solution.py:363
  223.2 7.8 %copy-start.1 = (s32[4,512]{1,0:T(4,128)S(1)}, s32[4,512]{1,0:T(4,128)}, u32[]{:S(2)}) copy-start(s32[4,512]{1,0:T(4,128)} %expired_ref.3) | copy-start | bytes 24580
  223.2 7.8 %copy-start.8 = (f32[4,512]{1,0:T(4,128)S(1)}, f32[4,512]{1,0:T(4,128)}, u32[]{:S(2)}) copy-start(f32[4,512]{1,0:T(4,128)} %acc_ref.1) | copy-start | bytes 24580
  223.2 17.3 %collective-permute-start.7 = (bf16[1024,256]{1,0:T(8,128)(2,1)S(1)}, bf16[1024,256]{1,0:T(8,128)(2,1)S(1)}, u32[]{:S(2)}, u32[]{:S(2)}) collective-permute-start(bf16[1024,256]{1,0:T(8,128)(2,1)S(1)} %bitcast.23), channel_id=1, source_target_pairs={{0,4},{4,0},{1,5},{5,1},{2,6},{6,2},{3,7},{7,3},{8,12},{12,8},{9,1... | collective-permute-start | bytes 1572872 | tf_op jit(solution)/shard_map/ppermute | solution.py:363

commit v6 on v5

--- a/solution.py
+++ b/solution.py
@@ -227,26 +227,24 @@
 
 
 def dense_kernel(
-    at_ref, feat_ref, w0, w1, w2, w3, u0, u1, u2, u3, labels_ref,
-    logits_ref, grad_ref, mine_ref, other_ref, held_ref, sem_ref,
+    at_ref, feat_ref, own_ref, near_ref, far_ref, u0, u1, u2, u3, labels_ref,
+    logits_ref, grad_ref, mine_ref, other_ref,
 ):
     parts, toks, feats = feat_ref.shape
     units = (u0, u1, u2, u3)
-    loads = [
-        pltpu.make_async_copy(w, held_ref.at[k], sem_ref.at[k])
-        for k, w in enumerate((w1, w2, w3))
-    ]
-    for load in loads:
-        load.start()
-    weights = [w0] + [held_ref.at[k] for k in range(parts - 1)]
     me, core = at_ref[0], at_ref[1]
+    order = [(2 * core + q) % parts for q in range(parts)]
     preacts, scores = [], []
-    for k, (w, u) in enumerate(zip(weights, units)):
-        if k > 0:
-            loads[k - 1].wait()
-        pre = sum(
-            dot(feat_ref[q], w[q * feats : (q + 1) * feats, :]) for q in range(parts)
-        )
+    for k, u in enumerate(units):
+        pre = jnp.zeros((toks, u.shape[1]), F32)
+        for q, at in enumerate(order):
+            if k == 0:
+                w = own_ref[pl.ds(pl.multiple_of(at * feats, feats), feats), :]
+            else:
+                half = near_ref if q < parts // 2 else far_ref
+                start = q % (parts // 2) * feats
+                w = half[k - 1, start : start + feats, :]
+            pre = pre + dot(feat_ref[at], w)
         hidden = jax.nn.silu(pre).astype(BF16).astype(F32)
         preacts.append(pre)
         scores.append(jnp.sum(hidden * u[...], axis=1, keepdims=True))
@@ -259,9 +257,8 @@
         logits = logits + score
     dlogit = (jax.nn.sigmoid(logits) - labels_ref[...])[:, 0:1]
     logits_ref[...] = jnp.broadcast_to(logits, logits_ref.shape)
-    start = pl.multiple_of(me * feats, feats)
     grads = jnp.zeros((toks, feats), F32)
-    for k, (w, u, pre) in enumerate(zip(weights, units, preacts)):
+    for k, (u, pre) in enumerate(zip(units, preacts)):
         dhidden = (dlogit * u[...] * silu_slope(pre)).astype(BF16)
         if k == 0:
             half = dhidden.shape[1] // 2
@@ -276,7 +273,13 @@
                 ).astype(BF16)
                 mine_ref[lines, :] = part[:, :half]
                 other_ref[lines, :] = part[:, half:]
-        grads = grads + dot(dhidden, w[pl.ds(start, feats), :], NT)
+            w = own_ref[pl.ds(pl.multiple_of(me * feats, feats), feats), :]
+        else:
+            lines = pl.ds(pl.multiple_of(me % (parts // 2) * feats, feats), feats)
+            w = jnp.where(
+                me // (parts // 2) == core, near_ref[k - 1, lines, :], far_ref[k - 1, lines, :]
+            )
+        grads = grads + dot(dhidden, w, NT)
     grad_ref[...] = grads
 
 
@@ -319,18 +322,6 @@
                 new_acc_ref[table : table + 1, cols] = line
 
 
-def near_kernel(at_ref, piece_ref, out_ref, sem):
-    copy = pltpu.make_async_copy(piece_ref, out_ref.at[at_ref[1]], sem)
-    copy.start()
-    copy.wait()
-
-
-def far_kernel(at_ref, piece_ref, begun_ref, out_ref, sem):
-    copy = pltpu.make_async_copy(piece_ref, out_ref.at[1 - at_ref[1]], sem)
-    copy.start()
-    copy.wait()
-
-
 def shape(dims, dtype):
     return jax.ShapeDtypeStruct(dims, dtype)
 
@@ -399,8 +390,11 @@
         )
     )
     arrived = a2a(request, DP)
+    lines, units_dev = hidden_weight.shape
     weight, _ = lax.optimization_barrier((hidden_weight, request))
-    weights = [weight] + [ring(weight, "mp", k) for k in range(1, parts)]
+    mine = lax.dynamic_slice(weight, (core * (lines // 2), 0), (lines // 2, units_dev))
+    near_weights = jnp.stack([ring(mine, "mp", k) for k in range(1, parts)])
+    far_weights = ring(near_weights, NEAR, 1)
     pick, sample_row = pl.pallas_call(
         samples_kernel,
         out_shape=(
@@ -449,8 +443,8 @@
         compiler_params=params(24),
         name="pool",
     )(returned, sample_row, inv)
-    features, place, weights, units = lax.optimization_barrier(
-        (features, place, weights, units)
+    features, place, near_weights, far_weights, units = lax.optimization_barrier(
+        (features, place, near_weights, far_weights, units)
     )
     portion = a2a(features, "mp")
     label_column = pl.pallas_call(
@@ -459,24 +453,19 @@
         compiler_params=params(4),
         name="labels",
     )(labels.reshape(1, toks))
-    units_dev = hidden_weight.shape[1]
-    lines, half = hidden_weight.shape[0], units_dev // 2
+    half = units_dev // 2
     logits, grad, mine, other = pl.pallas_call(
         dense_kernel,
-        in_specs=[smem, vmem, vmem] + [hbm] * (parts - 1) + [vmem] * (parts + 1),
+        in_specs=[smem] + [vmem] * (parts + 5),
         out_shape=(
             shape((toks, toks), F32),
             shape((toks, feats), F32),
             shape((lines, half), BF16),
             shape((lines, half), BF16),
         ),
-        scratch_shapes=[
-            pltpu.VMEM((parts - 1, lines, units_dev), BF16),
-            dma((parts - 1,)),
-        ],
         compiler_params=params(24),
         name="dense",
-    )(place, portion, weights[0], *map(held, weights[1:]), *units, label_column)
+    )(place, portion, hidden_weight, near_weights, far_weights, *units, label_column)
     joined = ring(other, NEAR, 1)
     share = lines // groups
     outgoing = pl.pallas_call(
@@ -504,20 +493,9 @@
     near = from_everyone(own, FAR)
     near = near.transpose(0, 1, 3, 2, 4).reshape(lines // 2, units_dev)
     far = ring(near, NEAR, 1)
-    weight_grad = None
-    for kernel, piece in ((near_kernel, near), (far_kernel, far)):
-        begun = [] if weight_grad is None else [weight_grad]
-        weight_grad = pl.pallas_call(
-            kernel,
-            in_specs=[smem, vmem] + [hbm] * len(begun),
-            out_specs=hbm,
-            out_shape=pltpu.HBM((2, lines // 2, units_dev), BF16),
-            input_output_aliases={2: 0} if begun else {},
-            scratch_shapes=[dma],
-            compiler_params=params(4),
-            name="near" if weight_grad is None else "far",
-        )(place, piece, *begun)
-    weight_grad = weight_grad.reshape(lines, units_dev)
+    weight_grad = jnp.concatenate(
+        [jnp.where(core == 0, near, far), jnp.where(core == 0, far, near)]
+    )
     new_rows, new_acc = pl.pallas_call(
         update_kernel,
         grid=(tabs,),

time: 243 us -> 236 us (0.971)
  blocking collectives: 132 us -> 102 us
  waiting for transfers between devices: 34.8 us -> 50.7 us
  starting transfers between devices: 41.9 us -> 50 us
  Pallas kernels: 30 us -> 26 us
  other arithmetic: 0.32 us -> 2.79 us
    all_to_all x3 -> x2, blocking collectives: 132 us -> 102 us  [a2a(): return lax.all_to_all(value, axis, split_axis=0, concat_axis=0, tiled=True)]
    all_to_all x2 -> x3, waiting for transfers between devices: 6.6 us -> 27 us  [a2a(): return lax.all_to_all(value, axis, split_axis=0, concat_axis=0, tiled=True)]
    all_to_all x2 -> x3, starting transfers between devices: 9.58 us -> 19.2 us  [a2a(): return lax.all_to_all(value, axis, split_axis=0, concat_axis=0, tiled=True)]
    ppermute x8 -> x9, waiting for transfers between devices: 28.2 us -> 23.7 us  [ring(): lax.ppermute(value, axis, [(i, (i + step) % size) for i in range(size)])]
    pallas_call x3 -> x1, Pallas kernels: 6.93 us -> 3.71 us  [shards(): pl.pallas_call(dense_kernel, in_specs=[smem] + [vmem] * (parts + 5), out_...]
    ppermute x8 -> x9, starting transfers between devices: 32.3 us -> 30.9 us  [ring(): lax.ppermute(value, axis, [(i, (i + step) % size) for i in range(size)])]
  transfers between devices with their start and end apart: 10 -> 12, of which waited for: 3 -> 7; matrix products, arithmetic and copies ran while one was open for 0% -> 1% of each run, Pallas kernels for 7% -> 6%
where the time goes in v6:
time: 236 us
  blocking collectives  102 us (43%)
  waiting for transfers between devices  50.7 us (21%)
  starting transfers between devices  50 us (21%)
  Pallas kernels  26 us (11%)
  local copies, waits for them, and re-layouts  3.33 us (1%)
  other arithmetic  2.79 us (1%)
    all_to_all x2, blocking collectives, a2a(): return lax.all_to_all(value, axis, split_axis=0, concat_axis=0, tiled=True)  102 us
    ppermute x9, starting transfers between devices, ring(): lax.ppermute(value, axis, [(i, (i + step) % size) for i in range(size)])  30.9 us
    all_to_all x3, waiting for transfers between devices, a2a(): return lax.all_to_all(value, axis, split_axis=0, concat_axis=0, tiled=True)  27 us
    ppermute x9, waiting for transfers between devices, ring(): lax.ppermute(value, axis, [(i, (i + step) % size) for i in range(size)])  23.7 us
    all_to_all x3, starting transfers between devices, a2a(): return lax.all_to_all(value, axis, split_axis=0, concat_axis=0, tiled=True)  19.2 us
    pallas_call x1, Pallas kernels, shards(): pl.pallas_call(update_kernel, grid=(tabs,), in_specs=[block((groups, cap,...  8.18 us
    pallas_call x1, Pallas kernels, shards(): pl.pallas_call(fetch_kernel, in_specs=[vmem, hbm, hbm], out_specs=hbm, ou...  4.73 us
  transfers between devices with their start and end apart: 12, of which 7 were waited for; matrix products, arithmetic and copies ran while one was open for 1% of the time, Pallas kernels for 6%

profile of v6, /device:TPU:1, one launch (start us, length us, event | category | flops | bytes accessed | tf_op | source)
XLA Modules:
  0.0 235.6 jit_solution(6593034197237850024)
XLA Ops:
  0.6 2.7 %slots.1 = (s32[128,64]{1,0:T(8,128)S(1)}, f32[128,64]{1,0:T(8,128)S(1)}, f32[4,128,128]{2,1,0:T(8,128)S(1)}) custom-call(s32[4,128]{1,0:T(4,128)} %len_ref.1, s32[4,8,128]{2,1,0:T(8,128)} %bitcast.42, s32[4,8,128]{2,1,0:T(8,128)} %bitcast.43, s32[4,8,128]{2,1,0:T(8,128)} %bitcast.44), custom_call_target="tpu_custom_call" | custom-call | tf_op jit(solution)/shard_map/slots/pallas_call | solution.py:372
  3.3 29.7 %all_to_all.31 = s32[128,1,64]{2,1,0:T(1,128)S(1)} all-to-all(s32[128,1,64]{2,1,0:T(1,128)S(1)} %bitcast.27), channel_id=1, replica_groups=mesh['dp_0'=8,'dp_1'=8,'dp_2'=2,'mp'=4] {'dp_0','dp_1','dp_2'}, dimensions={0} | all-to-all | bytes 65536 | tf_op jit(solution)/shard_map/all_to_all | solution.py:344
  33.0 4.7 %fetch.1 = bf16[128,64,128]{2,1,0:T(8,128)(2,1)} custom-call(s32[128,64]{1,0:T(8,128)S(1)} %bitcast.25, s32[4,512]{1,0:T(4,128)} %expired_ref.3, f32[4,512,128]{2,1,0:T(8,128)} %emb_ref.3), custom_call_target="tpu_custom_call" | custom-call | tf_op jit(solution)/shard_map/fetch/pallas_call | solution.py:413
  37.8 5.9 %all-to-all-start.1 = ((bf16[128,64,128]{2,1,0:T(8,128)(2,1)}), bf16[128,64,128]{2,1,0:T(8,128)(2,1)S(1)}, u32[]{:S(2)}, u32[]{:S(2)}) async-start(bf16[128,64,128]{2,1,0:T(8,128)(2,1)} %fetch.1), calls=%async_computation.1 | async-start | bytes 4194304 | tf_op jit(solution)/shard_map/all_to_all | solution.py:344
  43.8 4.4 %collective-permute-start.2 = (bf16[1024,256]{1,0:T(8,128)(2,1)S(1)}, bf16[1024,256]{1,0:T(8,128)(2,1)S(1)}, u32[]{:S(2)}, u32[]{:S(2)}) collective-permute-start(bf16[1024,256]{1,0:T(8,128)(2,1)S(1)} %constant_dynamic-slice_fusion), channel_id=1, source_target_pairs={{0,3},{1,0},{2,1},{3,2},{4,7},{5,4},{6,5},{7,6},{8,11},{9,8},{10,9... | collective-permute-start | bytes 1572872 | tf_op jit(solution)/shard_map/ppermute | solution.py:354
  48.1 2.4 %collective-permute-start.1 = (bf16[1024,256]{1,0:T(8,128)(2,1)S(1)}, bf16[1024,256]{1,0:T(8,128)(2,1)S(1)}, u32[]{:S(2)}, u32[]{:S(2)}) collective-permute-start(bf16[1024,256]{1,0:T(8,128)(2,1)S(1)} %constant_dynamic-slice_fusion), channel_id=1, source_target_pairs={{0,2},{1,3},{2,0},{3,1},{4,6},{5,7},{6,4},{7,5},{8,10},{9,11},{10,... | collective-permute-start | bytes 1572872 | tf_op jit(solution)/shard_map/ppermute | solution.py:354
  50.6 2.5 %collective-permute-start = (bf16[1024,256]{1,0:T(8,128)(2,1)S(1)}, bf16[1024,256]{1,0:T(8,128)(2,1)S(1)}, u32[]{:S(2)}, u32[]{:S(2)}) collective-permute-start(bf16[1024,256]{1,0:T(8,128)(2,1)S(1)} %constant_dynamic-slice_fusion), channel_id=1, source_target_pairs={{0,1},{1,2},{2,3},{3,0},{4,5},{5,6},{6,7},{7,4},{8,9},{9,10},{10,1... | collective-permute-start | bytes 1572872 | tf_op jit(solution)/shard_map/ppermute | solution.py:354
  53.1 6.1 %collective-permute-done.2 = bf16[1024,256]{1,0:T(8,128)(2,1)S(1)} collective-permute-done((bf16[1024,256]{1,0:T(8,128)(2,1)S(1)}, bf16[1024,256]{1,0:T(8,128)(2,1)S(1)}, u32[]{:S(2)}, u32[]{:S(2)}) %collective-permute-start.2) | collective-permute-done | bytes 524320 | tf_op jit(solution)/shard_map/ppermute | solution.py:354
  59.2 4.6 %collective-permute-done.1 = bf16[1024,256]{1,0:T(8,128)(2,1)S(1)} collective-permute-done((bf16[1024,256]{1,0:T(8,128)(2,1)S(1)}, bf16[1024,256]{1,0:T(8,128)(2,1)S(1)}, u32[]{:S(2)}, u32[]{:S(2)}) %collective-permute-start.1) | collective-permute-done | bytes 524320 | tf_op jit(solution)/shard_map/ppermute | solution.py:354
  63.8 12.8 %collective-permute-done = bf16[1024,256]{1,0:T(8,128)(2,1)S(1)} collective-permute-done((bf16[1024,256]{1,0:T(8,128)(2,1)S(1)}, bf16[1024,256]{1,0:T(8,128)(2,1)S(1)}, u32[]{:S(2)}, u32[]{:S(2)}) %collective-permute-start) | collective-permute-done | bytes 524320 | tf_op jit(solution)/shard_map/ppermute | solution.py:354
  78.0 2.4 %collective-permute-start.3 = (bf16[3,1024,256]{2,1,0:T(8,128)(2,1)}, bf16[3,1024,256]{2,1,0:T(8,128)(2,1)}, u32[]{:S(2)}, u32[]{:S(2)}) collective-permute-start(bf16[3,1024,256]{2,1,0:T(8,128)(2,1)} %pad_maximum_fusion.near_ref), channel_id=1, source_target_pairs={{0,4},{4,0},{1,5},{5,1},{2,6},{6,2},{3,7},{7,3},{8,12},{12,8},{9,1... | collective-permute-start | bytes 4718600 | tf_op jit(solution)/shard_map/ppermute | solution.py:354
  81.2 2.5 %samples.1 = (bf16[4,2048,128]{2,1,0:T(8,128)(2,1)}, f32[4,2048]{1,0:T(4,128)S(1)}) custom-call(f32[128,64]{1,0:T(8,128)S(1)} %copy-done.6), custom_call_target="tpu_custom_call" | custom-call | flops 4294967296 | bytes 1048576 | tf_op jit(solution)/shard_map/samples/pallas_call | solution.py:398
  85.8 3.4 %collective-permute-start.5 = (f32[1,256]{1,0:T(1,128)S(1)}, f32[1,256]{1,0:T(1,128)S(1)}, u32[]{:S(2)}, u32[]{:S(2)}) collective-permute-start(f32[1,256]{1,0:T(1,128)S(1)} %bitcast.29), channel_id=1, source_target_pairs={{0,2},{1,3},{2,0},{3,1},{4,6},{5,7},{6,4},{7,5},{8,10},{9,11},{10,... | collective-permute-start | bytes 3080 | tf_op jit(solution)/shard_map/ppermute | solution.py:354
  89.2 3.1 %collective-permute-start.6 = (f32[1,256]{1,0:T(1,128)S(1)}, f32[1,256]{1,0:T(1,128)S(1)}, u32[]{:S(2)}, u32[]{:S(2)}) collective-permute-start(f32[1,256]{1,0:T(1,128)S(1)} %bitcast.30), channel_id=1, source_target_pairs={{0,3},{1,0},{2,1},{3,2},{4,7},{5,4},{6,5},{7,6},{8,11},{9,8},{10,9... | collective-permute-start | bytes 3080 | tf_op jit(solution)/shard_map/ppermute | solution.py:354
  92.4 2.7 %all-to-all-done.1.rows_ref = bf16[128,64,128]{2,1,0:T(8,128)(2,1)S(1)} async-done(((bf16[128,64,128]{2,1,0:T(8,128)(2,1)}), bf16[128,64,128]{2,1,0:T(8,128)(2,1)S(1)}, u32[]{:S(2)}, u32[]{:S(2)}) %all-to-all-start.1) | async-done | bytes 2097184 | tf_op jit(solution)/shard_map/all_to_all | solution.py:344
  96.6 4.0 %all-to-all-start.2 = ((bf16[4,128,512]{2,1,0:T(8,128)(2,1)}), bf16[4,128,512]{2,1,0:T(8,128)(2,1)S(1)}, u32[]{:S(2)}, u32[]{:S(2)}) async-start(bf16[4,128,512]{2,1,0:T(8,128)(2,1)} %copy-done.1), calls=%async_computation.2 | async-start | bytes 1048576 | tf_op jit(solution)/shard_map/all_to_all | solution.py:344
  100.7 6.9 %all-to-all-done.2.feat_ref = bf16[4,128,512]{2,1,0:T(8,128)(2,1)S(1)} async-done(((bf16[4,128,512]{2,1,0:T(8,128)(2,1)}), bf16[4,128,512]{2,1,0:T(8,128)(2,1)S(1)}, u32[]{:S(2)}, u32[]{:S(2)}) %all-to-all-start.2) | async-done | bytes 524320 | tf_op jit(solution)/shard_map/all_to_all | solution.py:344
  107.6 3.7 %dense.1 = (f32[128,128]{1,0:T(8,128)S(1)}, f32[128,512]{1,0:T(8,128)S(1)}, bf16[2048,128]{1,0:T(8,128)(2,1)S(1)}, bf16[2048,128]{1,0:T(8,128)(2,1)S(1)}) custom-call(s32[2]{0:T(128)S(1)} %pad_add_fusion.at_ref, bf16[4,128,512]{2,1,0:T(8,128)(2,1)S(1)} %all-to-all-done.2.feat_ref, bf16[2048,256]{1,0:T(8,128)(2,1)S(1)} %copy-done, ...), custom_call_target="tpu_custom_call" | custom-call | tf_op jit(solution)/shard_map/dense/pallas_call | solution.py:457
  111.3 5.5 %collective-permute-start.7 = (bf16[2048,128]{1,0:T(8,128)(2,1)S(1)}, bf16[2048,128]{1,0:T(8,128)(2,1)S(1)}, u32[]{:S(2)}, u32[]{:S(2)}) collective-permute-start(bf16[2048,128]{1,0:T(8,128)(2,1)S(1)} %get-tuple-element.43), channel_id=1, source_target_pairs={{0,4},{4,0},{1,5},{5,1},{2,6},{6,2},{3,7},{7,3},{8,12},{12,8},{9,1... | collective-permute-start | bytes 1572872 | tf_op jit(solution)/shard_map/ppermute | solution.py:354
  118.6 72.1 %all_to_all.32.grads_ref = bf16[128,80,128]{2,1,0:T(8,128)(2,1)S(1)} all-to-all(bf16[128,80,128]{2,1,0:T(8,128)(2,1)S(1)} %constant_dynamic-update-slice_fusion), channel_id=1, replica_groups=mesh['dp_0'=8,'dp_1'=8,'dp_2'=2,'mp'=4] {'dp_0','dp_1','dp_2'}, dimensions={0} | all-to-all | bytes 5242880 | tf_op jit(solution)/shard_map/all_to_all | solution.py:344
  191.7 9.2 %all-to-all-start.4 = ((bf16[64,2,2,8,128]{4,3,2,1,0:T(8,128)(2,1)}), bf16[64,2,2,8,128]{4,3,2,1,0:T(8,128)(2,1)S(1)}, u32[]{:S(2)}, u32[]{:S(2)}) async-start(bf16[64,2,2,8,128]{4,3,2,1,0:T(8,128)(2,1)} %broadcast_in_dim.2), calls=%async_computation.4 | async-start | bytes 1048576 | tf_op jit(solution)/shard_map/all_to_all | solution.py:344
  201.0 17.5 %all-to-all-done.4 = bf16[64,2,2,8,128]{4,3,2,1,0:T(8,128)(2,1)S(1)} async-done(((bf16[64,2,2,8,128]{4,3,2,1,0:T(8,128)(2,1)}), bf16[64,2,2,8,128]{4,3,2,1,0:T(8,128)(2,1)S(1)}, u32[]{:S(2)}, u32[]{:S(2)}) %all-to-all-start.4) | async-done | bytes 524320 | tf_op jit(solution)/shard_map/all_to_all | solution.py:344
  218.5 5.1 %collective-permute-start.8 = (bf16[1024,256]{1,0:T(8,128)(2,1)S(1)}, bf16[1024,256]{1,0:T(8,128)(2,1)S(1)}, u32[]{:S(2)}, u32[]{:S(2)}) collective-permute-start(bf16[1024,256]{1,0:T(8,128)(2,1)S(1)} %bitcast.33), channel_id=1, source_target_pairs={{0,4},{4,0},{1,5},{5,1},{2,6},{6,2},{3,7},{7,3},{8,12},{12,8},{9,1... | collective-permute-start | bytes 1572872 | tf_op jit(solution)/shard_map/ppermute | solution.py:354
  226.3 8.2 %update.1 = (f32[4,512,128]{2,1,0:T(8,128)}, f32[4,512]{1,0:T(4,128)}) custom-call(bf16[128,80,128]{2,1,0:T(8,128)(2,1)S(1)} %all_to_all.32.grads_ref, f32[4,16,2048]{2,1,0:T(8,128)} %wanted.1.wanted_ref, f32[4,512,128]{2,1,0:T(8,128)} %emb_ref.3, s32[4,512]{1,0:T(4,128)S(1)} %copy-done.2, f32[4,512]{1,0:T(4,128)S(1)} %copy-done.7), custom_call_target="tpu_custom_call" | custom-call | flops 4294967296 | bytes 1048576 | tf_op jit(solution)/shard_map/update/pallas_call | solution.py:499
  (42 shorter events, 12.5 us)
Async XLA Ops:
  3.3 29.7 %copy-start.5 = (f32[128,64]{1,0:T(8,128)}, f32[128,64]{1,0:T(8,128)S(1)}, u32[]{:S(2)}) copy-start(f32[128,64]{1,0:T(8,128)S(1)} %get-tuple-element.27.sample_ref) | copy-start | bytes 98308
  37.8 5.9 %copy-start = (bf16[2048,256]{1,0:T(8,128)(2,1)S(1)}, bf16[2048,256]{1,0:T(8,128)(2,1)}, u32[]{:S(2)}) copy-start(bf16[2048,256]{1,0:T(8,128)(2,1)} %own_ref.1) | copy-start | bytes 3145732
  37.8 57.3 %all-to-all-start.1 = ((bf16[128,64,128]{2,1,0:T(8,128)(2,1)}), bf16[128,64,128]{2,1,0:T(8,128)(2,1)S(1)}, u32[]{:S(2)}, u32[]{:S(2)}) async-start(bf16[128,64,128]{2,1,0:T(8,128)(2,1)} %fetch.1), calls=%async_computation.1 | async-start | bytes 4194304 | tf_op jit(solution)/shard_map/all_to_all | solution.py:344
  43.8 15.4 %collective-permute-start.2 = (bf16[1024,256]{1,0:T(8,128)(2,1)S(1)}, bf16[1024,256]{1,0:T(8,128)(2,1)S(1)}, u32[]{:S(2)}, u32[]{:S(2)}) collective-permute-start(bf16[1024,256]{1,0:T(8,128)(2,1)S(1)} %constant_dynamic-slice_fusion), channel_id=1, source_target_pairs={{0,3},{1,0},{2,1},{3,2},{4,7},{5,4},{6,5},{7,6},{8,11},{9,8},{10,9... | collective-permute-start | bytes 1572872 | tf_op jit(solution)/shard_map/ppermute | solution.py:354
  48.1 15.6 %collective-permute-start.1 = (bf16[1024,256]{1,0:T(8,128)(2,1)S(1)}, bf16[1024,256]{1,0:T(8,128)(2,1)S(1)}, u32[]{:S(2)}, u32[]{:S(2)}) collective-permute-start(bf16[1024,256]{1,0:T(8,128)(2,1)S(1)} %constant_dynamic-slice_fusion), channel_id=1, source_target_pairs={{0,2},{1,3},{2,0},{3,1},{4,6},{5,7},{6,4},{7,5},{8,10},{9,11},{10,... | collective-permute-start | bytes 1572872 | tf_op jit(solution)/shard_map/ppermute | solution.py:354
  50.6 26.0 %collective-permute-start = (bf16[1024,256]{1,0:T(8,128)(2,1)S(1)}, bf16[1024,256]{1,0:T(8,128)(2,1)S(1)}, u32[]{:S(2)}, u32[]{:S(2)}) collective-permute-start(bf16[1024,256]{1,0:T(8,128)(2,1)S(1)} %constant_dynamic-slice_fusion), channel_id=1, source_target_pairs={{0,1},{1,2},{2,3},{3,0},{4,5},{5,6},{6,7},{7,4},{8,9},{9,10},{10,1... | collective-permute-start | bytes 1572872 | tf_op jit(solution)/shard_map/ppermute | solution.py:354
  78.0 18.6 %collective-permute-start.3 = (bf16[3,1024,256]{2,1,0:T(8,128)(2,1)}, bf16[3,1024,256]{2,1,0:T(8,128)(2,1)}, u32[]{:S(2)}, u32[]{:S(2)}) collective-permute-start(bf16[3,1024,256]{2,1,0:T(8,128)(2,1)} %pad_maximum_fusion.near_ref), channel_id=1, source_target_pairs={{0,4},{4,0},{1,5},{5,1},{2,6},{6,2},{3,7},{7,3},{8,12},{12,8},{9,1... | collective-permute-start | bytes 4718600 | tf_op jit(solution)/shard_map/ppermute | solution.py:354
  80.4 0.8 copy-start.6
  81.2 2.5 %copy-start.3 = (f32[256]{0:T(256)S(1)}, f32[256]{0:T(256)}, u32[]{:S(2)}) copy-start(f32[256]{0:T(256)} %param.18) | copy-start | bytes 3076
  83.7 16.9 %copy-start.4 = (s32[128]{0:T(128)S(1)}, s32[128]{0:T(128)}, u32[]{:S(2)}) copy-start(s32[128]{0:T(128)} %param.19) | copy-start | bytes 1540
  83.8 12.8 %collective-permute-start.4 = (f32[1,256]{1,0:T(1,128)S(1)}, f32[1,256]{1,0:T(1,128)S(1)}, u32[]{:S(2)}, u32[]{:S(2)}) collective-permute-start(f32[1,256]{1,0:T(1,128)S(1)} %bitcast.28), channel_id=1, source_target_pairs={{0,1},{1,2},{2,3},{3,0},{4,5},{5,6},{6,7},{7,4},{8,9},{9,10},{10,1... | collective-permute-start | bytes 3080 | tf_op jit(solution)/shard_map/ppermute | solution.py:354
  85.8 10.8 %collective-permute-start.5 = (f32[1,256]{1,0:T(1,128)S(1)}, f32[1,256]{1,0:T(1,128)S(1)}, u32[]{:S(2)}, u32[]{:S(2)}) collective-permute-start(f32[1,256]{1,0:T(1,128)S(1)} %bitcast.29), channel_id=1, source_target_pairs={{0,2},{1,3},{2,0},{3,1},{4,6},{5,7},{6,4},{7,5},{8,10},{9,11},{10,... | collective-permute-start | bytes 3080 | tf_op jit(solution)/shard_map/ppermute | solution.py:354
  89.2 7.4 %collective-permute-start.6 = (f32[1,256]{1,0:T(1,128)S(1)}, f32[1,256]{1,0:T(1,128)S(1)}, u32[]{:S(2)}, u32[]{:S(2)}) collective-permute-start(f32[1,256]{1,0:T(1,128)S(1)} %bitcast.30), channel_id=1, source_target_pairs={{0,3},{1,0},{2,1},{3,2},{4,7},{5,4},{6,5},{7,6},{8,11},{9,8},{10,9... | collective-permute-start | bytes 3080 | tf_op jit(solution)/shard_map/ppermute | solution.py:354
  95.8 0.8 copy-start.1
  96.6 11.0 %all-to-all-start.2 = ((bf16[4,128,512]{2,1,0:T(8,128)(2,1)}), bf16[4,128,512]{2,1,0:T(8,128)(2,1)S(1)}, u32[]{:S(2)}, u32[]{:S(2)}) async-start(bf16[4,128,512]{2,1,0:T(8,128)(2,1)} %copy-done.1), calls=%async_computation.2 | async-start | bytes 1048576 | tf_op jit(solution)/shard_map/all_to_all | solution.py:344
  107.6 9.2 %copy-start.8 = (bf16[4,2048,128]{2,1,0:T(8,128)(2,1)S(1)}, bf16[4,2048,128]{2,1,0:T(8,128)(2,1)}, u32[]{:S(2)}) copy-start(bf16[4,2048,128]{2,1,0:T(8,128)(2,1)} %get-tuple-element.41.pick_ref) | copy-start | bytes 6291460
  111.3 7.0 %collective-permute-start.7 = (bf16[2048,128]{1,0:T(8,128)(2,1)S(1)}, bf16[2048,128]{1,0:T(8,128)(2,1)S(1)}, u32[]{:S(2)}, u32[]{:S(2)}) collective-permute-start(bf16[2048,128]{1,0:T(8,128)(2,1)S(1)} %get-tuple-element.43), channel_id=1, source_target_pairs={{0,4},{4,0},{1,5},{5,1},{2,6},{6,2},{3,7},{7,3},{8,12},{12,8},{9,1... | collective-permute-start | bytes 1572872 | tf_op jit(solution)/shard_map/ppermute | solution.py:354
  191.7 26.8 %all-to-all-start.4 = ((bf16[64,2,2,8,128]{4,3,2,1,0:T(8,128)(2,1)}), bf16[64,2,2,8,128]{4,3,2,1,0:T(8,128)(2,1)S(1)}, u32[]{:S(2)}, u32[]{:S(2)}) async-start(bf16[64,2,2,8,128]{4,3,2,1,0:T(8,128)(2,1)} %broadcast_in_dim.2), calls=%async_computation.4 | async-start | bytes 1048576 | tf_op jit(solution)/shard_map/all_to_all | solution.py:344
  218.5 7.8 %copy-start.2 = (s32[4,512]{1,0:T(4,128)S(1)}, s32[4,512]{1,0:T(4,128)}, u32[]{:S(2)}) copy-start(s32[4,512]{1,0:T(4,128)} %expired_ref.3) | copy-start | bytes 24580
  218.5 7.8 %copy-start.7 = (f32[4,512]{1,0:T(4,128)S(1)}, f32[4,512]{1,0:T(4,128)}, u32[]{:S(2)}) copy-start(f32[4,512]{1,0:T(4,128)} %acc_ref.1) | copy-start | bytes 24580
  218.5 16.0 %collective-permute-start.8 = (bf16[1024,256]{1,0:T(8,128)(2,1)S(1)}, bf16[1024,256]{1,0:T(8,128)(2,1)S(1)}, u32[]{:S(2)}, u32[]{:S(2)}) collective-permute-start(bf16[1024,256]{1,0:T(8,128)(2,1)S(1)} %bitcast.33), channel_id=1, source_target_pairs={{0,4},{4,0},{1,5},{5,1},{2,6},{6,2},{3,7},{7,3},{8,12},{12,8},{9,1... | collective-permute-start | bytes 1572872 | tf_op jit(solution)/shard_map/ppermute | solution.py:354

commit v7 on v6

--- a/solution.py
+++ b/solution.py
@@ -100,7 +100,7 @@
     return flag((lane // width == kind) & (lane % width // cap == t))
 
 
-def samples_kernel(sample_ref, pick_ref, row_ref):
+def samples_kernel(sample_ref, inv_ref, pick_ref, row_ref):
     tabs, slots, toks = pick_ref.shape
     width = sample_ref.shape[1]
     cap = width // tabs
@@ -109,8 +109,11 @@
     for t in range(tabs):
         mine = of_table((width, toks), 0, t, 0, width, cap)
         pick_ref[t] = flag(dot(own, mine) == wanted)
-        row = dot(of_table((8, width), 1, t, 0, width, cap), own, NT)
-        row_ref[t : t + 1, :] = row[0:1]
+        row = dot(of_table((8, width), 1, t, 0, width, cap), own, NT)[0:1]
+        row_ref[t, :toks] = inv_ref[t]
+        row_ref[t, toks:] = jnp.concatenate(
+            [row[:, j : j + toks] for j in range(0, slots, toks)], axis=0
+        )
 
 
 def labels_kernel(label_ref, out_ref):
@@ -143,12 +146,12 @@
     for load in loads:
         load.start()
     arrived = arrived_ref[...]
-    low = (arrived & (half - 1)).astype(F32).T.astype(BF16)
-    side = (arrived >> (half.bit_length() - 1)).astype(F32).T.astype(BF16)
+    place = (arrived & (half - 1)) + 1
+    signed = jnp.where(arrived < half, place, -place).astype(F32).T.astype(BF16)
     diag = iota((emb, emb), 0) == iota((emb, emb), 1)
     parts = out_sem.shape[0]
     part = groups // parts
-    lane = iota((cap, emb), 1).astype(F32)
+    lane = (iota((cap, emb), 1) + 1).astype(F32)
     names = lane.astype(BF16), (lane + emb).astype(BF16)
     one, zero = jnp.ones((cap, emb), BF16), jnp.zeros((cap, emb), BF16)
     stores = []
@@ -162,18 +165,19 @@
                 for j in range(0, rows, emb):
                     gone = gone_ref[t : t + 1, j : j + emb].astype(F32)
                     column = jnp.sum(jnp.where(diag, gone, 0.0), axis=1, keepdims=True)
-                    at = j // half * emb
-                    table_ref[t, j % half : j % half + emb, at : at + emb] = jnp.where(
+                    to = j // half * emb
+                    table_ref[t, j % half : j % half + emb, to : to + emb] = jnp.where(
                         column > 0.5, 0.0, held_ref[t, j : j + emb, :]
                     ).astype(BF16)
             lines = slice(t * cap, (t + 1) * cap)
             picks, first = [], []
             for o in range(c * part, (c + 1) * part):
-                row = jnp.broadcast_to(low[lines, o : o + 1], (cap, emb))
+                row = jnp.broadcast_to(signed[lines, o : o + 1], (cap, emb))
+                at = jnp.abs(row)
                 picks.append(
-                    jnp.concatenate([jnp.where(row == n, one, zero) for n in names], axis=1)
+                    jnp.concatenate([jnp.where(at == n, one, zero) for n in names], axis=1)
                 )
-                first.append(jnp.broadcast_to(side[lines, o : o + 1], (cap, emb)) == zero)
+                first.append(row > zero)
             both = dot(jnp.concatenate(picks, axis=0), table_ref[t]).astype(BF16)
             line = jnp.where(jnp.concatenate(first, axis=0), both[:, :emb], both[:, emb:])
             sent_ref[mine, lines, :] = line.reshape(part, cap, emb)
@@ -205,18 +209,24 @@
     return jnp.concatenate([row] * (length // 8), axis=0).astype(BF16)
 
 
-def pool_kernel(rows_ref, sample_ref, inv_ref, out_ref):
+def pool_kernel(rows_ref, sample_ref, out_ref):
     groups, width, emb = rows_ref.shape
-    tabs, toks, _ = inv_ref.shape
+    tabs, _, toks = sample_ref.shape
     cap = width // tabs
     slots = groups * cap
     one, zero = jnp.ones((toks, slots), BF16), jnp.zeros((toks, slots), BF16)
     samples = sublanes(toks, slots)
     for t in range(tabs):
-        row = jnp.broadcast_to(sample_ref[t : t + 1, :] - 1.0, (16, slots)).astype(BF16)
+        row = jnp.concatenate(
+            [
+                jnp.broadcast_to(sample_ref[t, j : j + 1, :] - 1.0, (16, toks))
+                for j in range(toks, toks + slots // toks)
+            ],
+            axis=1,
+        ).astype(BF16)
         pick = jnp.where(jnp.concatenate([row] * (toks // 16), axis=0) == samples, one, zero)
         pooled = dot(pick, rows_ref[:, t * cap : (t + 1) * cap, :].reshape(slots, emb))
-        feature = (pooled * inv_ref[t]).astype(BF16)
+        feature = (pooled * sample_ref[t, :toks]).astype(BF16)
         for k in range(out_ref.shape[0]):
             out_ref[k, :, t * emb : (t + 1) * emb] = feature
 
@@ -399,12 +409,12 @@
         samples_kernel,
         out_shape=(
             pltpu.HBM((tabs, slots, toks), BF16),
-            shape((tabs, slots), F32),
+            shape((tabs, toks + slots // toks, toks), F32),
         ),
         compiler_params=params(24),
         cost_estimate=cost(4 << 30),
         name="samples",
-    )(sample)
+    )(sample, inv)
     held = functools.partial(pltpu.with_memory_space_constraint, memory_space=pltpu.HBM)
     smem, vmem, hbm = (
         pl.BlockSpec(memory_space=space) for space in (pltpu.SMEM, pltpu.VMEM, pltpu.HBM)
@@ -442,7 +452,7 @@
         out_shape=shape((parts, toks, feats), BF16),
         compiler_params=params(24),
         name="pool",
-    )(returned, sample_row, inv)
+    )(returned, sample_row)
     features, place, near_weights, far_weights, units = lax.optimization_barrier(
         (features, place, near_weights, far_weights, units)
     )

time: 236 us -> 238 us (level)
  transfers between devices with their start and end apart: 12 -> 12, of which waited for: 7 -> 6; matrix products, arithmetic and copies ran while one was open for 1% -> 1% of each run, Pallas kernels for 6% -> 6%
where the time goes in v7:
time: 238 us; the launch traced here: 237 us
  blocking collectives  103 us (43%)
  starting transfers between devices  50.2 us (21%)
  waiting for transfers between devices  49.6 us (21%)
  Pallas kernels  25.5 us (11%)
  local copies, waits for them, and re-layouts  4.98 us (2%)
  other arithmetic  2.79 us (1%)
    all_to_all x2, blocking collectives, a2a(): return lax.all_to_all(value, axis, split_axis=0, concat_axis=0, tiled=True)  103 us
    ppermute x9, starting transfers between devices, ring(): lax.ppermute(value, axis, [(i, (i + step) % size) for i in range(size)])  31 us
    all_to_all x3, waiting for transfers between devices, a2a(): return lax.all_to_all(value, axis, split_axis=0, concat_axis=0, tiled=True)  26.1 us
    ppermute x9, waiting for transfers between devices, ring(): lax.ppermute(value, axis, [(i, (i + step) % size) for i in range(size)])  23.5 us
    all_to_all x3, starting transfers between devices, a2a(): return lax.all_to_all(value, axis, split_axis=0, concat_axis=0, tiled=True)  19.2 us
    pallas_call x1, Pallas kernels, shards(): pl.pallas_call(update_kernel, grid=(tabs,), in_specs=[block((groups, cap,...  8.18 us
  transfers between devices with their start and end apart: 12, of which 6 were waited for; matrix products, arithmetic and copies ran while one was open for 1% of the time, Pallas kernels for 6%

profile of v7, /device:TPU:1, one launch (start us, length us, event | category | flops | bytes accessed | tf_op | source)
XLA Modules:
  0.0 236.8 jit_solution(6019827592877145030)
XLA Ops:
  0.6 2.7 %slots.1 = (s32[128,64]{1,0:T(8,128)S(1)}, f32[128,64]{1,0:T(8,128)S(1)}, f32[4,128,128]{2,1,0:T(8,128)S(1)}) custom-call(s32[4,128]{1,0:T(4,128)} %len_ref.1, s32[4,8,128]{2,1,0:T(8,128)} %bitcast.42, s32[4,8,128]{2,1,0:T(8,128)} %bitcast.43, s32[4,8,128]{2,1,0:T(8,128)} %bitcast.44), custom_call_target="tpu_custom_call" | custom-call | tf_op jit(solution)/shard_map/slots/pallas_call | solution.py:382
  4.0 29.7 %all_to_all.31 = s32[128,1,64]{2,1,0:T(1,128)S(1)} all-to-all(s32[128,1,64]{2,1,0:T(1,128)S(1)} %bitcast.27), channel_id=1, replica_groups=mesh['dp_0'=8,'dp_1'=8,'dp_2'=2,'mp'=4] {'dp_0','dp_1','dp_2'}, dimensions={0} | all-to-all | bytes 65536 | tf_op jit(solution)/shard_map/all_to_all | solution.py:354
  33.7 4.3 %fetch.1 = bf16[128,64,128]{2,1,0:T(8,128)(2,1)} custom-call(s32[128,64]{1,0:T(8,128)S(1)} %bitcast.25, s32[4,512]{1,0:T(4,128)} %expired_ref.3, f32[4,512,128]{2,1,0:T(8,128)} %emb_ref.3), custom_call_target="tpu_custom_call" | custom-call | tf_op jit(solution)/shard_map/fetch/pallas_call | solution.py:423
  38.0 5.9 %all-to-all-start.1 = ((bf16[128,64,128]{2,1,0:T(8,128)(2,1)}), bf16[128,64,128]{2,1,0:T(8,128)(2,1)S(1)}, u32[]{:S(2)}, u32[]{:S(2)}) async-start(bf16[128,64,128]{2,1,0:T(8,128)(2,1)} %fetch.1), calls=%async_computation.1 | async-start | bytes 4194304 | tf_op jit(solution)/shard_map/all_to_all | solution.py:354
  44.0 4.4 %collective-permute-start.2 = (bf16[1024,256]{1,0:T(8,128)(2,1)S(1)}, bf16[1024,256]{1,0:T(8,128)(2,1)S(1)}, u32[]{:S(2)}, u32[]{:S(2)}) collective-permute-start(bf16[1024,256]{1,0:T(8,128)(2,1)S(1)} %constant_dynamic-slice_fusion), channel_id=1, source_target_pairs={{0,3},{1,0},{2,1},{3,2},{4,7},{5,4},{6,5},{7,6},{8,11},{9,8},{10,9... | collective-permute-start | bytes 1572872 | tf_op jit(solution)/shard_map/ppermute | solution.py:364
  48.4 2.4 %collective-permute-start.1 = (bf16[1024,256]{1,0:T(8,128)(2,1)S(1)}, bf16[1024,256]{1,0:T(8,128)(2,1)S(1)}, u32[]{:S(2)}, u32[]{:S(2)}) collective-permute-start(bf16[1024,256]{1,0:T(8,128)(2,1)S(1)} %constant_dynamic-slice_fusion), channel_id=1, source_target_pairs={{0,2},{1,3},{2,0},{3,1},{4,6},{5,7},{6,4},{7,5},{8,10},{9,11},{10,... | collective-permute-start | bytes 1572872 | tf_op jit(solution)/shard_map/ppermute | solution.py:364
  50.8 2.5 %collective-permute-start = (bf16[1024,256]{1,0:T(8,128)(2,1)S(1)}, bf16[1024,256]{1,0:T(8,128)(2,1)S(1)}, u32[]{:S(2)}, u32[]{:S(2)}) collective-permute-start(bf16[1024,256]{1,0:T(8,128)(2,1)S(1)} %constant_dynamic-slice_fusion), channel_id=1, source_target_pairs={{0,1},{1,2},{2,3},{3,0},{4,5},{5,6},{6,7},{7,4},{8,9},{9,10},{10,1... | collective-permute-start | bytes 1572872 | tf_op jit(solution)/shard_map/ppermute | solution.py:364
  53.3 6.1 %collective-permute-done.2 = bf16[1024,256]{1,0:T(8,128)(2,1)S(1)} collective-permute-done((bf16[1024,256]{1,0:T(8,128)(2,1)S(1)}, bf16[1024,256]{1,0:T(8,128)(2,1)S(1)}, u32[]{:S(2)}, u32[]{:S(2)}) %collective-permute-start.2) | collective-permute-done | bytes 524320 | tf_op jit(solution)/shard_map/ppermute | solution.py:364
  59.4 4.6 %collective-permute-done.1 = bf16[1024,256]{1,0:T(8,128)(2,1)S(1)} collective-permute-done((bf16[1024,256]{1,0:T(8,128)(2,1)S(1)}, bf16[1024,256]{1,0:T(8,128)(2,1)S(1)}, u32[]{:S(2)}, u32[]{:S(2)}) %collective-permute-start.1) | collective-permute-done | bytes 524320 | tf_op jit(solution)/shard_map/ppermute | solution.py:364
  64.0 12.8 %collective-permute-done = bf16[1024,256]{1,0:T(8,128)(2,1)S(1)} collective-permute-done((bf16[1024,256]{1,0:T(8,128)(2,1)S(1)}, bf16[1024,256]{1,0:T(8,128)(2,1)S(1)}, u32[]{:S(2)}, u32[]{:S(2)}) %collective-permute-start) | collective-permute-done | bytes 524320 | tf_op jit(solution)/shard_map/ppermute | solution.py:364
  78.2 2.4 %collective-permute-start.3 = (bf16[3,1024,256]{2,1,0:T(8,128)(2,1)}, bf16[3,1024,256]{2,1,0:T(8,128)(2,1)}, u32[]{:S(2)}, u32[]{:S(2)}) collective-permute-start(bf16[3,1024,256]{2,1,0:T(8,128)(2,1)} %pad_maximum_fusion.near_ref), channel_id=1, source_target_pairs={{0,4},{4,0},{1,5},{5,1},{2,6},{6,2},{3,7},{7,3},{8,12},{12,8},{9,1... | collective-permute-start | bytes 4718600 | tf_op jit(solution)/shard_map/ppermute | solution.py:364
  82.4 2.5 %samples.1 = (bf16[4,2048,128]{2,1,0:T(8,128)(2,1)}, f32[4,144,128]{2,1,0:T(8,128)S(1)}) custom-call(f32[128,64]{1,0:T(8,128)S(1)} %copy-done.9, f32[4,128,128]{2,1,0:T(8,128)S(1)} %copy-done.6), custom_call_target="tpu_custom_call" | custom-call | flops 4294967296 | bytes 1048576 | tf_op jit(solution)/shard_map/samples/pallas_call | solution.py:408
  87.0 3.4 %collective-permute-start.5 = (f32[1,256]{1,0:T(1,128)S(1)}, f32[1,256]{1,0:T(1,128)S(1)}, u32[]{:S(2)}, u32[]{:S(2)}) collective-permute-start(f32[1,256]{1,0:T(1,128)S(1)} %bitcast.29), channel_id=1, source_target_pairs={{0,2},{1,3},{2,0},{3,1},{4,6},{5,7},{6,4},{7,5},{8,10},{9,11},{10,... | collective-permute-start | bytes 3080 | tf_op jit(solution)/shard_map/ppermute | solution.py:364
  90.4 3.1 %collective-permute-start.6 = (f32[1,256]{1,0:T(1,128)S(1)}, f32[1,256]{1,0:T(1,128)S(1)}, u32[]{:S(2)}, u32[]{:S(2)}) collective-permute-start(f32[1,256]{1,0:T(1,128)S(1)} %bitcast.30), channel_id=1, source_target_pairs={{0,3},{1,0},{2,1},{3,2},{4,7},{5,4},{6,5},{7,6},{8,11},{9,8},{10,9... | collective-permute-start | bytes 3080 | tf_op jit(solution)/shard_map/ppermute | solution.py:364
  96.8 4.0 %all-to-all-start.2 = ((bf16[4,128,512]{2,1,0:T(8,128)(2,1)}), bf16[4,128,512]{2,1,0:T(8,128)(2,1)S(1)}, u32[]{:S(2)}, u32[]{:S(2)}) async-start(bf16[4,128,512]{2,1,0:T(8,128)(2,1)} %copy-done.1), calls=%async_computation.2 | async-start | bytes 1048576 | tf_op jit(solution)/shard_map/all_to_all | solution.py:354
  101.0 6.8 %all-to-all-done.2.feat_ref = bf16[4,128,512]{2,1,0:T(8,128)(2,1)S(1)} async-done(((bf16[4,128,512]{2,1,0:T(8,128)(2,1)}), bf16[4,128,512]{2,1,0:T(8,128)(2,1)S(1)}, u32[]{:S(2)}, u32[]{:S(2)}) %all-to-all-start.2) | async-done | bytes 524320 | tf_op jit(solution)/shard_map/all_to_all | solution.py:354
  107.8 3.7 %dense.1 = (f32[128,128]{1,0:T(8,128)S(1)}, f32[128,512]{1,0:T(8,128)S(1)}, bf16[2048,128]{1,0:T(8,128)(2,1)S(1)}, bf16[2048,128]{1,0:T(8,128)(2,1)S(1)}) custom-call(s32[2]{0:T(128)S(1)} %pad_add_fusion.at_ref, bf16[4,128,512]{2,1,0:T(8,128)(2,1)S(1)} %all-to-all-done.2.feat_ref, bf16[2048,256]{1,0:T(8,128)(2,1)S(1)} %copy-done, ...), custom_call_target="tpu_custom_call" | custom-call | tf_op jit(solution)/shard_map/dense/pallas_call | solution.py:467
  111.5 5.7 %collective-permute-start.7 = (bf16[2048,128]{1,0:T(8,128)(2,1)S(1)}, bf16[2048,128]{1,0:T(8,128)(2,1)S(1)}, u32[]{:S(2)}, u32[]{:S(2)}) collective-permute-start(bf16[2048,128]{1,0:T(8,128)(2,1)S(1)} %get-tuple-element.43), channel_id=1, source_target_pairs={{0,4},{4,0},{1,5},{5,1},{2,6},{6,2},{3,7},{7,3},{8,12},{12,8},{9,1... | collective-permute-start | bytes 1572872 | tf_op jit(solution)/shard_map/ppermute | solution.py:364
  118.8 73.0 %all_to_all.32.grads_ref = bf16[128,80,128]{2,1,0:T(8,128)(2,1)S(1)} all-to-all(bf16[128,80,128]{2,1,0:T(8,128)(2,1)S(1)} %constant_dynamic-update-slice_fusion), channel_id=1, replica_groups=mesh['dp_0'=8,'dp_1'=8,'dp_2'=2,'mp'=4] {'dp_0','dp_1','dp_2'}, dimensions={0} | all-to-all | bytes 5242880 | tf_op jit(solution)/shard_map/all_to_all | solution.py:354
  192.9 9.2 %all-to-all-start.4 = ((bf16[64,2,2,8,128]{4,3,2,1,0:T(8,128)(2,1)}), bf16[64,2,2,8,128]{4,3,2,1,0:T(8,128)(2,1)S(1)}, u32[]{:S(2)}, u32[]{:S(2)}) async-start(bf16[64,2,2,8,128]{4,3,2,1,0:T(8,128)(2,1)} %broadcast_in_dim.2), calls=%async_computation.4 | async-start | bytes 1048576 | tf_op jit(solution)/shard_map/all_to_all | solution.py:354
  202.1 17.5 %all-to-all-done.4 = bf16[64,2,2,8,128]{4,3,2,1,0:T(8,128)(2,1)S(1)} async-done(((bf16[64,2,2,8,128]{4,3,2,1,0:T(8,128)(2,1)}), bf16[64,2,2,8,128]{4,3,2,1,0:T(8,128)(2,1)S(1)}, u32[]{:S(2)}, u32[]{:S(2)}) %all-to-all-start.4) | async-done | bytes 524320 | tf_op jit(solution)/shard_map/all_to_all | solution.py:354
  219.7 5.1 %collective-permute-start.8 = (bf16[1024,256]{1,0:T(8,128)(2,1)S(1)}, bf16[1024,256]{1,0:T(8,128)(2,1)S(1)}, u32[]{:S(2)}, u32[]{:S(2)}) collective-permute-start(bf16[1024,256]{1,0:T(8,128)(2,1)S(1)} %bitcast.33), channel_id=1, source_target_pairs={{0,4},{4,0},{1,5},{5,1},{2,6},{6,2},{3,7},{7,3},{8,12},{12,8},{9,1... | collective-permute-start | bytes 1572872 | tf_op jit(solution)/shard_map/ppermute | solution.py:364
  224.8 2.1 wanted.1.wanted_ref
  227.5 8.2 %update.1 = (f32[4,512,128]{2,1,0:T(8,128)}, f32[4,512]{1,0:T(4,128)}) custom-call(bf16[128,80,128]{2,1,0:T(8,128)(2,1)S(1)} %all_to_all.32.grads_ref, f32[4,16,2048]{2,1,0:T(8,128)} %wanted.1.wanted_ref, f32[4,512,128]{2,1,0:T(8,128)} %emb_ref.3, s32[4,512]{1,0:T(4,128)S(1)} %copy-done.2, f32[4,512]{1,0:T(4,128)S(1)} %copy-done.10), custom_call_target="tpu_custom_call" | custom-call | flops 4294967296 | bytes 1048576 | tf_op jit(solution)/shard_map/update/pallas_call | solution.py:509
  (48 shorter events, 13.7 us)
Async XLA Ops:
  3.3 0.7 copy-start.5
  4.0 29.7 %copy-start.8 = (f32[128,64]{1,0:T(8,128)}, f32[128,64]{1,0:T(8,128)S(1)}, u32[]{:S(2)}) copy-start(f32[128,64]{1,0:T(8,128)S(1)} %get-tuple-element.27.sample_ref) | copy-start | bytes 98308
  38.0 5.9 %copy-start = (bf16[2048,256]{1,0:T(8,128)(2,1)S(1)}, bf16[2048,256]{1,0:T(8,128)(2,1)}, u32[]{:S(2)}) copy-start(bf16[2048,256]{1,0:T(8,128)(2,1)} %own_ref.1) | copy-start | bytes 3145732
  38.0 57.3 %all-to-all-start.1 = ((bf16[128,64,128]{2,1,0:T(8,128)(2,1)}), bf16[128,64,128]{2,1,0:T(8,128)(2,1)S(1)}, u32[]{:S(2)}, u32[]{:S(2)}) async-start(bf16[128,64,128]{2,1,0:T(8,128)(2,1)} %fetch.1), calls=%async_computation.1 | async-start | bytes 4194304 | tf_op jit(solution)/shard_map/all_to_all | solution.py:354
  44.0 15.4 %collective-permute-start.2 = (bf16[1024,256]{1,0:T(8,128)(2,1)S(1)}, bf16[1024,256]{1,0:T(8,128)(2,1)S(1)}, u32[]{:S(2)}, u32[]{:S(2)}) collective-permute-start(bf16[1024,256]{1,0:T(8,128)(2,1)S(1)} %constant_dynamic-slice_fusion), channel_id=1, source_target_pairs={{0,3},{1,0},{2,1},{3,2},{4,7},{5,4},{6,5},{7,6},{8,11},{9,8},{10,9... | collective-permute-start | bytes 1572872 | tf_op jit(solution)/shard_map/ppermute | solution.py:364
  48.4 15.6 %collective-permute-start.1 = (bf16[1024,256]{1,0:T(8,128)(2,1)S(1)}, bf16[1024,256]{1,0:T(8,128)(2,1)S(1)}, u32[]{:S(2)}, u32[]{:S(2)}) collective-permute-start(bf16[1024,256]{1,0:T(8,128)(2,1)S(1)} %constant_dynamic-slice_fusion), channel_id=1, source_target_pairs={{0,2},{1,3},{2,0},{3,1},{4,6},{5,7},{6,4},{7,5},{8,10},{9,11},{10,... | collective-permute-start | bytes 1572872 | tf_op jit(solution)/shard_map/ppermute | solution.py:364
  50.8 26.0 %collective-permute-start = (bf16[1024,256]{1,0:T(8,128)(2,1)S(1)}, bf16[1024,256]{1,0:T(8,128)(2,1)S(1)}, u32[]{:S(2)}, u32[]{:S(2)}) collective-permute-start(bf16[1024,256]{1,0:T(8,128)(2,1)S(1)} %constant_dynamic-slice_fusion), channel_id=1, source_target_pairs={{0,1},{1,2},{2,3},{3,0},{4,5},{5,6},{6,7},{7,4},{8,9},{9,10},{10,1... | collective-permute-start | bytes 1572872 | tf_op jit(solution)/shard_map/ppermute | solution.py:364
  78.2 18.6 %collective-permute-start.3 = (bf16[3,1024,256]{2,1,0:T(8,128)(2,1)}, bf16[3,1024,256]{2,1,0:T(8,128)(2,1)}, u32[]{:S(2)}, u32[]{:S(2)}) collective-permute-start(bf16[3,1024,256]{2,1,0:T(8,128)(2,1)} %pad_maximum_fusion.near_ref), channel_id=1, source_target_pairs={{0,4},{4,0},{1,5},{5,1},{2,6},{6,2},{3,7},{7,3},{8,12},{12,8},{9,1... | collective-permute-start | bytes 4718600 | tf_op jit(solution)/shard_map/ppermute | solution.py:364
  80.6 1.0 copy-start.6
  81.6 0.8 copy-start.9
  82.4 2.5 %copy-start.3 = (f32[256]{0:T(256)S(1)}, f32[256]{0:T(256)}, u32[]{:S(2)}) copy-start(f32[256]{0:T(256)} %param.18) | copy-start | bytes 3076
  84.9 15.9 %copy-start.4 = (s32[128]{0:T(128)S(1)}, s32[128]{0:T(128)}, u32[]{:S(2)}) copy-start(s32[128]{0:T(128)} %param.19) | copy-start | bytes 1540
  84.9 11.9 %collective-permute-start.4 = (f32[1,256]{1,0:T(1,128)S(1)}, f32[1,256]{1,0:T(1,128)S(1)}, u32[]{:S(2)}, u32[]{:S(2)}) collective-permute-start(f32[1,256]{1,0:T(1,128)S(1)} %bitcast.28), channel_id=1, source_target_pairs={{0,1},{1,2},{2,3},{3,0},{4,5},{5,6},{6,7},{7,4},{8,9},{9,10},{10,1... | collective-permute-start | bytes 3080 | tf_op jit(solution)/shard_map/ppermute | solution.py:364
  87.0 9.8 %collective-permute-start.5 = (f32[1,256]{1,0:T(1,128)S(1)}, f32[1,256]{1,0:T(1,128)S(1)}, u32[]{:S(2)}, u32[]{:S(2)}) collective-permute-start(f32[1,256]{1,0:T(1,128)S(1)} %bitcast.29), channel_id=1, source_target_pairs={{0,2},{1,3},{2,0},{3,1},{4,6},{5,7},{6,4},{7,5},{8,10},{9,11},{10,... | collective-permute-start | bytes 3080 | tf_op jit(solution)/shard_map/ppermute | solution.py:364
  90.4 6.4 %collective-permute-start.6 = (f32[1,256]{1,0:T(1,128)S(1)}, f32[1,256]{1,0:T(1,128)S(1)}, u32[]{:S(2)}, u32[]{:S(2)}) collective-permute-start(f32[1,256]{1,0:T(1,128)S(1)} %bitcast.30), channel_id=1, source_target_pairs={{0,3},{1,0},{2,1},{3,2},{4,7},{5,4},{6,5},{7,6},{8,11},{9,8},{10,9... | collective-permute-start | bytes 3080 | tf_op jit(solution)/shard_map/ppermute | solution.py:364
  96.0 0.8 copy-start.1
  96.8 11.0 %all-to-all-start.2 = ((bf16[4,128,512]{2,1,0:T(8,128)(2,1)}), bf16[4,128,512]{2,1,0:T(8,128)(2,1)S(1)}, u32[]{:S(2)}, u32[]{:S(2)}) async-start(bf16[4,128,512]{2,1,0:T(8,128)(2,1)} %copy-done.1), calls=%async_computation.2 | async-start | bytes 1048576 | tf_op jit(solution)/shard_map/all_to_all | solution.py:354
  100.9 16.3 %copy-start.7 = (f32[4,128,128]{2,1,0:T(8,128)S(1)}, f32[4,128,128]{2,1,0:T(8,128)}, u32[]{:S(2)}) copy-start(f32[4,128,128]{2,1,0:T(8,128)} %copy-done.5) | copy-start | bytes 786436
  107.8 9.4 %copy-start.11 = (bf16[4,2048,128]{2,1,0:T(8,128)(2,1)S(1)}, bf16[4,2048,128]{2,1,0:T(8,128)(2,1)}, u32[]{:S(2)}) copy-start(bf16[4,2048,128]{2,1,0:T(8,128)(2,1)} %get-tuple-element.41.pick_ref) | copy-start | bytes 6291460
  111.5 7.1 %collective-permute-start.7 = (bf16[2048,128]{1,0:T(8,128)(2,1)S(1)}, bf16[2048,128]{1,0:T(8,128)(2,1)S(1)}, u32[]{:S(2)}, u32[]{:S(2)}) collective-permute-start(bf16[2048,128]{1,0:T(8,128)(2,1)S(1)} %get-tuple-element.43), channel_id=1, source_target_pairs={{0,4},{4,0},{1,5},{5,1},{2,6},{6,2},{3,7},{7,3},{8,12},{12,8},{9,1... | collective-permute-start | bytes 1572872 | tf_op jit(solution)/shard_map/ppermute | solution.py:364
  192.9 26.8 %all-to-all-start.4 = ((bf16[64,2,2,8,128]{4,3,2,1,0:T(8,128)(2,1)}), bf16[64,2,2,8,128]{4,3,2,1,0:T(8,128)(2,1)S(1)}, u32[]{:S(2)}, u32[]{:S(2)}) async-start(bf16[64,2,2,8,128]{4,3,2,1,0:T(8,128)(2,1)} %broadcast_in_dim.2), calls=%async_computation.4 | async-start | bytes 1048576 | tf_op jit(solution)/shard_map/all_to_all | solution.py:354
  219.7 7.8 %copy-start.2 = (s32[4,512]{1,0:T(4,128)S(1)}, s32[4,512]{1,0:T(4,128)}, u32[]{:S(2)}) copy-start(s32[4,512]{1,0:T(4,128)} %expired_ref.3) | copy-start | bytes 24580
  219.7 7.8 %copy-start.10 = (f32[4,512]{1,0:T(4,128)S(1)}, f32[4,512]{1,0:T(4,128)}, u32[]{:S(2)}) copy-start(f32[4,512]{1,0:T(4,128)} %acc_ref.1) | copy-start | bytes 24580
  219.7 16.0 %collective-permute-start.8 = (bf16[1024,256]{1,0:T(8,128)(2,1)S(1)}, bf16[1024,256]{1,0:T(8,128)(2,1)S(1)}, u32[]{:S(2)}, u32[]{:S(2)}) collective-permute-start(bf16[1024,256]{1,0:T(8,128)(2,1)S(1)} %bitcast.33), channel_id=1, source_target_pairs={{0,4},{4,0},{1,5},{5,1},{2,6},{6,2},{3,7},{7,3},{8,12},{12,8},{9,1... | collective-permute-start | bytes 1572872 | tf_op jit(solution)/shard_map/ppermute | solution.py:364
